TPU v7x, 128 devices: a whole 4x4x4 slice. The times are simulated.
128 devices in a mesh: row: 2 (over x_lo), col: 64 (over z, y, x_hi, core).
Axes of the slice: x: 4 (x_hi: 2, x_lo: 2; x = x_hi * 2 + x_lo), y: 4, z: 4, core: 2. Of those that a mesh axis runs over, the one named last changes fastest.
Arguments:
- panel: bfloat16 [196608, 1024], P('col', 'row'), may hold values from -0.1875 to 0.1875
- rhs: float32 [1024, 196608], P('row', 'col'), may hold values from -6 to 6
- diag_inverse: bfloat16 [2, 512, 512], replicated, may hold values from -1 to 2, as said below
Outputs:
- solved: bfloat16 [1024, 1024], P(None, 'row')
- updated: float32 [1024, 196608], P('row', 'col')
Inputs may be any that keep to these rules, and one draw needn't show every extreme that they name: `diag_inverse`: each block is lower triangular; its diagonal entries are 0.5 or more.
All inputs are finite; a program needn't handle non-finite values.
Results may differ from a plain program's by a relative error of at most 0.0065.
Values may be sent and summed in bfloat16 or wider, within the bound.
A program may use at most 128 MiB of HBM per device.

v0:
```python
import jax
import jax.numpy as jnp
from jax import lax
from jax.sharding import PartitionSpec as P


def rows_for(lines, length):
    spare = -len(lines) % length
    return jnp.pad(lines, [(0, spare)] + [(0, 0)] * (lines.ndim - 1))


def broadcast_by_parts(value, axis, root):
    lines = jnp.where(lax.axis_index(axis) == root, value, jnp.zeros_like(value)).reshape(
        -1, *value.shape[1:][-1:]
    )
    padded = rows_for(lines, lax.axis_size(axis))
    own = lax.psum_scatter(padded, axis, scatter_dimension=0, tiled=True)
    return lax.all_gather(own, axis, axis=0, tiled=True)[: len(lines)].reshape(value.shape)


def from_everyone(value, axis):
    copies = jnp.broadcast_to(value, (lax.axis_size(axis), *value.shape))
    return lax.all_to_all(copies, axis, split_axis=0, concat_axis=0, tiled=True)


def taken_together(value, axis):
    return from_everyone(value, axis).sum(axis=0)


def split_up(value, dim, length):
    lengths = value.shape
    tiles = value.reshape(*lengths[:dim], length, lengths[dim] // length, *lengths[dim + 1 :])
    return jnp.moveaxis(tiles, dim, 0)


def sum_at_owner(value, axis, dim):
    tiles = split_up(value, dim, lax.axis_size(axis))
    arrived = lax.all_to_all(tiles, axis, split_axis=0, concat_axis=0, tiled=True)
    return arrived.astype(jnp.float32).sum(axis=0)


def spread_block(values, owner):
    return broadcast_by_parts(values, "col", owner)


def shards(panel, rhs, diag_inverse):
    block_size = diag_inverse.shape[1]
    step_count = diag_inverse.shape[0]
    rows_dev = panel.shape[0]
    slice_count = rhs.shape[0]
    rhs_count = slice_count * lax.axis_size("row")
    row_index = lax.axis_index("row")
    col_index = lax.axis_index("col")
    dropped = (col_index < step_count) & (row_index >= col_index)
    top_block = jnp.where(dropped, jnp.zeros_like(panel[:block_size]), panel[:block_size])
    masked = jnp.concatenate([top_block, panel[block_size:]], axis=0)
    contract = (((1,), (1,)), ((), ()))
    own_solved = jnp.zeros((rhs_count, block_size), jnp.bfloat16)
    products = jnp.zeros((rhs_count, rows_dev), jnp.float32)
    for current in range(step_count):
        inverse = diag_inverse[current].astype(jnp.float32)
        partial_value = lax.cond(
            col_index == current,
            lambda: lax.dot_general(
                own_solved, masked[:block_size], contract, preferred_element_type=jnp.float32
            ),
            lambda: jnp.zeros((rhs_count, block_size), jnp.float32),
        )
        embedded = lax.dynamic_update_slice(
            jnp.zeros((rhs_count, block_size), jnp.float32),
            rhs[:, :block_size],
            (row_index * slice_count, jnp.int32(0)),
        )
        residual = taken_together(embedded - partial_value, "row")
        whole_block = jnp.dot(residual, inverse.T, precision=lax.Precision.HIGHEST).astype(
            jnp.bfloat16
        )
        arrived = spread_block(whole_block, current)
        own_solved = jnp.where(row_index == current, arrived, own_solved)
        products = lax.cond(
            row_index == current,
            lambda: lax.dot_general(arrived, masked, contract, preferred_element_type=jnp.float32),
            lambda: products,
        )
    reduced = sum_at_owner(products.astype(jnp.bfloat16), "row", 0)
    updated = rhs - reduced
    return (own_solved, updated)


def solution(mesh):
    placed = (P("col", "row"), P("row", "col"), P())
    return jax.shard_map(
        shards,
        mesh=mesh,
        in_specs=placed,
        out_specs=(P(None, "row"), P("row", "col")),
        check_vma=False,
    )
```

profile of v0, /device:TPU:1, one launch (start us, length us, event | category | flops | bytes accessed | tf_op | source)
XLA Modules:
  0.0 1041.3 jit_solution(9920857579655382945)
XLA Ops:
  7.2 0.0 reduce-scatter.3.cloned.1.call-start
  7.2 1.1 slice_select_fusion
  8.3 0.2 broadcast.15
  8.6 1.3 slice_dynamic-update-slice_fusion
  9.9 1.6 conditional.4
  9.9 1.6 broadcast.10
  11.5 2.1 sub.9
  13.5 0.6 broadcast_in_dim.13
  14.1 50.4 %all_to_all.15 = f32[2,1024,512]{2,1,0:T(8,128)} all-to-all(f32[2,1024,512]{2,1,0:T(8,128)S(1)} %broadcast_in_dim.13), channel_id=1, replica_groups=mesh['row'=2,'col'=64] {'row'}, dimensions={0} | all-to-all | bytes 8388608 | tf_op jit(solution)/shard_map/all_to_all | solution.py:23
  64.6 4.2 reduce_sum.27
  68.7 4.5 fusion.3
  73.2 0.0 reduce-scatter.3.cloned.1.call-update
  73.2 0.0 all-gather.3.cloned.1.call-start
  73.3 334.0 %reduce-scatter.3.cloned.1.call-done = bf16[16,512]{1,0:T(8,128)(2,1)} async-done(((bf16[1024,512]{1,0:T(8,128)(2,1)}), bf16[16,512]{1,0:T(8,128)(2,1)}) %reduce-scatter.3.cloned.1.call-update) | async-done | bytes 16400 | tf_op jit(solution)/shard_map/reduce_scatter | solution.py:17
  407.3 0.0 all-gather.3.cloned.1.call-update
  407.3 0.0 reduce-scatter.5.cloned.1.call-start
  407.4 70.8 %all-gather.3.cloned.1.call-done = bf16[1024,512]{1,0:T(8,128)(2,1)} async-done(((bf16[16,512]{1,0:T(8,128)(2,1)}), bf16[1024,512]{1,0:T(8,128)(2,1)}) %all-gather.3.cloned.1.call-update) | async-done | bytes 1048592 | tf_op jit(solution)/shard_map/all_gather | solution.py:18
  478.1 2.3 broadcast_select_fusion
  480.4 3.3 conditional.5
  480.4 3.3 fusion.9
  483.7 2.1 sub.10
  485.8 0.6 broadcast_in_dim.14
  486.4 50.4 %all_to_all.16 = f32[2,1024,512]{2,1,0:T(8,128)} all-to-all(f32[2,1024,512]{2,1,0:T(8,128)S(1)} %broadcast_in_dim.14), channel_id=1, replica_groups=mesh['row'=2,'col'=64] {'row'}, dimensions={0} | all-to-all | bytes 8388608 | tf_op jit(solution)/shard_map/all_to_all | solution.py:23
  536.7 2.9 reduce_sum.28
  539.6 3.9 fusion.4
  543.4 0.0 slice-start
  543.4 0.0 reduce-scatter.5.cloned.1.call-update
  543.5 0.0 all-gather.5.cloned.1.call-start
  543.5 325.5 %reduce-scatter.5.cloned.1.call-done = bf16[16,512]{1,0:T(8,128)(2,1)} async-done(((bf16[1024,512]{1,0:T(8,128)(2,1)}), bf16[16,512]{1,0:T(8,128)(2,1)}) %reduce-scatter.5.cloned.1.call-update) | async-done | bytes 16400 | tf_op jit(solution)/shard_map/reduce_scatter | solution.py:17
  869.0 0.0 all-gather.5.cloned.1.call-update
  869.1 0.0 slice-done
  869.1 1.8 pad_maximum_fusion
  870.9 8.4 conditional.6
  870.9 8.4 fusion.10
  879.3 60.2 %all-gather.5.cloned.1.call-done = bf16[1024,512]{1,0:T(8,128)(2,1)} async-done(((bf16[16,512]{1,0:T(8,128)(2,1)}), bf16[1024,512]{1,0:T(8,128)(2,1)}) %all-gather.5.cloned.1.call-update) | async-done | bytes 1048592 | tf_op jit(solution)/shard_map/all_gather | solution.py:18
  939.5 0.0 copy-start
  939.5 0.0 copy-start.1
  939.5 10.1 all-to-all-start.2
  949.6 0.0 copy-done
  949.6 0.0 copy-done.1
  949.6 1.1 broadcast_select_fusion.1
  950.7 72.5 %all-to-all-done.2 = bf16[2,512,3072]{2,1,0:T(8,128)(2,1)} async-done(((bf16[2,512,3072]{2,1,0:T(8,128)(2,1)}), bf16[2,512,3072]{2,1,0:T(8,128)(2,1)}, u32[]{:S(2)}, u32[]{:S(2)}) %all-to-all-start.2) | async-done | bytes 6291488 | tf_op jit(solution)/shard_map/all_to_all | solution.py:38
  1023.1 5.0 convert_reduce_fusion
  1028.1 6.6 sub.11
  (1 shorter events, 0.0 us)
Async XLA Ops:
  7.2 400.1 %reduce-scatter.3.cloned.1.call-start = ((), (), s32[]{:S(2)}) async-start(), calls=%async_computation.5 | async-start | bytes 1064960 | tf_op jit(solution)/shard_map/reduce_scatter | solution.py:17
  73.2 404.9 %all-gather.3.cloned.1.call-start = ((), (), s32[]{:S(2)}) async-start(), calls=%async_computation.6 | async-start | bytes 1064960 | tf_op jit(solution)/shard_map/all_gather | solution.py:18
  407.3 461.7 %reduce-scatter.5.cloned.1.call-start = ((), (), s32[]{:S(2)}) async-start(), calls=%async_computation.7 | async-start | bytes 1064960 | tf_op jit(solution)/shard_map/reduce_scatter | solution.py:17
  543.4 325.6 %slice-start = ((bf16[3072,512]{1,0:T(8,128)(2,1)}), bf16[2560,512]{1,0:T(8,128)(2,1)S(1)}, s32[]{:S(2)}) async-start(bf16[3072,512]{1,0:T(8,128)(2,1)} %param.11), calls=%async_computation.9 | async-start | bytes 5242880 | tf_op jit(solution)/shard_map/slice | solution.py:56
  543.5 396.0 %all-gather.5.cloned.1.call-start = ((), (), s32[]{:S(2)}) async-start(), calls=%async_computation.8 | async-start | bytes 1064960 | tf_op jit(solution)/shard_map/all_gather | solution.py:18
  939.5 10.1 copy-start
  939.5 10.1 copy-start.1
  939.5 83.6 %all-to-all-start.2 = ((bf16[2,512,3072]{2,1,0:T(8,128)(2,1)}), bf16[2,512,3072]{2,1,0:T(8,128)(2,1)}, u32[]{:S(2)}, u32[]{:S(2)}) async-start(bf16[2,512,3072]{2,1,0:T(8,128)(2,1)} %bitcast.16), calls=%async_computation.4 | async-start | bytes 12582912 | tf_op jit(solution)/shard_map/all_to_all | solution.py:38
Sparse Core Ops, SparseCore 0:
  73.3 333.9 reduce-scatter.2
  410.5 67.5 all-gather.2
  543.6 325.4 reduce-scatter.4
  872.1 67.3 all-gather.4
where the time goes:
time: 1040 us
  waiting for transfers between devices  863 us (83%)
  blocking collectives  101 us (10%)
  other arithmetic  29 us (3%)
  matrix products  20 us (2%)
  between operations  13.8 us (1%)
    reduce_scatter x2, waiting for transfers between devices, broadcast_by_parts(): own = lax.psum_scatter(padded, axis, scatter_dimension=0, tiled=True)  660 us
    all_gather x2, waiting for transfers between devices, broadcast_by_parts(): lax.all_gather(own, axis, axis=0, tiled=True)[:len(lines)]  131 us
    all_to_all x2, blocking collectives, from_everyone(): return lax.all_to_all(copies, axis, split_axis=0, concat_axis=0, tiled=True)  101 us
    all_to_all x1, waiting for transfers between devices, sum_at_owner(): lax.all_to_all(tiles, axis, split_axis=0, concat_axis=0, tiled=True)  72.5 us
  transfers between devices with their start and end apart: 5, of which 5 were waited for; matrix products, arithmetic and copies ran while one was open for 1% of the time, Pallas kernels for 0%

commit v1 on v0

v1 whole, which is shorter than its diff:
```python
import functools

import jax
import jax.numpy as jnp
from jax import lax
from jax.experimental import pallas as pl
from jax.experimental.pallas import tpu as pltpu
from jax.sharding import PartitionSpec as P

MESH = pl.DeviceIdType.MESH
NT = (((1,), (1,)), ((), ()))
SIDE = 4
PIECES = SIDE * SIDE
CHUNK = 256
FIRST = 4


def remote(src, dst, send, recv, row, col):
    return pltpu.make_async_remote_copy(
        src_ref=src, dst_ref=dst, send_sem=send, recv_sem=recv,
        device_id=(row, col), device_id_type=MESH,
    )


def kernel(
    panel, rhs, inverse, updated, solved,
    own, other, work, mine, cross, made, before, inv,
    panel_send, panel_recv, scatter_send, scatter_recv, before_send, before_recv,
    x_send, x_recv, y_send, y_recv, z_send, z_recv, core_send, core_recv,
    load_sem, store_sem, solved_sem,
):
    block = inv.shape[0]
    rows_dev = own.shape[0]
    chunks = rows_dev // CHUNK
    row = lax.axis_index("row")
    col = lax.axis_index("col")
    core = lax.rem(col, 2)
    x_hi = lax.rem(col // 2, 2)
    piece = col // 4
    y = lax.rem(piece, SIDE)
    z = piece // SIDE
    length = block // PIECES
    plane = length * SIDE
    has_cross = core == row

    def at(z_, y_, x_, core_):
        return ((z_ * SIDE + y_) * 2 + x_) * 2 + core_

    load_own = pltpu.make_async_copy(panel, own, load_sem.at[0])
    load_first = pltpu.make_async_copy(
        rhs.at[:, pl.ds(0, block)], work.at[:, pl.ds(0, block)], load_sem.at[1]
    )
    load_rest = pltpu.make_async_copy(
        rhs.at[:, pl.ds(block, rows_dev - block)],
        work.at[:, pl.ds(block, rows_dev - block)],
        load_sem.at[2],
    )
    load_inv = pltpu.make_async_copy(inverse.at[core], inv, load_sem.at[3])
    load_first.start()

    @pl.when(col < 2)
    def _():
        load_inv.start()

    barrier = pltpu.get_barrier_semaphore()

    def greet(row_, col_):
        pl.semaphore_signal(barrier, inc=1, device_id=(row_, col_), device_id_type=MESH)

    greet(1 - row, col)
    greet(row, at(z, y, x_hi, 1 - core))
    greet(row, at(z, y, 1 - x_hi, core))
    greet(1 - row, at(z, y, 1 - x_hi, core))
    for d in range(1, SIDE):
        greet(row, at(z, lax.rem(y + d, SIDE), x_hi, core))
        greet(row, at(lax.rem(z + d, SIDE), y, x_hi, core))

    @pl.when(col < 2)
    def _():
        @pl.loop(1, PIECES)
        def _(p):
            greet(row, p * 4 + core)

    @pl.when((x_hi == 0) & (piece > 0))
    def _():
        greet(row, core)

    pl.semaphore_wait(
        barrier,
        10 + jnp.where(col < 2, PIECES - 1, 0) + jnp.where((x_hi == 0) & (piece > 0), 1, 0),
    )

    def panel_copy(j):
        part = pl.ds(pl.multiple_of(j * CHUNK, CHUNK), CHUNK)
        return remote(
            panel.at[part], other.at[part], panel_send.at[j], panel_recv.at[j], 1 - row, col
        )

    @pl.loop(0, FIRST)
    def _(j):
        panel_copy(j).start()

    load_own.start()
    load_rest.start()
    load_first.wait()
    load_own.wait()
    load_rest.wait()

    before_copy = remote(made, before, before_send, before_recv, row, 1)

    def scatter_copy(p):
        part = pl.ds(pl.multiple_of(p * length, length), length)
        return remote(
            made.at[part], mine.at[core, part], scatter_send.at[p], scatter_recv, row, p * 4 + core
        )

    def solve(factor):
        @pl.loop(0, 4)
        def _(i):
            tall = block // 4
            part = pl.ds(pl.multiple_of(i * tall, tall), tall)
            rest = work[part, :block]
            if factor is not None:
                rest = rest - lax.dot_general(
                    before[part, :], factor[:block, :], NT, preferred_element_type=jnp.float32
                )
            top = rest.astype(jnp.bfloat16)
            rest = rest - top.astype(jnp.float32)
            middle = rest.astype(jnp.bfloat16)
            low = (rest - middle.astype(jnp.float32)).astype(jnp.bfloat16)
            total = lax.dot_general(low, inv[...], NT, preferred_element_type=jnp.float32)
            total += lax.dot_general(middle, inv[...], NT, preferred_element_type=jnp.float32)
            total += lax.dot_general(top, inv[...], NT, preferred_element_type=jnp.float32)
            made[part, :] = total.astype(jnp.bfloat16)

    @pl.when(col < 2)
    def _():
        load_inv.wait()

        @pl.when(col == 0)
        def _():
            solve(None)
            before_copy.start()

        @pl.when(col == 1)
        def _():
            before_copy.wait_recv()

            @pl.when(row == 0)
            def _():
                solve(own)

            @pl.when(row == 1)
            def _():
                for j in range(block // CHUNK):
                    panel_copy(j).wait_recv()
                solve(other)

        @pl.loop(1, PIECES)
        def _(p):
            scatter_copy(p).start()

        mine[core, :length, :] = made[:length, :]

    def spot(p, count=1):
        return pl.ds(pl.multiple_of(p * length, length), length * count)

    here = spot(piece)
    x_across = remote(
        mine.at[core, here], mine.at[core, here], x_send.at[0], x_recv.at[0], row, at(z, y, 1, core)
    )
    x_cross = [
        remote(
            mine.at[core, here], cross.at[here], x_send.at[1 + i], x_recv.at[1],
            1 - row, at(z, y, i, core),
        )
        for i in range(2)
    ]

    @pl.when(x_hi == 0)
    def _():
        @pl.when(piece > 0)
        def _():
            scatter_copy(piece).wait_recv()

        x_across.start()

        @pl.when(~has_cross)
        def _():
            for copy in x_cross:
                copy.start()

    @pl.loop(FIRST, chunks)
    def _(j):
        panel_copy(j).start()

    @pl.when(x_hi == 1)
    def _():
        x_across.wait_recv()

    def y_copy(which, buffer, d, p):
        return remote(
            buffer.at[spot(p)], buffer.at[spot(p)], y_send.at[which, d - 1], y_recv.at[which, d - 1],
            row, at(z, lax.rem(y + d, SIDE), x_hi, core),
        )

    def z_copy(which, buffer, d, p):
        return remote(
            buffer.at[spot(p, SIDE)], buffer.at[spot(p, SIDE)],
            z_send.at[which, d - 1], z_recv.at[which, d - 1],
            row, at(lax.rem(z + d, SIDE), y, x_hi, core),
        )

    own_half = mine.at[core]
    for d in range(1, SIDE):
        y_copy(0, own_half, d, piece).start()

    @pl.when(has_cross)
    def _():
        x_cross[0].wait_recv()
        for d in range(1, SIDE):
            y_copy(1, cross, d, piece).start()

    def y_from(d):
        return z * SIDE + lax.rem(y + SIDE - d, SIDE)

    def z_from(d):
        return lax.rem(z + SIDE - d, SIDE) * SIDE

    for d in range(1, SIDE):
        y_copy(0, own_half, d, y_from(d)).wait_recv()
    for d in range(1, SIDE):
        z_copy(0, own_half, d, z * SIDE).start()

    @pl.when(has_cross)
    def _():
        for d in range(1, SIDE):
            y_copy(1, cross, d, y_from(d)).wait_recv()
        for d in range(1, SIDE):
            z_copy(1, cross, d, z * SIDE).start()

    buddy = at(z, y, x_hi, 1 - core)
    give = remote(own_half, own_half, core_send.at[0], core_recv.at[0], row, buddy)
    theirs = mine.at[1 - core]
    take = remote(theirs, theirs, core_send.at[0], core_recv.at[0], row, buddy)
    share_cross = remote(cross, cross, core_send.at[1], core_recv.at[1], row, buddy)

    for d in range(1, SIDE):
        z_copy(0, own_half, d, z_from(d)).wait_recv()
    give.start()

    @pl.when(has_cross)
    def _():
        for d in range(1, SIDE):
            z_copy(1, cross, d, z_from(d)).wait_recv()
        share_cross.start()

    take.wait_recv()

    @pl.when(~has_cross)
    def _():
        share_cross.wait_recv()

    put_mine = pltpu.make_async_copy(
        mine.at[row], solved.at[pl.ds(pl.multiple_of(row * block, block), block)], solved_sem.at[0]
    )
    put_cross = pltpu.make_async_copy(
        cross, solved.at[pl.ds(pl.multiple_of((1 - row) * block, block), block)], solved_sem.at[1]
    )
    put_mine.start()
    put_cross.start()

    @pl.when((col < 2) & (row >= col))
    def _():
        own[:block, :] = jnp.zeros((block, own.shape[1]), own.dtype)

    @pl.when(~((col == 1) & (row == 1)))
    def _():
        for j in range(block // CHUNK):
            panel_copy(j).wait_recv()

    @pl.when((col < 2) & (1 - row >= col))
    def _():
        other[:block, :] = jnp.zeros((block, other.shape[1]), other.dtype)

    def store(j):
        part = pl.ds(pl.multiple_of(j * CHUNK, CHUNK), CHUNK)
        return pltpu.make_async_copy(work.at[:, part], updated.at[:, part], store_sem.at[j])

    def update(j):
        part = pl.ds(pl.multiple_of(j * CHUNK, CHUNK), CHUNK)
        total = lax.dot_general(
            mine[row], own[part, :], NT, preferred_element_type=jnp.float32
        )
        total += lax.dot_general(
            mine[1 - row], other[part, :], NT, preferred_element_type=jnp.float32
        )
        work[:, part] -= total
        store(j).start()

    @pl.loop(0, block // CHUNK)
    def _(j):
        update(j)

    @pl.loop(block // CHUNK, chunks)
    def _(j):
        panel_copy(j).wait_recv()
        update(j)

    @pl.loop(0, chunks)
    def _(j):
        panel_copy(j).wait_send()
        store(j).wait()

    put_mine.wait()
    put_cross.wait()
    give.wait_send()
    for d in range(1, SIDE):
        y_copy(0, own_half, d, piece).wait_send()
        z_copy(0, own_half, d, z * SIDE).wait_send()

    @pl.when(has_cross)
    def _():
        share_cross.wait_send()
        for d in range(1, SIDE):
            y_copy(1, cross, d, piece).wait_send()
            z_copy(1, cross, d, z * SIDE).wait_send()

    @pl.when(x_hi == 0)
    def _():
        x_across.wait_send()

        @pl.when(~has_cross)
        def _():
            for copy in x_cross:
                copy.wait_send()

    @pl.when(col < 2)
    def _():
        @pl.when(col == 0)
        def _():
            before_copy.wait_send()

        @pl.loop(1, PIECES)
        def _(p):
            scatter_copy(p).wait_send()


def shards(panel, rhs, inverse):
    rows_dev, width = panel.shape
    half = rhs.shape[0]
    block = inverse.shape[1]
    chunks = rows_dev // CHUNK
    any_space = pl.BlockSpec(memory_space=pl.ANY)
    dma = pltpu.SemaphoreType.DMA
    updated, solved = pl.pallas_call(
        kernel,
        out_shape=(
            jax.ShapeDtypeStruct(rhs.shape, jnp.float32),
            jax.ShapeDtypeStruct((2 * half, block), jnp.bfloat16),
        ),
        in_specs=[any_space] * 3,
        out_specs=(any_space, any_space),
        scratch_shapes=[
            pltpu.VMEM((rows_dev, width), jnp.bfloat16),
            pltpu.VMEM((rows_dev, width), jnp.bfloat16),
            pltpu.VMEM(rhs.shape, jnp.float32),
            pltpu.VMEM((2, half, block), jnp.bfloat16),
            pltpu.VMEM((half, block), jnp.bfloat16),
            pltpu.VMEM((half, block), jnp.bfloat16),
            pltpu.VMEM((half, block), jnp.bfloat16),
            pltpu.VMEM((block, block), jnp.bfloat16),
            dma((chunks,)), dma((chunks,)), dma((PIECES,)), dma, dma, dma,
            dma((3,)), dma((2,)), dma((2, 3)), dma((2, 3)), dma((2, 3)), dma((2, 3)),
            dma((2,)), dma((2,)),
            dma((4,)), dma((chunks,)), dma((2,)),
        ],
        compiler_params=pltpu.CompilerParams(collective_id=0, has_side_effects=True),
        name="window",
    )(panel, rhs, inverse)
    return solved, updated


def solution(mesh):
    return jax.shard_map(
        shards,
        mesh=mesh,
        in_specs=(P("col", "row"), P("row", "col"), P()),
        out_specs=(P(None, "row"), P("row", "col")),
        check_vma=False,
    )
```

time: 1040 us -> 89.2 us (0.09)
  waiting for transfers between devices: 863 us -> 0 us
  blocking collectives: 101 us -> 0 us
  Pallas kernels: 0 us -> 79.3 us
  other arithmetic: 29 us -> 0 us
  matrix products: 20 us -> 0 us
  between operations: 13.8 us -> 0.64 us
    reduce_scatter x2 -> x0, waiting for transfers between devices: 660 us -> none  [broadcast_by_parts(): own = lax.psum_scatter(padded, axis, scatter_dimension=0, tiled=True)]
    all_gather x2 -> x0, waiting for transfers between devices: 131 us -> none  [broadcast_by_parts(): lax.all_gather(own, axis, axis=0, tiled=True)[:len(lines)]]
    all_to_all x2 -> x0, blocking collectives: 101 us -> none  [from_everyone(): return lax.all_to_all(copies, axis, split_axis=0, concat_axis=0, tiled=True)]
    pallas_call x0 -> x1, Pallas kernels: none -> 79.3 us  [shards(): pl.pallas_call(kernel, out_shape=(jax.ShapeDtypeStruct(rhs.shape, jnp.flo...]
    all_to_all x1 -> x0, waiting for transfers between devices: 72.5 us -> none  [sum_at_owner(): lax.all_to_all(tiles, axis, split_axis=0, concat_axis=0, tiled=True)]
    dot_general x4 -> x0, matrix products: 20 us -> none  [the longest x1 8.38 us: shards(): lax.dot_general(arrived, masked, contract, preferred_element_type=jnp.flo...]
    reduce_sum x3 -> x0, other arithmetic: 12 us -> none  [the longest x2 7.02 us: taken_together(): return from_everyone(value, axis).sum(axis=0)]
    sub x3 -> x0, other arithmetic: 10.7 us -> none  [the longest x1 6.62 us: shards(): updated = rhs - reduced]
  transfers between devices with their start and end apart: 5 -> 0, of which waited for: 5 -> 0; matrix products, arithmetic and copies ran while one was open for 1% -> 0% of each run, Pallas kernels for 0% -> 0%
where the time goes in v1:
time: 89.2 us; the launch traced here: 88.5 us
  Pallas kernels  79.3 us (89%)
  local copies, waits for them, and re-layouts  8.5 us (10%)
    pallas_call x1, Pallas kernels, shards(): pl.pallas_call(kernel, out_shape=(jax.ShapeDtypeStruct(rhs.shape, jnp.flo...  79.3 us
    unnamed x2, local copies, waits for them, and re-layouts  8.5 us

profile of v1, /device:TPU:1, one launch (start us, length us, event | category | flops | bytes accessed | tf_op | source)
XLA Modules:
  0.0 88.5 jit_solution(5408343109572799829)
XLA Ops:
  0.6 79.3 %window.1 = (f32[512,3072]{1,0:T(8,128)}, bf16[1024,512]{1,0:T(8,128)(2,1)}) custom-call(bf16[3072,512]{1,0:T(8,128)(2,1)} %panel.1, f32[512,3072]{1,0:T(8,128)} %rhs.1, bf16[2,512,512]{2,1,0:T(8,128)(2,1)} %inverse.1), custom_call_target="tpu_custom_call" | custom-call | tf_op jit(solution)/shard_map/window/pallas_call | solution.py:356
  80.0 2.3 %copy.7 = bf16[1024,512]{1,0:T(8,128)(2,1)} copy(bf16[1024,512]{1,0:T(8,128)(2,1)} %get-tuple-element.8) | data formatting | bytes 2097152
  82.2 6.2 %copy.8 = f32[512,3072]{1,0:T(8,128)} copy(f32[512,3072]{1,0:T(8,128)} %get-tuple-element.9) | data formatting | bytes 12582912

commit v2 on v1

--- a/solution.py
+++ b/solution.py
@@ -12,6 +12,7 @@
 SIDE = 4
 PIECES = SIDE * SIDE
 CHUNK = 256
+STORES = 8
 FIRST = 4
 
 
@@ -23,11 +24,11 @@
 
 
 def kernel(
-    panel, rhs, inverse, updated, solved,
-    own, other, work, mine, cross, made, before, inv,
+    panel, rhs, inverse, work, solved,
+    own, other, mine, cross, made, before, inv,
     panel_send, panel_recv, scatter_send, scatter_recv, before_send, before_recv,
     x_send, x_recv, y_send, y_recv, z_send, z_recv, core_send, core_recv,
-    load_sem, store_sem, solved_sem,
+    load_sem,
 ):
     block = inv.shape[0]
     rows_dev = own.shape[0]
@@ -96,7 +97,19 @@
             panel.at[part], other.at[part], panel_send.at[j], panel_recv.at[j], 1 - row, col
         )
 
-    @pl.loop(0, FIRST)
+    own_dropped = (col < 2) & (row >= col)
+    other_dropped = (col < 2) & (1 - row >= col)
+    top = block // CHUNK
+
+    def top_copies(act):
+        for j in range(top):
+            act(panel_copy(j))
+
+    @pl.when(~own_dropped)
+    def _():
+        top_copies(lambda copy: copy.start())
+
+    @pl.loop(top, FIRST)
     def _(j):
         panel_copy(j).start()
 
@@ -124,13 +137,13 @@
                 rest = rest - lax.dot_general(
                     before[part, :], factor[:block, :], NT, preferred_element_type=jnp.float32
                 )
-            top = rest.astype(jnp.bfloat16)
-            rest = rest - top.astype(jnp.float32)
+            high = rest.astype(jnp.bfloat16)
+            rest = rest - high.astype(jnp.float32)
             middle = rest.astype(jnp.bfloat16)
             low = (rest - middle.astype(jnp.float32)).astype(jnp.bfloat16)
             total = lax.dot_general(low, inv[...], NT, preferred_element_type=jnp.float32)
             total += lax.dot_general(middle, inv[...], NT, preferred_element_type=jnp.float32)
-            total += lax.dot_general(top, inv[...], NT, preferred_element_type=jnp.float32)
+            total += lax.dot_general(high, inv[...], NT, preferred_element_type=jnp.float32)
             made[part, :] = total.astype(jnp.bfloat16)
 
     @pl.when(col < 2)
@@ -152,8 +165,7 @@
 
             @pl.when(row == 1)
             def _():
-                for j in range(block // CHUNK):
-                    panel_copy(j).wait_recv()
+                top_copies(lambda copy: copy.wait_recv())
                 solve(other)
 
         @pl.loop(1, PIECES)
@@ -261,31 +273,20 @@
     def _():
         share_cross.wait_recv()
 
-    put_mine = pltpu.make_async_copy(
-        mine.at[row], solved.at[pl.ds(pl.multiple_of(row * block, block), block)], solved_sem.at[0]
-    )
-    put_cross = pltpu.make_async_copy(
-        cross, solved.at[pl.ds(pl.multiple_of((1 - row) * block, block), block)], solved_sem.at[1]
-    )
-    put_mine.start()
-    put_cross.start()
-
-    @pl.when((col < 2) & (row >= col))
+    solved[pl.ds(pl.multiple_of(row * block, block), block), :] = mine[row]
+    solved[pl.ds(pl.multiple_of((1 - row) * block, block), block), :] = cross[...]
+
+    @pl.when(own_dropped)
     def _():
         own[:block, :] = jnp.zeros((block, own.shape[1]), own.dtype)
 
-    @pl.when(~((col == 1) & (row == 1)))
-    def _():
-        for j in range(block // CHUNK):
-            panel_copy(j).wait_recv()
-
-    @pl.when((col < 2) & (1 - row >= col))
+    @pl.when(other_dropped)
     def _():
         other[:block, :] = jnp.zeros((block, other.shape[1]), other.dtype)
 
-    def store(j):
-        part = pl.ds(pl.multiple_of(j * CHUNK, CHUNK), CHUNK)
-        return pltpu.make_async_copy(work.at[:, part], updated.at[:, part], store_sem.at[j])
+    @pl.when(~other_dropped & ~((col == 1) & (row == 1)))
+    def _():
+        top_copies(lambda copy: copy.wait_recv())
 
     def update(j):
         part = pl.ds(pl.multiple_of(j * CHUNK, CHUNK), CHUNK)
@@ -296,24 +297,25 @@
             mine[1 - row], other[part, :], NT, preferred_element_type=jnp.float32
         )
         work[:, part] -= total
-        store(j).start()
-
-    @pl.loop(0, block // CHUNK)
+
+    @pl.loop(0, top)
     def _(j):
         update(j)
 
-    @pl.loop(block // CHUNK, chunks)
+    @pl.loop(top, chunks)
     def _(j):
         panel_copy(j).wait_recv()
         update(j)
 
-    @pl.loop(0, chunks)
+    @pl.when(~own_dropped)
+    def _():
+        top_copies(lambda copy: copy.wait_send())
+
+    @pl.loop(top, chunks)
     def _(j):
         panel_copy(j).wait_send()
-        store(j).wait()
-
-    put_mine.wait()
-    put_cross.wait()
+
+
     give.wait_send()
     for d in range(1, SIDE):
         y_copy(0, own_half, d, piece).wait_send()
@@ -344,6 +346,18 @@
         @pl.loop(1, PIECES)
         def _(p):
             scatter_copy(p).wait_send()
+
+
+def flush(work, made, updated, solved, sem):
+    rows = work.shape[0] // STORES
+    copies = [pltpu.make_async_copy(made, solved, sem.at[STORES])]
+    for i in range(STORES):
+        part = pl.ds(i * rows, rows)
+        copies.append(pltpu.make_async_copy(work.at[part], updated.at[part], sem.at[i]))
+    for copy in copies:
+        copy.start()
+    for copy in copies:
+        copy.wait()
 
 
 def shards(panel, rhs, inverse):
@@ -351,20 +365,23 @@
     half = rhs.shape[0]
     block = inverse.shape[1]
     chunks = rows_dev // CHUNK
-    any_space = pl.BlockSpec(memory_space=pl.ANY)
+    on_chip = pl.BlockSpec(memory_space=pltpu.VMEM)
     dma = pltpu.SemaphoreType.DMA
-    updated, solved = pl.pallas_call(
+    in_hbm = pl.BlockSpec(memory_space=pltpu.HBM)
+    panel, rhs, inverse = (
+        pltpu.with_memory_space_constraint(value, pltpu.HBM) for value in (panel, rhs, inverse)
+    )
+    work, made = pl.pallas_call(
         kernel,
         out_shape=(
-            jax.ShapeDtypeStruct(rhs.shape, jnp.float32),
-            jax.ShapeDtypeStruct((2 * half, block), jnp.bfloat16),
+            pltpu.VMEM(rhs.shape, jnp.float32),
+            pltpu.VMEM((2 * half, block), jnp.bfloat16),
         ),
-        in_specs=[any_space] * 3,
-        out_specs=(any_space, any_space),
+        in_specs=[in_hbm] * 3,
+        out_specs=(on_chip, on_chip),
         scratch_shapes=[
             pltpu.VMEM((rows_dev, width), jnp.bfloat16),
             pltpu.VMEM((rows_dev, width), jnp.bfloat16),
-            pltpu.VMEM(rhs.shape, jnp.float32),
             pltpu.VMEM((2, half, block), jnp.bfloat16),
             pltpu.VMEM((half, block), jnp.bfloat16),
             pltpu.VMEM((half, block), jnp.bfloat16),
@@ -373,11 +390,25 @@
             dma((chunks,)), dma((chunks,)), dma((PIECES,)), dma, dma, dma,
             dma((3,)), dma((2,)), dma((2, 3)), dma((2, 3)), dma((2, 3)), dma((2, 3)),
             dma((2,)), dma((2,)),
-            dma((4,)), dma((chunks,)), dma((2,)),
+            dma((4,)),
         ],
-        compiler_params=pltpu.CompilerParams(collective_id=0, has_side_effects=True),
+        compiler_params=pltpu.CompilerParams(
+            collective_id=0, has_side_effects=True, vmem_limit_bytes=24 << 20
+        ),
         name="window",
     )(panel, rhs, inverse)
+    updated, solved = pl.pallas_call(
+        flush,
+        out_shape=(
+            jax.ShapeDtypeStruct(rhs.shape, jnp.float32),
+            jax.ShapeDtypeStruct((2 * half, block), jnp.bfloat16),
+        ),
+        in_specs=[on_chip] * 2,
+        out_specs=(in_hbm, in_hbm),
+        scratch_shapes=[dma((STORES + 1,))],
+        compiler_params=pltpu.CompilerParams(vmem_limit_bytes=16 << 20),
+        name="flush",
+    )(work, made)
     return solved, updated
 
 

time: 89.2 us -> 79.8 us (0.89)
  the two profiles are of different devices: /device:TPU:1 before, /device:TPU:8 now
where the time goes in v2:
time: 79.8 us; the launch traced here: 79.7 us
  Pallas kernels  79.1 us (99%)
    pallas_call x1, Pallas kernels, shards(): pl.pallas_call(kernel, out_shape=(pltpu.VMEM(rhs.shape, jnp.float32), plt...  76 us
    pallas_call x1, Pallas kernels, shards(): pl.pallas_call(flush, out_shape=(jax.ShapeDtypeStruct(rhs.shape, jnp.floa...  3.05 us

profile of v2, /device:TPU:8, one launch (start us, length us, event | category | flops | bytes accessed | tf_op | source)
XLA Modules:
  0.0 79.7 jit_solution(17195226962639805840)
XLA Ops:
  0.6 76.0 %window.1 = (f32[512,3072]{1,0:T(8,128)S(1)}, bf16[1024,512]{1,0:T(8,128)(2,1)S(1)}) custom-call(bf16[3072,512]{1,0:T(8,128)(2,1)} %panel.1, f32[512,3072]{1,0:T(8,128)} %rhs.1, bf16[2,512,512]{2,1,0:T(8,128)(2,1)} %inverse.1), custom_call_target="tpu_custom_call" | custom-call | tf_op jit(solution)/shard_map/window/pallas_call | solution.py:374
  76.7 3.0 %flush.1 = (f32[512,3072]{1,0:T(8,128)}, bf16[1024,512]{1,0:T(8,128)(2,1)}) custom-call(f32[512,3072]{1,0:T(8,128)S(1)} %get-tuple-element.6.work, bf16[1024,512]{1,0:T(8,128)(2,1)S(1)} %get-tuple-element.7.made), custom_call_target="tpu_custom_call" | custom-call | tf_op jit(solution)/shard_map/flush/pallas_call | solution.py:400

commit v3 on v0

v3 whole, which is shorter than its diff:
```python
import functools

import jax
import jax.numpy as jnp
from jax import lax
from jax.experimental import pallas as pl
from jax.experimental.pallas import tpu as pltpu
from jax.sharding import PartitionSpec as P


MESH = pl.DeviceIdType.MESH
NT = (((1,), (1,)), ((), ()))
SIDE = 4
PIECES = SIDE * SIDE
CHUNK = 256
PARTS = (512, 768, 768, 768, 256)
EARLY = 2
DMA = pltpu.SemaphoreType.DMA
HBM = pl.BlockSpec(memory_space=pltpu.HBM)
VMEM = pl.BlockSpec(memory_space=pltpu.VMEM)
ANY = pl.BlockSpec(memory_space=pl.ANY)
BUSY = pl.CostEstimate(flops=10**10, bytes_accessed=10**6, transcendentals=0)


def place():
    row = lax.axis_index("row")
    col = lax.axis_index("col")
    piece = col // 4
    return row, col, lax.rem(col, 2), lax.rem(col // 2, 2), piece // SIDE, lax.rem(piece, SIDE)


def at(z, y, x, core):
    return ((z * SIDE + y) * 2 + x) * 2 + core


def remote(src, dst, send, recv, row, col):
    return pltpu.make_async_remote_copy(
        src_ref=src, dst_ref=dst, send_sem=send, recv_sem=recv,
        device_id=(row, col), device_id_type=MESH,
    )


def greet(row, col):
    pl.semaphore_signal(
        pltpu.get_barrier_semaphore(), inc=1, device_id=(row, col), device_id_type=MESH
    )


def rows(i, length):
    return pl.ds(pl.multiple_of(i * length, length), length)


def cut_kernel(panel, after, *refs):
    *parts, sem = refs
    start = panel.shape[0] - sum(part.shape[0] for part in parts)
    copies = []
    for i, part in enumerate(parts):
        copies.append(
            pltpu.make_async_copy(panel.at[pl.ds(start, part.shape[0])], part, sem.at[i])
        )
        start += part.shape[0]
    for copy in copies:
        copy.start()
    for copy in copies:
        copy.wait()


def first_kernel(panel, part, sem):
    copy = pltpu.make_async_copy(panel.at[pl.ds(0, part.shape[0])], part, sem)
    copy.start()
    copy.wait()


def cut(panel, lengths):
    width = panel.shape[1]
    params = pltpu.CompilerParams(vmem_limit_bytes=8 << 20)
    first = pl.pallas_call(
        first_kernel,
        out_shape=pltpu.VMEM((lengths[0], width), panel.dtype),
        in_specs=[HBM],
        out_specs=VMEM,
        scratch_shapes=[DMA],
        compiler_params=params,
        name="cut_first",
    )(panel)
    others = pl.pallas_call(
        cut_kernel,
        out_shape=tuple(pltpu.VMEM((length, width), panel.dtype) for length in lengths[1:]),
        in_specs=[HBM, ANY],
        out_specs=(VMEM,) * len(lengths[1:]),
        scratch_shapes=[DMA((len(lengths) - 1,))],
        compiler_params=params,
        name="cut_others",
    )(panel, first)
    return [first, *others]


def solve(value, before, below, inv, made):
    tall = made.shape[0] // 4

    @pl.loop(0, 4)
    def _(i):
        part = rows(i, tall)
        rest = value[part, : made.shape[1]]
        if below is not None:
            rest = rest - lax.dot_general(
                before[part, :], below[...], NT, preferred_element_type=jnp.float32
            )
        high = rest.astype(jnp.bfloat16)
        rest = rest - high.astype(jnp.float32)
        middle = rest.astype(jnp.bfloat16)
        low = (rest - middle.astype(jnp.float32)).astype(jnp.bfloat16)
        total = lax.dot_general(low, inv[...], NT, preferred_element_type=jnp.float32)
        total += lax.dot_general(middle, inv[...], NT, preferred_element_type=jnp.float32)
        total += lax.dot_general(high, inv[...], NT, preferred_element_type=jnp.float32)
        made[part, :] = total.astype(jnp.bfloat16)


def piece_rows(h, z, y, half):
    length = half // (2 * PIECES)
    index = z * SIDE + y if h == 0 else y * SIDE + z
    return pl.ds(pl.multiple_of(h * (half // 2) + index * length, length), length)


def scatter_copy(h, p, made, land, send, recv, row, core):
    length = land.shape[0] // 2
    source = made.at[piece_rows(h, p // SIDE, lax.rem(p, SIDE), made.shape[0])]
    return remote(
        source, land.at[pl.ds(h * length, length)], send.at[h, p], recv.at[h], row, p * 4 + core
    )


def keep_own(made, piece_out):
    length = piece_out.shape[0] // 2
    for h in range(2):
        piece_out[h * length : (h + 1) * length, :] = made[piece_rows(h, 0, 0, made.shape[0]), :]


def early_kernel(
    rhs, panel, inverse, after, held, piece_out, before,
    factor, inv, made, land, load_sem, scatter_send, scatter_recv, before_send, before_recv,
):
    row, col, core, x_hi, _, _ = place()
    piece = col // 4
    block = inv.shape[0]
    late = (row == 1) & (core == 1)

    load_value = pltpu.make_async_copy(
        rhs.at[:, pl.ds(0, block)], held.at[:, pl.ds(0, block)], load_sem.at[0]
    )
    others = pl.ds(block, rhs.shape[1] - block)
    load_others = pltpu.make_async_copy(rhs.at[:, others], held.at[:, others], load_sem.at[1])
    load_value.start()
    before_copy = remote(made, before, before_send, before_recv, row, 1)

    @pl.when(col < 2)
    def _():
        load_inv = pltpu.make_async_copy(inverse.at[core], inv, load_sem.at[2])
        load_factor = pltpu.make_async_copy(panel.at[pl.ds(0, block)], factor, load_sem.at[3])
        load_inv.start()
        load_factor.start()
        greet(row, 1 - core)

        @pl.when(~late)
        def _():
            @pl.loop(1, PIECES)
            def _(p):
                greet(row, p * 4 + core)

        load_others.start()
        pl.semaphore_wait(
            pltpu.get_barrier_semaphore(), 1 + jnp.where(late, 0, PIECES - 1)
        )
        load_value.wait()
        load_inv.wait()
        load_factor.wait()

        @pl.when(col == 0)
        def _():
            solve(held, None, None, inv, made)
            before_copy.start()

        @pl.when(col == 1)
        def _():
            before_copy.wait_recv()

            @pl.when(row == 0)
            def _():
                solve(held, before, factor, inv, made)

        @pl.when(~late)
        def _():
            @pl.loop(1, PIECES)
            def _(p):
                for h in range(2):
                    scatter_copy(h, p, made, land, scatter_send, scatter_recv, row, core).start()

            keep_own(made, piece_out)

        @pl.when(col == 0)
        def _():
            before_copy.wait_send()

        @pl.when(~late)
        def _():
            @pl.loop(1, PIECES)
            def _(p):
                for h in range(2):
                    scatter_copy(
                        h, p, made, land, scatter_send, scatter_recv, row, core
                    ).wait_send()

    @pl.when(col >= 2)
    def _():
        load_others.start()
        load_value.wait()

    @pl.when((x_hi == 0) & (piece > 0) & ~late)
    def _():
        greet(row, core)
        pl.semaphore_wait(pltpu.get_barrier_semaphore(), 1)
        for h in range(2):
            scatter_copy(
                h, piece, made, land, scatter_send, scatter_recv, row, core
            ).wait_recv()
        piece_out[...] = land[...]

    load_others.wait()


def solve_early(rhs, panel, inverse, after):
    half, block = rhs.shape[0], inverse.shape[1]
    length = half // PIECES
    return pl.pallas_call(
        early_kernel,
        out_shape=(
            pltpu.VMEM(rhs.shape, rhs.dtype),
            pltpu.VMEM((length, block), jnp.bfloat16),
            pltpu.VMEM((half, block), jnp.bfloat16),
        ),
        in_specs=[HBM] * 3 + [ANY],
        out_specs=(VMEM,) * 3,
        scratch_shapes=[
            pltpu.VMEM((block, block), jnp.bfloat16),
            pltpu.VMEM((block, block), jnp.bfloat16),
            pltpu.VMEM((half, block), jnp.bfloat16),
            pltpu.VMEM((length, block), jnp.bfloat16),
            DMA((4,)), DMA((2, PIECES)), DMA((2,)), DMA, DMA,
        ],
        compiler_params=pltpu.CompilerParams(
            collective_id=0, has_side_effects=True, vmem_limit_bytes=20 << 20
        ),
        cost_estimate=BUSY,
        name="early",
    )(rhs, panel, inverse, after)


def late_kernel(
    inverse, held, piece_in, before, first, piece_out,
    inv, made, land, load_sem, scatter_send, scatter_recv,
):
    row, col, core, x_hi, _, _ = place()
    piece = col // 4
    late = (row == 1) & (core == 1) & (x_hi == 0)

    @pl.when(~late)
    def _():
        piece_out[...] = piece_in[...]

    @pl.when(late & (piece == 0))
    def _():
        load_inv = pltpu.make_async_copy(inverse.at[1], inv, load_sem)
        load_inv.start()

        @pl.loop(1, PIECES)
        def _(p):
            greet(row, p * 4 + core)

        load_inv.wait()
        solve(held, before, first, inv, made)
        pl.semaphore_wait(pltpu.get_barrier_semaphore(), PIECES - 1)

        @pl.loop(1, PIECES)
        def _(p):
            for h in range(2):
                scatter_copy(h, p, made, land, scatter_send, scatter_recv, row, core).start()

        keep_own(made, piece_out)

        @pl.loop(1, PIECES)
        def _(p):
            for h in range(2):
                scatter_copy(h, p, made, land, scatter_send, scatter_recv, row, core).wait_send()

    @pl.when(late & (piece > 0))
    def _():
        greet(row, core)
        pl.semaphore_wait(pltpu.get_barrier_semaphore(), 1)
        for h in range(2):
            scatter_copy(h, piece, made, land, scatter_send, scatter_recv, row, core).wait_recv()
        piece_out[...] = land[...]


def solve_late(inverse, held, piece, before, first):
    half, block = before.shape
    return pl.pallas_call(
        late_kernel,
        out_shape=pltpu.VMEM(piece.shape, piece.dtype),
        in_specs=[HBM] + [VMEM] * 4,
        out_specs=VMEM,
        scratch_shapes=[
            pltpu.VMEM((block, block), jnp.bfloat16),
            pltpu.VMEM((half, block), jnp.bfloat16),
            pltpu.VMEM(piece.shape, jnp.bfloat16),
            DMA, DMA((2, PIECES)), DMA((2,)),
        ],
        compiler_params=pltpu.CompilerParams(
            collective_id=1, has_side_effects=True, vmem_limit_bytes=20 << 20
        ),
        cost_estimate=BUSY,
        name="late",
    )(inverse, held, piece, before, first)


def gather_kernel(
    own_piece, taken, full, rest,
    mine, cross, x_send, x_recv, send_sem, recv_sem, core_send, core_recv,
):
    row, _, core, x_hi, z, y = place()
    half = cross.shape[0]
    length = own_piece.shape[0] // 2
    has_cross = core == row
    steps = range(1, SIDE)

    @pl.when(x_hi == 0)
    def _():
        for h in range(2):
            here = slice(h * length, (h + 1) * length)
            mine[core, piece_rows(h, z, y, half), :] = own_piece[here, :]

            @pl.when(has_cross)
            def _():
                cross[piece_rows(h, z, y, half), :] = taken[here, :]

    side = at(z, y, 1 - x_hi, core)
    greet(1 - row, side)
    greet(row, at(z, y, x_hi, 1 - core))
    for d in steps:
        greet(row, at(z, lax.rem(y + d, SIDE), x_hi, core))
        greet(row, at(lax.rem(z + d, SIDE), y, x_hi, core))
    pl.semaphore_wait(pltpu.get_barrier_semaphore(), 8)

    def x_copy(which, h):
        here = pl.ds(h * length, length)
        to = piece_rows(h, z, y, half)
        return remote(
            (own_piece if which else taken).at[here],
            cross.at[to] if which else mine.at[core, to],
            x_send.at[which, h], x_recv.at[which, h], 1 - row, side,
        )

    @pl.when(x_hi == 0)
    def _():
        for h in range(2):
            x_copy(0, h).start()

        @pl.when(~has_cross)
        def _():
            for h in range(2):
                x_copy(1, h).start()

    @pl.when(x_hi == 1)
    def _():
        for h in range(2):
            x_copy(0, h).wait_recv()

        @pl.when(has_cross)
        def _():
            for h in range(2):
                x_copy(1, h).wait_recv()

    def copy(which, h, stage, d, back=False):
        buffer = cross if which else mine.at[core]
        along_y = (h == 0) == (stage == 0)
        turn = SIDE - d if back else d
        y_, z_ = (lax.rem(y + turn, SIDE), z) if along_y else (y, lax.rem(z + turn, SIDE))
        from_y, from_z = (y_, z_) if back else (y, z)
        if stage == 0:
            part = piece_rows(h, from_z, from_y, half)
        else:
            group = from_z if h == 0 else from_y
            part = pl.ds(
                pl.multiple_of(h * (half // 2) + group * (half // 8), half // 8), half // 8
            )
        y_to, z_to = (lax.rem(y + d, SIDE), z) if along_y else (y, lax.rem(z + d, SIDE))
        return remote(
            buffer.at[part], buffer.at[part],
            send_sem.at[which, h, stage, d - 1], recv_sem.at[which, h, stage, d - 1],
            row, at(z_to, y_to, x_hi, core),
        )

    def start(which, stage, h):
        for d in steps:
            copy(which, h, stage, d).start()

    def arrive(which, stage, h):
        for d in steps:
            copy(which, h, stage, d, True).wait_recv()

    for h in range(2):
        start(0, 0, h)

    @pl.when(has_cross)
    def _():
        for h in range(2):
            start(1, 0, h)

    for h in range(2):
        arrive(0, 0, h)
        start(0, 1, h)

    @pl.when(has_cross)
    def _():
        for h in range(2):
            arrive(1, 0, h)
            start(1, 1, h)

    buddy = at(z, y, x_hi, 1 - core)

    def share(which, h, take=False):
        part = pl.ds(h * (half // 2), half // 2)
        buffer = cross if which else mine.at[1 - core if take else core]
        return remote(
            buffer.at[part], buffer.at[part], core_send.at[which, h], core_recv.at[which, h],
            row, buddy,
        )

    for h in range(2):
        arrive(0, 1, h)
        share(0, h).start()

    @pl.when(has_cross)
    def _():
        for h in range(2):
            arrive(1, 1, h)
            share(1, h).start()

    for h in range(2):
        share(0, h, True).wait_recv()

    @pl.when(~has_cross)
    def _():
        for h in range(2):
            share(1, h, True).wait_recv()

    full[rows(row, half), :] = mine[row]
    full[rows(1 - row, half), :] = cross[...]
    rest[...] = mine[1 - row]

    def sent(which):
        for h in range(2):
            share(which, h).wait_send()
            for stage in range(2):
                for d in steps:
                    copy(which, h, stage, d).wait_send()

    sent(0)

    @pl.when(has_cross)
    def _():
        sent(1)

    @pl.when(x_hi == 0)
    def _():
        for h in range(2):
            x_copy(0, h).wait_send()

        @pl.when(~has_cross)
        def _():
            for h in range(2):
                x_copy(1, h).wait_send()


def gather_pieces(piece, taken):
    length, block = piece.shape
    half = length * PIECES
    return pl.pallas_call(
        gather_kernel,
        out_shape=(
            pltpu.VMEM((2 * half, block), jnp.bfloat16),
            pltpu.VMEM((half, block), jnp.bfloat16),
        ),
        in_specs=[VMEM] * 2,
        out_specs=(VMEM, VMEM),
        scratch_shapes=[
            pltpu.VMEM((2, half, block), jnp.bfloat16),
            pltpu.VMEM((half, block), jnp.bfloat16),
            DMA((2, 2)), DMA((2, 2)), DMA((2, 2, 2, 3)), DMA((2, 2, 2, 3)), DMA((2, 2)), DMA((2, 2)),
        ],
        compiler_params=pltpu.CompilerParams(
            collective_id=2, has_side_effects=True, vmem_limit_bytes=12 << 20
        ),
        cost_estimate=BUSY,
        name="gather",
    )(piece, taken)


def begin_kernel(held, full, rest, *refs, count, early):
    owns, parts = refs[:count], refs[count : count + early]
    updated, solved, ahead, work, store_sem = refs[count + early :]
    row, col = lax.axis_index("row"), lax.axis_index("col")
    block = rest.shape[0]
    ready = work.shape[1]

    put_solved = pltpu.make_async_copy(full, solved, store_sem.at[0])
    put_solved.start()

    def store(j):
        part = rows(j, CHUNK)
        return pltpu.make_async_copy(work.at[:, part], updated.at[:, part], store_sem.at[1 + j])

    def step(first, i, mine, theirs, mask):
        here = rows(i, CHUNK)
        own = mine[here, :]
        if mask:
            own = jnp.where((col < 2) & (row >= col), jnp.zeros_like(own), own)
        total = lax.dot_general(
            full[rows(row, block), :], own, NT, preferred_element_type=jnp.float32
        )
        column = rows(first + i, CHUNK)
        if theirs is None:
            ahead[:, rows(first + i - ready // CHUNK, CHUNK)] = held[:, column] - total
            return
        other = theirs[here, :]
        if mask:
            other = jnp.where((col < 2) & (1 - row >= col), jnp.zeros_like(other), other)
        total += lax.dot_general(rest[...], other, NT, preferred_element_type=jnp.float32)
        work[:, column] = held[:, column] - total
        store(first + i).start()

    first = 0
    for index, mine in enumerate(owns):
        theirs = parts[index] if index < early else None
        here = mine.shape[0] // CHUNK
        top = min(here, max(0, block // CHUNK - first))
        for low, high, mask in ((0, top, True), (top, here, False)):
            if high > low:
                pl.loop(low, high)(
                    functools.partial(
                        lambda i, first, mine, theirs, mask: step(first, i, mine, theirs, mask),
                        first=first, mine=mine, theirs=theirs, mask=mask,
                    )
                )
        first += here

    put_solved.wait()

    @pl.loop(0, ready // CHUNK)
    def _(j):
        store(j).wait()


def begin(held, full, rest, owns, parts):
    half, rows_dev = held.shape
    ready = sum(part.shape[0] for part in parts)
    return pl.pallas_call(
        functools.partial(begin_kernel, count=len(owns), early=len(parts)),
        out_shape=(
            pltpu.HBM(held.shape, jnp.float32),
            pltpu.HBM(full.shape, full.dtype),
            pltpu.VMEM((half, rows_dev - ready), jnp.float32),
        ),
        in_specs=[VMEM] * (3 + len(owns) + len(parts)),
        out_specs=(HBM, HBM, VMEM),
        scratch_shapes=[
            pltpu.VMEM((half, ready), jnp.float32),
            DMA((1 + ready // CHUNK,)),
        ],
        compiler_params=pltpu.CompilerParams(vmem_limit_bytes=32 << 20),
        cost_estimate=BUSY,
        name="begin",
    )(held, full, rest, *owns, *parts)


def finish_kernel(start, offset, held, ahead, part, rest, updated, work, store_sem):
    length = part.shape[0]
    stores = []
    for j in range(length // CHUNK):
        here = pl.ds(j * CHUNK, CHUNK)
        total = lax.dot_general(
            rest[...], part[here, :], NT, preferred_element_type=jnp.float32
        )
        work[:, here] = ahead[:, pl.ds(offset + j * CHUNK, CHUNK)] - total
        stores.append(
            pltpu.make_async_copy(
                work.at[:, here], updated.at[:, pl.ds(start + j * CHUNK, CHUNK)], store_sem.at[j]
            )
        )
        stores[-1].start()
    for copy in stores:
        copy.wait()


def finish(updated, ahead, part, rest, start, offset):
    length = part.shape[0]
    return pl.pallas_call(
        functools.partial(finish_kernel, start, offset),
        out_shape=pltpu.HBM(updated.shape, updated.dtype),
        in_specs=[HBM, VMEM, VMEM, VMEM],
        out_specs=HBM,
        scratch_shapes=[
            pltpu.VMEM((ahead.shape[0], length), jnp.float32),
            DMA((length // CHUNK,)),
        ],
        input_output_aliases={0: 0},
        compiler_params=pltpu.CompilerParams(vmem_limit_bytes=12 << 20),
        cost_estimate=pl.CostEstimate(flops=10**9, bytes_accessed=10**6, transcendentals=0),
    )(updated, ahead, part, rest)


def swap(value):
    taken = lax.ppermute(value, "row", [(0, 1), (1, 0)])
    return pltpu.with_memory_space_constraint(taken, pltpu.VMEM)


def shards(panel, rhs, inverse):
    panel, rhs, inverse = (
        pltpu.with_memory_space_constraint(value, pltpu.HBM) for value in (panel, rhs, inverse)
    )
    count = len(PARTS)
    starts = [sum(PARTS[:i]) for i in range(count)]
    sent = cut(panel, PARTS)
    arrived = [swap(sent[i]) for i in range(count)]
    held, piece, before = solve_early(rhs, panel, inverse, sent[1])
    piece = solve_late(inverse, held, piece, before, arrived[0])
    col_count = lax.axis_size("col")
    pairs = [
        (row * col_count + col + core, (1 - row) * col_count + col + core)
        for row in range(2) for col in range(0, col_count, 4) for core in range(2)
    ]
    taken = lax.ppermute(piece, ("row", "col"), pairs)
    full, rest = gather_pieces(piece, taken)
    updated, solved, ahead = begin(held, full, rest, sent, arrived[:EARLY])
    for i in range(EARLY, count):
        updated = finish(updated, ahead, arrived[i], rest, starts[i], starts[i] - starts[EARLY])
    return solved, updated


def solution(mesh):
    return jax.shard_map(
        shards,
        mesh=mesh,
        in_specs=(P("col", "row"), P("row", "col"), P()),
        out_specs=(P(None, "row"), P("row", "col")),
        check_vma=False,
    )
```

time: 1040 us -> 85 us (0.08)
  waiting for transfers between devices: 863 us -> 27.1 us
  blocking collectives: 101 us -> 0 us
  Pallas kernels: 0 us -> 48.6 us
  other arithmetic: 29 us -> 0 us
  matrix products: 20 us -> 0 us
  between operations: 13.8 us -> 0.71 us
    reduce_scatter x2 -> x0, waiting for transfers between devices: 660 us -> none  [broadcast_by_parts(): own = lax.psum_scatter(padded, axis, scatter_dimension=0, tiled=True)]
    all_gather x2 -> x0, waiting for transfers between devices: 131 us -> none  [broadcast_by_parts(): lax.all_gather(own, axis, axis=0, tiled=True)[:len(lines)]]
    all_to_all x2 -> x0, blocking collectives: 101 us -> none  [from_everyone(): return lax.all_to_all(copies, axis, split_axis=0, concat_axis=0, tiled=True)]
    all_to_all x1 -> x0, waiting for transfers between devices: 72.5 us -> none  [sum_at_owner(): lax.all_to_all(tiles, axis, split_axis=0, concat_axis=0, tiled=True)]
    pallas_call x0 -> x9, Pallas kernels: none -> 48.6 us  [the longest x1 20.1 us: solve_early(): pl.pallas_call(early_kernel, out_shape=(pltpu.VMEM(rhs.shape, rhs.dtype),...]
    ppermute x0 -> x6, waiting for transfers between devices: none -> 27.1 us  [the longest x5 27.1 us: swap(): taken = lax.ppermute(value, 'row', [(0, 1), (1, 0)])]
    dot_general x4 -> x0, matrix products: 20 us -> none  [the longest x1 8.38 us: shards(): lax.dot_general(arrived, masked, contract, preferred_element_type=jnp.flo...]
    reduce_sum x3 -> x0, other arithmetic: 12 us -> none  [the longest x2 7.02 us: taken_together(): return from_everyone(value, axis).sum(axis=0)]
  transfers between devices with their start and end apart: 5 -> 6, of which waited for: 5 -> 4; matrix products, arithmetic and copies ran while one was open for 1% -> 0% of each run, Pallas kernels for 0% -> 54%
where the time goes in v3:
time: 85 us; the launch traced here: 84.8 us
  Pallas kernels  48.6 us (57%)
  waiting for transfers between devices  27.1 us (32%)
  starting transfers between devices  8.32 us (10%)
    ppermute x5, waiting for transfers between devices, swap(): taken = lax.ppermute(value, 'row', [(0, 1), (1, 0)])  27.1 us
    pallas_call x1, Pallas kernels, solve_early(): pl.pallas_call(early_kernel, out_shape=(pltpu.VMEM(rhs.shape, rhs.dtype),...  20.1 us
    pallas_call x1, Pallas kernels, gather_pieces(): pl.pallas_call(gather_kernel, out_shape=(pltpu.VMEM((2 * half, block), jn...  16.3 us
    ppermute x5, starting transfers between devices, swap(): taken = lax.ppermute(value, 'row', [(0, 1), (1, 0)])  5.12 us
    pallas_call x1, Pallas kernels, begin(): pl.pallas_call(functools.partial(begin_kernel, count=len(owns), early=len...  4.79 us
    pallas_call x3, Pallas kernels, finish(): pl.pallas_call(functools.partial(finish_kernel, start, offset), out_shape...  4.34 us
    ppermute x1, starting transfers between devices, shards(): taken = lax.ppermute(piece, ('row', 'col'), pairs)  3.2 us
  transfers between devices with their start and end apart: 6, of which 4 were waited for; matrix products, arithmetic and copies ran while one was open for 0% of the time, Pallas kernels for 54%

profile of v3, /device:TPU:1, one launch (start us, length us, event | category | flops | bytes accessed | tf_op | source)
XLA Modules:
  0.0 84.8 jit_solution(7999086417629364386)
XLA Ops:
  0.6 1.1 %cut_first.1.after.refs_0_ = bf16[512,512]{1,0:T(8,128)(2,1)S(1)} custom-call(bf16[3072,512]{1,0:T(8,128)(2,1)} %panel.5), custom_call_target="tpu_custom_call" | custom-call | tf_op jit(solution)/shard_map/cut_first/pallas_call | solution.py:77
  1.7 2.1 %collective-permute-start = (bf16[512,512]{1,0:T(8,128)(2,1)S(1)}, bf16[512,512]{1,0:T(8,128)(2,1)S(1)}, u32[]{:S(2)}, u32[]{:S(2)}) collective-permute-start(bf16[512,512]{1,0:T(8,128)(2,1)S(1)} %cut_first.1.after.refs_0_), channel_id=1, source_target_pairs={{0,64},{64,0},{1,65},{65,1},{2,66},{66,2},{3,67},{67,3},{4,68},{68... | collective-permute-start | bytes 1572872 | tf_op jit(solution)/shard_map/ppermute | solution.py:622
  3.8 1.7 %cut_others.1 = (bf16[768,512]{1,0:T(8,128)(2,1)S(1)}, bf16[768,512]{1,0:T(8,128)(2,1)S(1)}, bf16[768,512]{1,0:T(8,128)(2,1)S(1)}, bf16[256,512]{1,0:T(8,128)(2,1)S(1)}) custom-call(bf16[3072,512]{1,0:T(8,128)(2,1)} %panel.5, bf16[512,512]{1,0:T(8,128)(2,1)S(1)} %cut_first.1.after.refs_0_), custom_call_target="tpu_custom_call" | custom-call | tf_op jit(solution)/shard_map/cut_others/pallas_call | solution.py:86
  5.5 20.1 %early.1 = (f32[512,3072]{1,0:T(8,128)S(1)}, bf16[32,512]{1,0:T(8,128)(2,1)S(1)}, bf16[512,512]{1,0:T(8,128)(2,1)S(1)}) custom-call(f32[512,3072]{1,0:T(8,128)} %rhs.1, bf16[3072,512]{1,0:T(8,128)(2,1)} %panel.5, bf16[2,512,512]{2,1,0:T(8,128)(2,1)} %inverse.3, bf16[768,512]{1,0:T(8,128)(2,1)S(1)} %get-tuple-element.14.after.refs_1_), custom_call_target="tpu_custom_call" | custom-call | flops 10000000000 | bytes 1000000 | tf_op jit(solution)/shard_map/early/pallas_call | solution.py:234
  25.6 0.0 collective-permute-done.first.refs_5_
  25.6 0.4 late.1.own_piece
  26.0 3.2 %collective-permute-start.1 = (bf16[32,512]{1,0:T(8,128)(2,1)S(1)}, bf16[32,512]{1,0:T(8,128)(2,1)S(1)}, u32[]{:S(2)}, u32[]{:S(2)}) collective-permute-start(bf16[32,512]{1,0:T(8,128)(2,1)S(1)} %late.1.own_piece), channel_id=1, source_target_pairs={{0,64},{1,65},{4,68},{5,69},{8,72},{9,73},{12,76},{13,77},{16,80},... | collective-permute-start | bytes 98312 | tf_op jit(solution)/shard_map/ppermute | solution.py:641
  29.2 0.3 collective-permute-start.2
  29.5 1.3 %collective-permute-start.3 = (bf16[768,512]{1,0:T(8,128)(2,1)S(1)}, bf16[768,512]{1,0:T(8,128)(2,1)S(1)}, u32[]{:S(2)}, u32[]{:S(2)}) collective-permute-start(bf16[768,512]{1,0:T(8,128)(2,1)S(1)} %get-tuple-element.20.refs_2_), channel_id=1, source_target_pairs={{0,64},{64,0},{1,65},{65,1},{2,66},{66,2},{3,67},{67,3},{4,68},{68... | collective-permute-start | bytes 2359304 | tf_op jit(solution)/shard_map/ppermute | solution.py:622
  30.8 0.2 collective-permute-start.4
  30.9 1.3 %collective-permute-start.5 = (bf16[256,512]{1,0:T(8,128)(2,1)S(1)}, bf16[256,512]{1,0:T(8,128)(2,1)S(1)}, u32[]{:S(2)}, u32[]{:S(2)}) collective-permute-start(bf16[256,512]{1,0:T(8,128)(2,1)S(1)} %get-tuple-element.22.refs_4_), channel_id=1, source_target_pairs={{0,64},{64,0},{1,65},{65,1},{2,66},{66,2},{3,67},{67,3},{4,68},{68... | collective-permute-start | bytes 786440 | tf_op jit(solution)/shard_map/ppermute | solution.py:622
  32.2 0.0 collective-permute-done.1.taken
  32.2 16.3 %gather.1 = (bf16[1024,512]{1,0:T(8,128)(2,1)S(1)}, bf16[512,512]{1,0:T(8,128)(2,1)S(1)}) custom-call(bf16[32,512]{1,0:T(8,128)(2,1)S(1)} %late.1.own_piece, bf16[32,512]{1,0:T(8,128)(2,1)S(1)} %collective-permute-done.1.taken), custom_call_target="tpu_custom_call" | custom-call | flops 10000000000 | bytes 1000000 | tf_op jit(solution)/shard_map/gather/pallas_call | solution.py:487
  48.5 0.3 collective-permute-done.2.refs_6_
  48.9 4.8 %begin.1 = (f32[512,3072]{1,0:T(8,128)}, bf16[1024,512]{1,0:T(8,128)(2,1)}, f32[512,1792]{1,0:T(8,128)S(1)}) custom-call(f32[512,3072]{1,0:T(8,128)S(1)} %get-tuple-element.15.held, bf16[1024,512]{1,0:T(8,128)(2,1)S(1)} %get-tuple-element.18.full, bf16[512,512]{1,0:T(8,128)(2,1)S(1)} %get-tuple-element.19.rest, bf16[512,512]{1,0:T(8,128)(2,1)S(1)} %cut_first.1.after.refs_0_, ...), custom_call_target="tpu_custom_call" | custom-call | flops 10000000000 | bytes 1000000 | tf_op jit(solution)/shard_map/begin/pallas_call | solution.py:566
  53.7 12.1 %collective-permute-done.3.part = bf16[768,512]{1,0:T(8,128)(2,1)S(1)} collective-permute-done((bf16[768,512]{1,0:T(8,128)(2,1)S(1)}, bf16[768,512]{1,0:T(8,128)(2,1)S(1)}, u32[]{:S(2)}, u32[]{:S(2)}) %collective-permute-start.3) | collective-permute-done | bytes 786464 | tf_op jit(solution)/shard_map/ppermute | solution.py:622
  65.7 1.6 %shard_map.50.held = f32[512,3072]{1,0:T(8,128)} custom-call(f32[512,3072]{1,0:T(8,128)} %get-tuple-element.24.held, f32[512,1792]{1,0:T(8,128)S(1)} %get-tuple-element.25.ahead, bf16[768,512]{1,0:T(8,128)(2,1)S(1)} %collective-permute-done.3.part, bf16[512,512]{1,0:T(8,128)(2,1)S(1)} %get-tuple-element.19.rest), custom_call_target="tpu_custom_call", output_to_operand_aliasing={{}: (0, {})} | custom-call | flops 1000000000 | bytes 1000000 | tf_op jit(solution)/shard_map/pallas_call | solution.py:606
  67.3 13.5 %collective-permute-done.4.part = bf16[768,512]{1,0:T(8,128)(2,1)S(1)} collective-permute-done((bf16[768,512]{1,0:T(8,128)(2,1)S(1)}, bf16[768,512]{1,0:T(8,128)(2,1)S(1)}, u32[]{:S(2)}, u32[]{:S(2)}) %collective-permute-start.4) | collective-permute-done | bytes 786464 | tf_op jit(solution)/shard_map/ppermute | solution.py:622
  80.9 1.6 %shard_map.51.held = f32[512,3072]{1,0:T(8,128)} custom-call(f32[512,3072]{1,0:T(8,128)} %shard_map.50.held, f32[512,1792]{1,0:T(8,128)S(1)} %get-tuple-element.25.ahead, bf16[768,512]{1,0:T(8,128)(2,1)S(1)} %collective-permute-done.4.part, bf16[512,512]{1,0:T(8,128)(2,1)S(1)} %get-tuple-element.19.rest), custom_call_target="tpu_custom_call", output_to_operand_aliasing={{}: (0, {})} | custom-call | flops 1000000000 | bytes 1000000 | tf_op jit(solution)/shard_map/pallas_call | solution.py:606
  82.5 1.2 %collective-permute-done.5.part = bf16[256,512]{1,0:T(8,128)(2,1)S(1)} collective-permute-done((bf16[256,512]{1,0:T(8,128)(2,1)S(1)}, bf16[256,512]{1,0:T(8,128)(2,1)S(1)}, u32[]{:S(2)}, u32[]{:S(2)}) %collective-permute-start.5) | collective-permute-done | bytes 262176 | tf_op jit(solution)/shard_map/ppermute | solution.py:622
  83.7 1.1 %shard_map.52 = f32[512,3072]{1,0:T(8,128)} custom-call(f32[512,3072]{1,0:T(8,128)} %shard_map.51.held, f32[512,1792]{1,0:T(8,128)S(1)} %get-tuple-element.25.ahead, bf16[256,512]{1,0:T(8,128)(2,1)S(1)} %collective-permute-done.5.part, bf16[512,512]{1,0:T(8,128)(2,1)S(1)} %get-tuple-element.19.rest), custom_call_target="tpu_custom_call", output_to_operand_aliasing={{}: (0, {})} | custom-call | flops 1000000000 | bytes 1000000 | tf_op jit(solution)/shard_map/pallas_call | solution.py:606
Async XLA Ops:
  1.7 23.9 %collective-permute-start = (bf16[512,512]{1,0:T(8,128)(2,1)S(1)}, bf16[512,512]{1,0:T(8,128)(2,1)S(1)}, u32[]{:S(2)}, u32[]{:S(2)}) collective-permute-start(bf16[512,512]{1,0:T(8,128)(2,1)S(1)} %cut_first.1.after.refs_0_), channel_id=1, source_target_pairs={{0,64},{64,0},{1,65},{65,1},{2,66},{66,2},{3,67},{67,3},{4,68},{68... | collective-permute-start | bytes 1572872 | tf_op jit(solution)/shard_map/ppermute | solution.py:622
  26.0 6.2 %collective-permute-start.1 = (bf16[32,512]{1,0:T(8,128)(2,1)S(1)}, bf16[32,512]{1,0:T(8,128)(2,1)S(1)}, u32[]{:S(2)}, u32[]{:S(2)}) collective-permute-start(bf16[32,512]{1,0:T(8,128)(2,1)S(1)} %late.1.own_piece), channel_id=1, source_target_pairs={{0,64},{1,65},{4,68},{5,69},{8,72},{9,73},{12,76},{13,77},{16,80},... | collective-permute-start | bytes 98312 | tf_op jit(solution)/shard_map/ppermute | solution.py:641
  29.2 19.6 %collective-permute-start.2 = (bf16[768,512]{1,0:T(8,128)(2,1)S(1)}, bf16[768,512]{1,0:T(8,128)(2,1)S(1)}, u32[]{:S(2)}, u32[]{:S(2)}) collective-permute-start(bf16[768,512]{1,0:T(8,128)(2,1)S(1)} %get-tuple-element.14.after.refs_1_), channel_id=1, source_target_pairs={{0,64},{64,0},{1,65},{65,1},{2,66},{66,2},{3,67},{67,3},{4,68},{68... | collective-permute-start | bytes 2359304 | tf_op jit(solution)/shard_map/ppermute | solution.py:622
  29.5 36.2 %collective-permute-start.3 = (bf16[768,512]{1,0:T(8,128)(2,1)S(1)}, bf16[768,512]{1,0:T(8,128)(2,1)S(1)}, u32[]{:S(2)}, u32[]{:S(2)}) collective-permute-start(bf16[768,512]{1,0:T(8,128)(2,1)S(1)} %get-tuple-element.20.refs_2_), channel_id=1, source_target_pairs={{0,64},{64,0},{1,65},{65,1},{2,66},{66,2},{3,67},{67,3},{4,68},{68... | collective-permute-start | bytes 2359304 | tf_op jit(solution)/shard_map/ppermute | solution.py:622
  30.8 50.1 %collective-permute-start.4 = (bf16[768,512]{1,0:T(8,128)(2,1)S(1)}, bf16[768,512]{1,0:T(8,128)(2,1)S(1)}, u32[]{:S(2)}, u32[]{:S(2)}) collective-permute-start(bf16[768,512]{1,0:T(8,128)(2,1)S(1)} %get-tuple-element.21.refs_3_), channel_id=1, source_target_pairs={{0,64},{64,0},{1,65},{65,1},{2,66},{66,2},{3,67},{67,3},{4,68},{68... | collective-permute-start | bytes 2359304 | tf_op jit(solution)/shard_map/ppermute | solution.py:622
  30.9 52.7 %collective-permute-start.5 = (bf16[256,512]{1,0:T(8,128)(2,1)S(1)}, bf16[256,512]{1,0:T(8,128)(2,1)S(1)}, u32[]{:S(2)}, u32[]{:S(2)}) collective-permute-start(bf16[256,512]{1,0:T(8,128)(2,1)S(1)} %get-tuple-element.22.refs_4_), channel_id=1, source_target_pairs={{0,64},{64,0},{1,65},{65,1},{2,66},{66,2},{3,67},{67,3},{4,68},{68... | collective-permute-start | bytes 786440 | tf_op jit(solution)/shard_map/ppermute | solution.py:622

commit v4 on v3

v4 whole, which is shorter than its diff:
```python
import functools

import jax
import jax.numpy as jnp
from jax import lax
from jax.experimental import pallas as pl
from jax.experimental.pallas import tpu as pltpu
from jax.sharding import PartitionSpec as P


MESH = pl.DeviceIdType.MESH
NT = (((1,), (1,)), ((), ()))
SIDE = 4
PIECES = SIDE * SIDE
PARTS = (512, 768, 768, 896, 128)
EARLY = 2
DMA = pltpu.SemaphoreType.DMA
HBM = pl.BlockSpec(memory_space=pltpu.HBM)
VMEM = pl.BlockSpec(memory_space=pltpu.VMEM)
ANY = pl.BlockSpec(memory_space=pl.ANY)
BUSY = pl.CostEstimate(flops=10**10, bytes_accessed=10**6, transcendentals=0)


def place():
    row = lax.axis_index("row")
    col = lax.axis_index("col")
    piece = col // 4
    return row, col, lax.rem(col, 2), lax.rem(col // 2, 2), piece // SIDE, lax.rem(piece, SIDE)


def at(z, y, x, core):
    return ((z * SIDE + y) * 2 + x) * 2 + core


def remote(src, dst, send, recv, row, col):
    return pltpu.make_async_remote_copy(
        src_ref=src, dst_ref=dst, send_sem=send, recv_sem=recv,
        device_id=(row, col), device_id_type=MESH,
    )


def greet(row, col):
    pl.semaphore_signal(
        pltpu.get_barrier_semaphore(), inc=1, device_id=(row, col), device_id_type=MESH
    )


def rows(i, length):
    return pl.ds(pl.multiple_of(i * length, length), length)


def cut_kernel(panel, after, *refs):
    *parts, sem = refs
    start = panel.shape[0] - sum(part.shape[0] for part in parts)
    copies = []
    for i, part in enumerate(parts):
        copies.append(
            pltpu.make_async_copy(panel.at[pl.ds(start, part.shape[0])], part, sem.at[i])
        )
        start += part.shape[0]
    for copy in copies:
        copy.start()
    for copy in copies:
        copy.wait()


def lead_kernel(panel, own, got, load_sem, send_sem, recv_sem):
    row, col, core, _, _, _ = place()
    load = pltpu.make_async_copy(panel.at[pl.ds(0, own.shape[0])], own, load_sem)
    load.start()

    @pl.when(core == 1)
    def _():
        copy = remote(own, got, send_sem, recv_sem, 1 - row, col)
        greet(1 - row, col)
        pl.semaphore_wait(pltpu.get_barrier_semaphore(), 1)
        load.wait()
        copy.start()
        copy.wait()

    @pl.when(core == 0)
    def _():
        load.wait()


def lead(panel, length):
    part = pltpu.VMEM((length, panel.shape[1]), panel.dtype)
    return pl.pallas_call(
        lead_kernel,
        out_shape=(part, part),
        in_specs=[HBM],
        out_specs=(VMEM, VMEM),
        scratch_shapes=[DMA, DMA, DMA],
        compiler_params=pltpu.CompilerParams(
            collective_id=1, has_side_effects=True, vmem_limit_bytes=8 << 20
        ),
        name="lead",
    )(panel)


def cut(panel, lengths, first):
    width = panel.shape[1]
    return pl.pallas_call(
        cut_kernel,
        out_shape=tuple(pltpu.VMEM((length, width), panel.dtype) for length in lengths),
        in_specs=[HBM, ANY],
        out_specs=(VMEM,) * len(lengths),
        scratch_shapes=[DMA((len(lengths),))],
        compiler_params=pltpu.CompilerParams(vmem_limit_bytes=8 << 20),
        name="cut",
    )(panel, first)


def solve(value, before, below, inv, made):
    tall = made.shape[0] // 4

    @pl.loop(0, 4)
    def _(i):
        part = rows(i, tall)
        rest = value[part, : made.shape[1]]
        if below is not None:
            rest = rest - lax.dot_general(
                before[part, :], below[...], NT, preferred_element_type=jnp.float32
            )
        high = rest.astype(jnp.bfloat16)
        rest = rest - high.astype(jnp.float32)
        middle = rest.astype(jnp.bfloat16)
        low = (rest - middle.astype(jnp.float32)).astype(jnp.bfloat16)
        total = lax.dot_general(low, inv[...], NT, preferred_element_type=jnp.float32)
        total += lax.dot_general(middle, inv[...], NT, preferred_element_type=jnp.float32)
        total += lax.dot_general(high, inv[...], NT, preferred_element_type=jnp.float32)
        made[part, :] = total.astype(jnp.bfloat16)


def piece_rows(h, z, y, half):
    length = half // (2 * PIECES)
    index = z * SIDE + y if h == 0 else y * SIDE + z
    return pl.ds(pl.multiple_of(h * (half // 2) + index * length, length), length)


def scatter_copy(h, p, made, land, send, recv, row, core):
    source = made.at[piece_rows(h, p // SIDE, lax.rem(p, SIDE), made.shape[0])]
    to_row = row if h == 0 else 1 - row
    return remote(source, land, send.at[h, p], recv, to_row, p * 4 + 2 * h + core)


def solve_kernel(
    rhs, inverse, own, got, after, held, piece_out,
    inv, made, before, land, load_sem, scatter_send, scatter_recv, before_send, before_recv,
):
    row, col, core, x_hi, _, _ = place()
    piece = col // 4
    block = inv.shape[0]
    load_value = pltpu.make_async_copy(
        rhs.at[:, pl.ds(0, block)], held.at[:, pl.ds(0, block)], load_sem.at[0]
    )
    others = pl.ds(block, rhs.shape[1] - block)
    load_others = pltpu.make_async_copy(rhs.at[:, others], held.at[:, others], load_sem.at[1])
    load_value.start()
    before_copy = remote(made, before, before_send, before_recv, row, 1)

    @pl.when(col < 2)
    def _():
        load_inv = pltpu.make_async_copy(inverse.at[core], inv, load_sem.at[2])
        load_inv.start()
        load_others.start()
        greet(row, 1 - core)

        @pl.loop(1, PIECES)
        def _(p):
            greet(row, p * 4 + core)

        @pl.loop(0, PIECES)
        def _(p):
            greet(1 - row, p * 4 + 2 + core)

        load_value.wait()
        load_inv.wait()

        @pl.when(col == 0)
        def _():
            solve(held, None, None, inv, made)

        pl.semaphore_wait(pltpu.get_barrier_semaphore(), 2 * PIECES)

        @pl.when(col == 0)
        def _():
            before_copy.start()

        @pl.when(col == 1)
        def _():
            before_copy.wait_recv()

            @pl.when(row == 0)
            def _():
                solve(held, before, own, inv, made)

            @pl.when(row == 1)
            def _():
                solve(held, before, got, inv, made)

        def scattered(act):
            @pl.loop(1, PIECES)
            def _(p):
                act(scatter_copy(0, p, made, land, scatter_send, scatter_recv, row, core))

            @pl.loop(0, PIECES)
            def _(p):
                act(scatter_copy(1, p, made, land, scatter_send, scatter_recv, row, core))

        scattered(lambda copy: copy.start())
        piece_out[...] = made[piece_rows(0, 0, 0, made.shape[0]), :]

        @pl.when(col == 0)
        def _():
            before_copy.wait_send()

        scattered(lambda copy: copy.wait_send())

    @pl.when(col >= 2)
    def _():
        load_others.start()
        load_value.wait()
        source_row = jnp.where(x_hi == 0, row, 1 - row)
        greet(source_row, core)
        pl.semaphore_wait(pltpu.get_barrier_semaphore(), 1)
        scatter_copy(0, piece, made, land, scatter_send, scatter_recv, row, core).wait_recv()
        piece_out[...] = land[...]

    load_others.wait()


def solve_pieces(rhs, inverse, own, got, after):
    half, block = rhs.shape[0], inverse.shape[1]
    length = half // (2 * PIECES)
    return pl.pallas_call(
        solve_kernel,
        out_shape=(
            pltpu.VMEM(rhs.shape, rhs.dtype),
            pltpu.VMEM((length, block), jnp.bfloat16),
        ),
        in_specs=[HBM] * 2 + [VMEM] * 2 + [ANY],
        out_specs=(VMEM, VMEM),
        scratch_shapes=[
            pltpu.VMEM((block, block), jnp.bfloat16),
            pltpu.VMEM((half, block), jnp.bfloat16),
            pltpu.VMEM((half, block), jnp.bfloat16),
            pltpu.VMEM((length, block), jnp.bfloat16),
            DMA((3,)), DMA((2, PIECES)), DMA, DMA, DMA,
        ],
        compiler_params=pltpu.CompilerParams(
            collective_id=0, has_side_effects=True, vmem_limit_bytes=20 << 20
        ),
        cost_estimate=BUSY,
        name="solve",
    )(rhs, inverse, own, got, after)


def gather_kernel(
    own_piece, taken, full, rest,
    mine, cross, x_send, x_recv, send_sem, recv_sem, core_send, core_recv,
):
    row, _, core, x_hi, z, y = place()
    half = cross.shape[0]
    has_cross = core == row
    steps = range(1, SIDE)

    for h, (kept, crossed) in enumerate(((own_piece, taken), (taken, own_piece))):
        @pl.when(x_hi == h)
        def _():
            here = piece_rows(h, z, y, half)
            mine[core, here, :] = kept[...]

            @pl.when(has_cross)
            def _():
                cross[here, :] = crossed[...]

    side = at(z, y, 1 - x_hi, core)
    greet(1 - row, side)
    greet(row, at(z, y, x_hi, 1 - core))
    for d in steps:
        greet(row, at(z, lax.rem(y + d, SIDE), x_hi, core))
        greet(row, at(lax.rem(z + d, SIDE), y, x_hi, core))
    pl.semaphore_wait(pltpu.get_barrier_semaphore(), 8)

    def x_copy(which, h, source):
        to = piece_rows(h, z, y, half)
        return remote(
            source, cross.at[to] if which else mine.at[core, to],
            x_send.at[which], x_recv.at[which], 1 - row, side,
        )

    for h, (kept, crossed) in enumerate(((own_piece, taken), (taken, own_piece))):
        @pl.when(x_hi == h)
        def _():
            x_copy(0, h, crossed).start()

            @pl.when(~has_cross)
            def _():
                x_copy(1, h, kept).start()

    for h in range(2):
        @pl.when(x_hi == 1 - h)
        def _():
            x_copy(0, h, taken).wait_recv()

            @pl.when(has_cross)
            def _():
                x_copy(1, h, taken).wait_recv()

    def copy(which, h, stage, d, back=False):
        buffer = cross if which else mine.at[core]
        along_y = (h == 0) == (stage == 0)
        turn = SIDE - d if back else d
        y_, z_ = (lax.rem(y + turn, SIDE), z) if along_y else (y, lax.rem(z + turn, SIDE))
        from_y, from_z = (y_, z_) if back else (y, z)
        if stage == 0:
            part = piece_rows(h, from_z, from_y, half)
        else:
            group = from_z if h == 0 else from_y
            part = pl.ds(
                pl.multiple_of(h * (half // 2) + group * (half // 8), half // 8), half // 8
            )
        y_to, z_to = (lax.rem(y + d, SIDE), z) if along_y else (y, lax.rem(z + d, SIDE))
        return remote(
            buffer.at[part], buffer.at[part],
            send_sem.at[which, h, stage, d - 1], recv_sem.at[which, h, stage, d - 1],
            row, at(z_to, y_to, x_hi, core),
        )

    def start(which, stage, h):
        for d in steps:
            copy(which, h, stage, d).start()

    def arrive(which, stage, h):
        for d in steps:
            copy(which, h, stage, d, True).wait_recv()

    for h in range(2):
        start(0, 0, h)

    @pl.when(has_cross)
    def _():
        for h in range(2):
            start(1, 0, h)

    for h in range(2):
        arrive(0, 0, h)
        start(0, 1, h)

    @pl.when(has_cross)
    def _():
        for h in range(2):
            arrive(1, 0, h)
            start(1, 1, h)

    buddy = at(z, y, x_hi, 1 - core)

    def share(which, h, take=False):
        part = pl.ds(h * (half // 2), half // 2)
        buffer = cross if which else mine.at[1 - core if take else core]
        return remote(
            buffer.at[part], buffer.at[part], core_send.at[which, h], core_recv.at[which, h],
            row, buddy,
        )

    for h in range(2):
        arrive(0, 1, h)
        share(0, h).start()

    @pl.when(has_cross)
    def _():
        for h in range(2):
            arrive(1, 1, h)
            share(1, h).start()

    for h in range(2):
        share(0, h, True).wait_recv()

    @pl.when(~has_cross)
    def _():
        for h in range(2):
            share(1, h, True).wait_recv()

    full[rows(row, half), :] = mine[row]
    full[rows(1 - row, half), :] = cross[...]
    rest[...] = mine[1 - row]

    def sent(which):
        for h in range(2):
            share(which, h).wait_send()
            for stage in range(2):
                for d in steps:
                    copy(which, h, stage, d).wait_send()

    sent(0)

    @pl.when(has_cross)
    def _():
        sent(1)

    x_copy(0, 0, taken).wait_send()

    @pl.when(~has_cross)
    def _():
        x_copy(1, 0, taken).wait_send()


def gather_pieces(piece, taken):
    length, block = piece.shape
    half = length * 2 * PIECES
    return pl.pallas_call(
        gather_kernel,
        out_shape=(
            pltpu.VMEM((2 * half, block), jnp.bfloat16),
            pltpu.VMEM((half, block), jnp.bfloat16),
        ),
        in_specs=[VMEM] * 2,
        out_specs=(VMEM, VMEM),
        scratch_shapes=[
            pltpu.VMEM((2, half, block), jnp.bfloat16),
            pltpu.VMEM((half, block), jnp.bfloat16),
            DMA((2,)), DMA((2,)), DMA((2, 2, 2, 3)), DMA((2, 2, 2, 3)), DMA((2, 2)), DMA((2, 2)),
        ],
        compiler_params=pltpu.CompilerParams(
            collective_id=2, has_side_effects=True, vmem_limit_bytes=12 << 20
        ),
        cost_estimate=BUSY,
        name="gather",
    )(piece, taken)


def chunk_of(length):
    return 256 if length % 256 == 0 else 128


def begin_kernel(held, full, rest, *refs, count, early):
    owns, parts, got = refs[:count], refs[count : count + early], refs[count + early]
    updated, solved, ahead, work, store_sem = refs[count + early + 1 :]
    row, col = lax.axis_index("row"), lax.axis_index("col")
    block = rest.shape[0]
    ready = work.shape[1]

    put_solved = pltpu.make_async_copy(full, solved, store_sem.at[0])
    put_solved.start()

    def store(index, start, length):
        part = pl.ds(start, length)
        return pltpu.make_async_copy(
            work.at[:, part], updated.at[:, part], store_sem.at[1 + index]
        )

    def step(i, start, mine, theirs):
        chunk = chunk_of(mine.shape[0])
        here = rows(i, chunk)
        column = pl.ds(pl.multiple_of(start + i * chunk, chunk), chunk)
        own = mine[here, :]
        if start == 0:
            own = jnp.where((col < 2) & (row >= col), jnp.zeros_like(own), own)
        total = lax.dot_general(
            full[rows(row, block), :], own, NT, preferred_element_type=jnp.float32
        )
        if theirs is None:
            ahead[:, pl.ds(pl.multiple_of(start + i * chunk - ready, chunk), chunk)] = (
                held[:, column] - total
            )
            return
        other = theirs[here, :]
        if start == 0:
            other = jnp.where(lax.rem(col, 2) == 1, got[here, :], other)
            other = jnp.where((col < 2) & (1 - row >= col), jnp.zeros_like(other), other)
        total += lax.dot_general(rest[...], other, NT, preferred_element_type=jnp.float32)
        work[:, column] = held[:, column] - total

    start = 0
    stores = []
    for index, mine in enumerate(owns):
        length = mine.shape[0]
        theirs = parts[index] if index < early else None
        pl.loop(0, length // chunk_of(length))(
            functools.partial(step, start=start, mine=mine, theirs=theirs)
        )
        if index < early:
            stores.append(store(index, start, length))
            stores[-1].start()
        start += length

    put_solved.wait()
    for copy in stores:
        copy.wait()


def begin(held, full, rest, owns, parts, got):
    half, rows_dev = held.shape
    ready = sum(part.shape[0] for part in parts)
    return pl.pallas_call(
        functools.partial(begin_kernel, count=len(owns), early=len(parts)),
        out_shape=(
            pltpu.HBM(held.shape, jnp.float32),
            pltpu.HBM(full.shape, full.dtype),
            pltpu.VMEM((half, rows_dev - ready), jnp.float32),
        ),
        in_specs=[VMEM] * (4 + len(owns) + len(parts)),
        out_specs=(HBM, HBM, VMEM),
        scratch_shapes=[
            pltpu.VMEM((half, ready), jnp.float32),
            DMA((1 + len(parts),)),
        ],
        compiler_params=pltpu.CompilerParams(vmem_limit_bytes=32 << 20),
        cost_estimate=BUSY,
        name="begin",
    )(held, full, rest, *owns, *parts, got)


def finish_kernel(start, offset, held, ahead, part, rest, updated, work, store_sem):
    length = part.shape[0]
    chunk = chunk_of(length)
    stores = []
    for j in range(length // chunk):
        here = pl.ds(j * chunk, chunk)
        total = lax.dot_general(
            rest[...], part[here, :], NT, preferred_element_type=jnp.float32
        )
        work[:, here] = ahead[:, pl.ds(offset + j * chunk, chunk)] - total
        stores.append(
            pltpu.make_async_copy(
                work.at[:, here], updated.at[:, pl.ds(start + j * chunk, chunk)], store_sem.at[j]
            )
        )
        stores[-1].start()
    for copy in stores:
        copy.wait()


def finish(updated, ahead, part, rest, start, offset):
    length = part.shape[0]
    return pl.pallas_call(
        functools.partial(finish_kernel, start, offset),
        out_shape=pltpu.HBM(updated.shape, updated.dtype),
        in_specs=[HBM, VMEM, VMEM, VMEM],
        out_specs=HBM,
        scratch_shapes=[
            pltpu.VMEM((ahead.shape[0], length), jnp.float32),
            DMA((length // chunk_of(length),)),
        ],
        input_output_aliases={0: 0},
        compiler_params=pltpu.CompilerParams(vmem_limit_bytes=12 << 20),
        cost_estimate=pl.CostEstimate(flops=10**9, bytes_accessed=10**6, transcendentals=0),
    )(updated, ahead, part, rest)


def swap(value, cores=(0, 1)):
    col_count = lax.axis_size("col")
    pairs = [
        (row * col_count + col, (1 - row) * col_count + col)
        for row in range(2) for col in range(col_count) if col % 2 in cores
    ]
    taken = lax.ppermute(value, ("row", "col"), pairs)
    return pltpu.with_memory_space_constraint(taken, pltpu.VMEM)


def shards(panel, rhs, inverse):
    panel, rhs, inverse = (
        pltpu.with_memory_space_constraint(value, pltpu.HBM) for value in (panel, rhs, inverse)
    )
    count = len(PARTS)
    starts = [sum(PARTS[:i]) for i in range(count)]
    first, got = lead(panel, PARTS[0])
    sent = [first, *cut(panel, PARTS[1:], first)]
    arrived = [swap(sent[i], (0, 1) if i else (0,)) for i in range(count)]
    held, piece = solve_pieces(rhs, inverse, first, got, sent[1])
    taken = swap(piece)
    full, rest = gather_pieces(piece, taken)
    updated, solved, ahead = begin(held, full, rest, sent, arrived[:EARLY], got)
    for i in range(EARLY, count):
        updated = finish(updated, ahead, arrived[i], rest, starts[i], starts[i] - starts[EARLY])
    return solved, updated


def solution(mesh):
    return jax.shard_map(
        shards,
        mesh=mesh,
        in_specs=(P("col", "row"), P("row", "col"), P()),
        out_specs=(P(None, "row"), P("row", "col")),
        check_vma=False,
    )
```

time: 85 us -> 86.4 us (1.016)
  Pallas kernels: 48.6 us -> 58.4 us
  starting transfers between devices: 8.32 us -> 4.08 us
  waiting for transfers between devices: 27.1 us -> 22.9 us
    pallas_call x3 -> x2, Pallas kernels: 21.5 us -> 26.3 us  [the longest x1 16.6 us: solve_pieces(): pl.pallas_call(solve_kernel, out_shape=(pltpu.VMEM(rhs.shape, rhs.dtype),...]
    ppermute x6, starting transfers between devices: 8.32 us -> 4.08 us  [swap(): taken = lax.ppermute(value, ('row', 'col'), pairs)]
    ppermute x6, waiting for transfers between devices: 27.1 us -> 22.9 us  [swap(): taken = lax.ppermute(value, ('row', 'col'), pairs)]
    pallas_call x1, Pallas kernels: 16.3 us -> 20 us  [gather_pieces(): pl.pallas_call(gather_kernel, out_shape=(pltpu.VMEM((2 * half, block), jn...]
    pallas_call x1, Pallas kernels: 4.79 us -> 5.8 us  [begin(): pl.pallas_call(functools.partial(begin_kernel, count=len(owns), early=len...]
  transfers between devices with their start and end apart: 6 -> 6, of which waited for: 4 -> 2; matrix products, arithmetic and copies ran while one was open for 0% -> 0% of each run, Pallas kernels for 54% -> 34%
where the time goes in v4:
time: 86.4 us; the launch traced here: 86.2 us
  Pallas kernels  58.4 us (68%)
  waiting for transfers between devices  22.9 us (27%)
  starting transfers between devices  4.08 us (5%)
    ppermute x6, waiting for transfers between devices, swap(): taken = lax.ppermute(value, ('row', 'col'), pairs)  22.9 us
    pallas_call x1, Pallas kernels, gather_pieces(): pl.pallas_call(gather_kernel, out_shape=(pltpu.VMEM((2 * half, block), jn...  20 us
    pallas_call x1, Pallas kernels, solve_pieces(): pl.pallas_call(solve_kernel, out_shape=(pltpu.VMEM(rhs.shape, rhs.dtype),...  16.6 us
    pallas_call x1, Pallas kernels, lead(): pl.pallas_call(lead_kernel, out_shape=(part, part), in_specs=[HBM], out_s...  9.73 us
    pallas_call x1, Pallas kernels, begin(): pl.pallas_call(functools.partial(begin_kernel, count=len(owns), early=len...  5.8 us
    pallas_call x3, Pallas kernels, finish(): pl.pallas_call(functools.partial(finish_kernel, start, offset), out_shape...  4.63 us
    ppermute x6, starting transfers between devices, swap(): taken = lax.ppermute(value, ('row', 'col'), pairs)  4.08 us
  transfers between devices with their start and end apart: 6, of which 2 were waited for; matrix products, arithmetic and copies ran while one was open for 0% of the time, Pallas kernels for 34%

profile of v4, /device:TPU:1, one launch (start us, length us, event | category | flops | bytes accessed | tf_op | source)
XLA Modules:
  0.0 86.2 jit_solution(778080895631025269)
XLA Ops:
  0.6 9.7 %lead.1 = (bf16[512,512]{1,0:T(8,128)(2,1)S(1)}, bf16[512,512]{1,0:T(8,128)(2,1)S(1)}) custom-call(bf16[3072,512]{1,0:T(8,128)(2,1)} %panel.3), custom_call_target="tpu_custom_call" | custom-call | tf_op jit(solution)/shard_map/lead/pallas_call | solution.py:88
  10.4 1.7 %cut.1 = (bf16[768,512]{1,0:T(8,128)(2,1)S(1)}, bf16[768,512]{1,0:T(8,128)(2,1)S(1)}, bf16[896,512]{1,0:T(8,128)(2,1)S(1)}, bf16[128,512]{1,0:T(8,128)(2,1)S(1)}) custom-call(bf16[3072,512]{1,0:T(8,128)(2,1)} %panel.3, bf16[512,512]{1,0:T(8,128)(2,1)S(1)} %get-tuple-element.15.after.own.refs_0_), custom_call_target="tpu_custom_call" | custom-call | tf_op jit(solution)/shard_map/cut/pallas_call | solution.py:103
  12.1 16.6 %solve.1 = (f32[512,3072]{1,0:T(8,128)S(1)}, bf16[16,512]{1,0:T(8,128)(2,1)S(1)}) custom-call(f32[512,3072]{1,0:T(8,128)} %rhs.1, bf16[2,512,512]{2,1,0:T(8,128)(2,1)} %inverse.1, bf16[512,512]{1,0:T(8,128)(2,1)S(1)} %get-tuple-element.15.after.own.refs_0_, bf16[512,512]{1,0:T(8,128)(2,1)S(1)} %get-tuple-element.16.got.refs_7_, ...), custom_call_target="tpu_custom_call" | custom-call | flops 10000000000 | bytes 1000000 | tf_op jit(solution)/shard_map/solve/pallas_call | solution.py:236
  28.7 0.4 collective-permute-start
  29.1 1.2 %collective-permute-start.2 = (bf16[768,512]{1,0:T(8,128)(2,1)S(1)}, bf16[768,512]{1,0:T(8,128)(2,1)S(1)}, u32[]{:S(2)}, u32[]{:S(2)}) collective-permute-start(bf16[768,512]{1,0:T(8,128)(2,1)S(1)} %get-tuple-element.17.after.refs_1_), channel_id=1, source_target_pairs={{0,64},{1,65},{2,66},{3,67},{4,68},{5,69},{6,70},{7,71},{8,72},{9,... | collective-permute-start | bytes 2359304 | tf_op jit(solution)/shard_map/ppermute | solution.py:558
  30.2 0.7 collective-permute-start.1
  30.9 0.4 collective-permute-start.3
  31.3 1.2 %collective-permute-start.4 = (bf16[896,512]{1,0:T(8,128)(2,1)S(1)}, bf16[896,512]{1,0:T(8,128)(2,1)S(1)}, u32[]{:S(2)}, u32[]{:S(2)}) collective-permute-start(bf16[896,512]{1,0:T(8,128)(2,1)S(1)} %get-tuple-element.23.refs_3_), channel_id=1, source_target_pairs={{0,64},{1,65},{2,66},{3,67},{4,68},{5,69},{6,70},{7,71},{8,72},{9,... | collective-permute-start | bytes 2752520 | tf_op jit(solution)/shard_map/ppermute | solution.py:558
  32.5 0.0 collective-permute-done.taken
  32.5 0.3 collective-permute-start.5
  32.8 20.0 %gather.1 = (bf16[1024,512]{1,0:T(8,128)(2,1)S(1)}, bf16[512,512]{1,0:T(8,128)(2,1)S(1)}) custom-call(bf16[16,512]{1,0:T(8,128)(2,1)S(1)} %get-tuple-element.19.own_piece, bf16[16,512]{1,0:T(8,128)(2,1)S(1)} %collective-permute-done.taken), custom_call_target="tpu_custom_call" | custom-call | flops 10000000000 | bytes 1000000 | tf_op jit(solution)/shard_map/gather/pallas_call | solution.py:412
  52.7 0.0 collective-permute-done.1.refs_5_
  52.8 0.0 collective-permute-done.2.refs_6_
  52.8 5.8 %begin.1 = (f32[512,3072]{1,0:T(8,128)}, bf16[1024,512]{1,0:T(8,128)(2,1)}, f32[512,1792]{1,0:T(8,128)S(1)}) custom-call(f32[512,3072]{1,0:T(8,128)S(1)} %get-tuple-element.18.held, bf16[1024,512]{1,0:T(8,128)(2,1)S(1)} %get-tuple-element.20.full, bf16[512,512]{1,0:T(8,128)(2,1)S(1)} %get-tuple-element.21.rest, ...), custom_call_target="tpu_custom_call" | custom-call | flops 10000000000 | bytes 1000000 | tf_op jit(solution)/shard_map/begin/pallas_call | solution.py:496
  58.6 6.9 %collective-permute-done.3.part = bf16[768,512]{1,0:T(8,128)(2,1)S(1)} collective-permute-done((bf16[768,512]{1,0:T(8,128)(2,1)S(1)}, bf16[768,512]{1,0:T(8,128)(2,1)S(1)}, u32[]{:S(2)}, u32[]{:S(2)}) %collective-permute-start.3) | collective-permute-done | bytes 786464 | tf_op jit(solution)/shard_map/ppermute | solution.py:558
  65.5 1.6 %shard_map.50.held = f32[512,3072]{1,0:T(8,128)} custom-call(f32[512,3072]{1,0:T(8,128)} %get-tuple-element.26.held, f32[512,1792]{1,0:T(8,128)S(1)} %get-tuple-element.27.ahead, bf16[768,512]{1,0:T(8,128)(2,1)S(1)} %collective-permute-done.3.part, bf16[512,512]{1,0:T(8,128)(2,1)S(1)} %get-tuple-element.21.rest), custom_call_target="tpu_custom_call", output_to_operand_aliasing={{}: (0, {})} | custom-call | flops 1000000000 | bytes 1000000 | tf_op jit(solution)/shard_map/pallas_call | solution.py:537
  67.1 16.0 %collective-permute-done.4.part = bf16[896,512]{1,0:T(8,128)(2,1)S(1)} collective-permute-done((bf16[896,512]{1,0:T(8,128)(2,1)S(1)}, bf16[896,512]{1,0:T(8,128)(2,1)S(1)}, u32[]{:S(2)}, u32[]{:S(2)}) %collective-permute-start.4) | collective-permute-done | bytes 917536 | tf_op jit(solution)/shard_map/ppermute | solution.py:558
  83.1 2.0 %shard_map.51.held = f32[512,3072]{1,0:T(8,128)} custom-call(f32[512,3072]{1,0:T(8,128)} %shard_map.50.held, f32[512,1792]{1,0:T(8,128)S(1)} %get-tuple-element.27.ahead, bf16[896,512]{1,0:T(8,128)(2,1)S(1)} %collective-permute-done.4.part, bf16[512,512]{1,0:T(8,128)(2,1)S(1)} %get-tuple-element.21.rest), custom_call_target="tpu_custom_call", output_to_operand_aliasing={{}: (0, {})} | custom-call | flops 1000000000 | bytes 1000000 | tf_op jit(solution)/shard_map/pallas_call | solution.py:537
  85.1 0.0 collective-permute-done.5.part
  85.2 1.0 %shard_map.52 = f32[512,3072]{1,0:T(8,128)} custom-call(f32[512,3072]{1,0:T(8,128)} %shard_map.51.held, f32[512,1792]{1,0:T(8,128)S(1)} %get-tuple-element.27.ahead, bf16[128,512]{1,0:T(8,128)(2,1)S(1)} %collective-permute-done.5.part, bf16[512,512]{1,0:T(8,128)(2,1)S(1)} %get-tuple-element.21.rest), custom_call_target="tpu_custom_call", output_to_operand_aliasing={{}: (0, {})} | custom-call | flops 1000000000 | bytes 1000000 | tf_op jit(solution)/shard_map/pallas_call | solution.py:537
Async XLA Ops:
  28.7 3.8 %collective-permute-start = (bf16[16,512]{1,0:T(8,128)(2,1)S(1)}, bf16[16,512]{1,0:T(8,128)(2,1)S(1)}, u32[]{:S(2)}, u32[]{:S(2)}) collective-permute-start(bf16[16,512]{1,0:T(8,128)(2,1)S(1)} %get-tuple-element.19.own_piece), channel_id=1, source_target_pairs={{0,64},{1,65},{2,66},{3,67},{4,68},{5,69},{6,70},{7,71},{8,72},{9,... | collective-permute-start | bytes 49160 | tf_op jit(solution)/shard_map/ppermute | solution.py:558
  29.1 23.7 %collective-permute-start.2 = (bf16[768,512]{1,0:T(8,128)(2,1)S(1)}, bf16[768,512]{1,0:T(8,128)(2,1)S(1)}, u32[]{:S(2)}, u32[]{:S(2)}) collective-permute-start(bf16[768,512]{1,0:T(8,128)(2,1)S(1)} %get-tuple-element.17.after.refs_1_), channel_id=1, source_target_pairs={{0,64},{1,65},{2,66},{3,67},{4,68},{5,69},{6,70},{7,71},{8,72},{9,... | collective-permute-start | bytes 2359304 | tf_op jit(solution)/shard_map/ppermute | solution.py:558
  30.2 22.5 %collective-permute-start.1 = (bf16[512,512]{1,0:T(8,128)(2,1)S(1)}, bf16[512,512]{1,0:T(8,128)(2,1)S(1)}, u32[]{:S(2)}, u32[]{:S(2)}) collective-permute-start(bf16[512,512]{1,0:T(8,128)(2,1)S(1)} %get-tuple-element.15.after.own.refs_0_), channel_id=1, source_target_pairs={{0,64},{2,66},{4,68},{6,70},{8,72},{10,74},{12,76},{14,78},{16,80}... | collective-permute-start | bytes 1572872 | tf_op jit(solution)/shard_map/ppermute | solution.py:558
  30.9 34.6 %collective-permute-start.3 = (bf16[768,512]{1,0:T(8,128)(2,1)S(1)}, bf16[768,512]{1,0:T(8,128)(2,1)S(1)}, u32[]{:S(2)}, u32[]{:S(2)}) collective-permute-start(bf16[768,512]{1,0:T(8,128)(2,1)S(1)} %get-tuple-element.22.refs_2_), channel_id=1, source_target_pairs={{0,64},{1,65},{2,66},{3,67},{4,68},{5,69},{6,70},{7,71},{8,72},{9,... | collective-permute-start | bytes 2359304 | tf_op jit(solution)/shard_map/ppermute | solution.py:558
  31.3 51.8 %collective-permute-start.4 = (bf16[896,512]{1,0:T(8,128)(2,1)S(1)}, bf16[896,512]{1,0:T(8,128)(2,1)S(1)}, u32[]{:S(2)}, u32[]{:S(2)}) collective-permute-start(bf16[896,512]{1,0:T(8,128)(2,1)S(1)} %get-tuple-element.23.refs_3_), channel_id=1, source_target_pairs={{0,64},{1,65},{2,66},{3,67},{4,68},{5,69},{6,70},{7,71},{8,72},{9,... | collective-permute-start | bytes 2752520 | tf_op jit(solution)/shard_map/ppermute | solution.py:558
  32.5 52.7 %collective-permute-start.5 = (bf16[128,512]{1,0:T(8,128)(2,1)S(1)}, bf16[128,512]{1,0:T(8,128)(2,1)S(1)}, u32[]{:S(2)}, u32[]{:S(2)}) collective-permute-start(bf16[128,512]{1,0:T(8,128)(2,1)S(1)} %get-tuple-element.24.refs_4_), channel_id=1, source_target_pairs={{0,64},{1,65},{2,66},{3,67},{4,68},{5,69},{6,70},{7,71},{8,72},{9,... | collective-permute-start | bytes 393224 | tf_op jit(solution)/shard_map/ppermute | solution.py:558

commit v5 on v4

--- a/solution.py
+++ b/solution.py
@@ -12,7 +12,7 @@
 NT = (((1,), (1,)), ((), ()))
 SIDE = 4
 PIECES = SIDE * SIDE
-PARTS = (512, 768, 768, 896, 128)
+PARTS = (512, 768, 768, 640, 256, 128)
 EARLY = 2
 DMA = pltpu.SemaphoreType.DMA
 HBM = pl.BlockSpec(memory_space=pltpu.HBM)
@@ -49,87 +49,66 @@
     return pl.ds(pl.multiple_of(i * length, length), length)
 
 
-def cut_kernel(panel, after, *refs):
-    *parts, sem = refs
-    start = panel.shape[0] - sum(part.shape[0] for part in parts)
-    copies = []
+def lead_kernel(panel, *refs):
+    *parts, got, load_sem, send_sem, recv_sem = refs
+    row, col, core, _, _, _ = place()
+    loads = []
+    start = 0
     for i, part in enumerate(parts):
-        copies.append(
-            pltpu.make_async_copy(panel.at[pl.ds(start, part.shape[0])], part, sem.at[i])
+        loads.append(
+            pltpu.make_async_copy(panel.at[pl.ds(start, part.shape[0])], part, load_sem.at[i])
         )
         start += part.shape[0]
-    for copy in copies:
-        copy.start()
-    for copy in copies:
-        copy.wait()
-
-
-def lead_kernel(panel, own, got, load_sem, send_sem, recv_sem):
-    row, col, core, _, _, _ = place()
-    load = pltpu.make_async_copy(panel.at[pl.ds(0, own.shape[0])], own, load_sem)
-    load.start()
+    for load in loads:
+        load.start()
 
     @pl.when(core == 1)
     def _():
-        copy = remote(own, got, send_sem, recv_sem, 1 - row, col)
+        copy = remote(parts[0], got, send_sem, recv_sem, 1 - row, col)
         greet(1 - row, col)
         pl.semaphore_wait(pltpu.get_barrier_semaphore(), 1)
-        load.wait()
+        loads[0].wait()
         copy.start()
         copy.wait()
 
     @pl.when(core == 0)
     def _():
+        loads[0].wait()
+
+    for load in loads[1:]:
         load.wait()
 
 
-def lead(panel, length):
-    part = pltpu.VMEM((length, panel.shape[1]), panel.dtype)
-    return pl.pallas_call(
+def lead(panel, lengths):
+    parts = [pltpu.VMEM((length, panel.shape[1]), panel.dtype) for length in lengths]
+    *parts, got = pl.pallas_call(
         lead_kernel,
-        out_shape=(part, part),
+        out_shape=(*parts, parts[0]),
         in_specs=[HBM],
-        out_specs=(VMEM, VMEM),
-        scratch_shapes=[DMA, DMA, DMA],
+        out_specs=(VMEM,) * (len(parts) + 1),
+        scratch_shapes=[DMA((len(lengths),)), DMA, DMA],
         compiler_params=pltpu.CompilerParams(
             collective_id=1, has_side_effects=True, vmem_limit_bytes=8 << 20
         ),
         name="lead",
     )(panel)
-
-
-def cut(panel, lengths, first):
-    width = panel.shape[1]
-    return pl.pallas_call(
-        cut_kernel,
-        out_shape=tuple(pltpu.VMEM((length, width), panel.dtype) for length in lengths),
-        in_specs=[HBM, ANY],
-        out_specs=(VMEM,) * len(lengths),
-        scratch_shapes=[DMA((len(lengths),))],
-        compiler_params=pltpu.CompilerParams(vmem_limit_bytes=8 << 20),
-        name="cut",
-    )(panel, first)
+    return parts, got
 
 
 def solve(value, before, below, inv, made):
-    tall = made.shape[0] // 4
-
-    @pl.loop(0, 4)
-    def _(i):
-        part = rows(i, tall)
-        rest = value[part, : made.shape[1]]
-        if below is not None:
-            rest = rest - lax.dot_general(
-                before[part, :], below[...], NT, preferred_element_type=jnp.float32
-            )
-        high = rest.astype(jnp.bfloat16)
-        rest = rest - high.astype(jnp.float32)
-        middle = rest.astype(jnp.bfloat16)
-        low = (rest - middle.astype(jnp.float32)).astype(jnp.bfloat16)
-        total = lax.dot_general(low, inv[...], NT, preferred_element_type=jnp.float32)
-        total += lax.dot_general(middle, inv[...], NT, preferred_element_type=jnp.float32)
-        total += lax.dot_general(high, inv[...], NT, preferred_element_type=jnp.float32)
-        made[part, :] = total.astype(jnp.bfloat16)
+    rest = value[:, : made.shape[1]]
+    if below is not None:
+        rest = rest - lax.dot_general(
+            before[...], below[...], NT, preferred_element_type=jnp.float32
+        )
+    high = rest.astype(jnp.bfloat16)
+    rest = rest - high.astype(jnp.float32)
+    middle = rest.astype(jnp.bfloat16)
+    low = (rest - middle.astype(jnp.float32)).astype(jnp.bfloat16)
+    total = lax.dot_general(low, inv[...], NT, preferred_element_type=jnp.float32)
+    total += lax.dot_general(middle, inv[...], NT, preferred_element_type=jnp.float32)
+    total += lax.dot_general(high, inv[...], NT, preferred_element_type=jnp.float32)
+    made[...] = total.astype(jnp.bfloat16)
 
 
 def piece_rows(h, z, y, half):
@@ -549,11 +528,11 @@
     )(updated, ahead, part, rest)
 
 
-def swap(value, cores=(0, 1)):
+def swap(value, takes):
     col_count = lax.axis_size("col")
     pairs = [
         (row * col_count + col, (1 - row) * col_count + col)
-        for row in range(2) for col in range(col_count) if col % 2 in cores
+        for row in range(2) for col in range(col_count) if takes(col)
     ]
     taken = lax.ppermute(value, ("row", "col"), pairs)
     return pltpu.with_memory_space_constraint(taken, pltpu.VMEM)
@@ -565,11 +544,10 @@
     )
     count = len(PARTS)
     starts = [sum(PARTS[:i]) for i in range(count)]
-    first, got = lead(panel, PARTS[0])
-    sent = [first, *cut(panel, PARTS[1:], first)]
-    arrived = [swap(sent[i], (0, 1) if i else (0,)) for i in range(count)]
-    held, piece = solve_pieces(rhs, inverse, first, got, sent[1])
-    taken = swap(piece)
+    sent, got = lead(panel, PARTS)
+    arrived = [swap(sent[i], lambda col: i > 0 or (col % 2 == 0 and col > 0)) for i in range(count)]
+    held, piece = solve_pieces(rhs, inverse, sent[0], got, sent[1])
+    taken = swap(piece, lambda col: True)
     full, rest = gather_pieces(piece, taken)
     updated, solved, ahead = begin(held, full, rest, sent, arrived[:EARLY], got)
     for i in range(EARLY, count):

time: 86.4 us -> 84.2 us (0.975)
  the two profiles are of different devices: /device:TPU:1 before, /device:TPU:124 now
where the time goes in v5:
time: 84.2 us; the launch traced here: 84 us
  Pallas kernels  41.8 us (50%)
  waiting for transfers between devices  32.9 us (39%)
  starting transfers between devices  8.61 us (10%)
    ppermute x7, waiting for transfers between devices, swap(): taken = lax.ppermute(value, ('row', 'col'), pairs)  32.9 us
    pallas_call x1, Pallas kernels, gather_pieces(): pl.pallas_call(gather_kernel, out_shape=(pltpu.VMEM((2 * half, block), jn...  16.6 us
    pallas_call x1, Pallas kernels, solve_pieces(): pl.pallas_call(solve_kernel, out_shape=(pltpu.VMEM(rhs.shape, rhs.dtype),...  12.4 us
    ppermute x7, starting transfers between devices, swap(): taken = lax.ppermute(value, ('row', 'col'), pairs)  8.61 us
    pallas_call x4, Pallas kernels, finish(): pl.pallas_call(functools.partial(finish_kernel, start, offset), out_shape...  5.43 us
    pallas_call x1, Pallas kernels, begin(): pl.pallas_call(functools.partial(begin_kernel, count=len(owns), early=len...  5.36 us
    pallas_call x1, Pallas kernels, lead(): pl.pallas_call(lead_kernel, out_shape=(*parts, parts[0]), in_specs=[HBM],...  1.95 us
  transfers between devices with their start and end apart: 7, of which 5 were waited for; matrix products, arithmetic and copies ran while one was open for 0% of the time, Pallas kernels for 31%

profile of v5, /device:TPU:124, one launch (start us, length us, event | category | flops | bytes accessed | tf_op | source)
XLA Modules:
  0.0 84.0 jit_solution(2784932701328674997)
XLA Ops:
  0.6 2.0 %lead.1 = (bf16[512,512]{1,0:T(8,128)(2,1)S(1)}, bf16[768,512]{1,0:T(8,128)(2,1)S(1)}, bf16[768,512]{1,0:T(8,128)(2,1)S(1)}, bf16[640,512]{1,0:T(8,128)(2,1)S(1)...) custom-call(bf16[3072,512]{1,0:T(8,128)(2,1)} %panel.1), custom_call_target="tpu_custom_call" | custom-call | tf_op jit(solution)/shard_map/lead/pallas_call | solution.py:84
  2.6 12.4 %solve.1 = (f32[512,3072]{1,0:T(8,128)S(1)}, bf16[16,512]{1,0:T(8,128)(2,1)S(1)}) custom-call(f32[512,3072]{1,0:T(8,128)} %rhs.1, bf16[2,512,512]{2,1,0:T(8,128)(2,1)} %inverse.1, bf16[512,512]{1,0:T(8,128)(2,1)S(1)} %get-tuple-element.16.own.refs_0_, bf16[512,512]{1,0:T(8,128)(2,1)S(1)} %get-tuple-element.17.got.refs_8_, ...), custom_call_target="tpu_custom_call" | custom-call | flops 10000000000 | bytes 1000000 | tf_op jit(solution)/shard_map/solve/pallas_call | solution.py:215
  15.0 2.5 %collective-permute-start = (bf16[16,512]{1,0:T(8,128)(2,1)S(1)}, bf16[16,512]{1,0:T(8,128)(2,1)S(1)}, u32[]{:S(2)}, u32[]{:S(2)}) collective-permute-start(bf16[16,512]{1,0:T(8,128)(2,1)S(1)} %get-tuple-element.20.own_piece), channel_id=1, source_target_pairs={{0,64},{1,65},{2,66},{3,67},{4,68},{5,69},{6,70},{7,71},{8,72},{9,... | collective-permute-start | bytes 49160 | tf_op jit(solution)/shard_map/ppermute | solution.py:537
  17.5 0.1 collective-permute-start.2
  17.6 3.8 %collective-permute-start.1 = (bf16[512,512]{1,0:T(8,128)(2,1)S(1)}, bf16[512,512]{1,0:T(8,128)(2,1)S(1)}, u32[]{:S(2)}, u32[]{:S(2)}) collective-permute-start(bf16[512,512]{1,0:T(8,128)(2,1)S(1)} %get-tuple-element.16.own.refs_0_), channel_id=1, source_target_pairs={{2,66},{4,68},{6,70},{8,72},{10,74},{12,76},{14,78},{16,80},{18,82... | collective-permute-start | bytes 1572872 | tf_op jit(solution)/shard_map/ppermute | solution.py:537
  21.4 0.2 collective-permute-start.3
  21.6 1.9 %collective-permute-start.4 = (bf16[640,512]{1,0:T(8,128)(2,1)S(1)}, bf16[640,512]{1,0:T(8,128)(2,1)S(1)}, u32[]{:S(2)}, u32[]{:S(2)}) collective-permute-start(bf16[640,512]{1,0:T(8,128)(2,1)S(1)} %get-tuple-element.24.refs_3_), channel_id=1, source_target_pairs={{0,64},{1,65},{2,66},{3,67},{4,68},{5,69},{6,70},{7,71},{8,72},{9,... | collective-permute-start | bytes 1966088 | tf_op jit(solution)/shard_map/ppermute | solution.py:537
  23.5 0.0 collective-permute-done.taken
  23.5 0.1 collective-permute-start.5
  23.6 16.6 %gather.1 = (bf16[1024,512]{1,0:T(8,128)(2,1)S(1)}, bf16[512,512]{1,0:T(8,128)(2,1)S(1)}) custom-call(bf16[16,512]{1,0:T(8,128)(2,1)S(1)} %get-tuple-element.20.own_piece, bf16[16,512]{1,0:T(8,128)(2,1)S(1)} %collective-permute-done.taken), custom_call_target="tpu_custom_call" | custom-call | flops 10000000000 | bytes 1000000 | tf_op jit(solution)/shard_map/gather/pallas_call | solution.py:391
  40.3 3.9 %collective-permute-done.1.refs_6_ = bf16[512,512]{1,0:T(8,128)(2,1)S(1)} collective-permute-done((bf16[512,512]{1,0:T(8,128)(2,1)S(1)}, bf16[512,512]{1,0:T(8,128)(2,1)S(1)}, u32[]{:S(2)}, u32[]{:S(2)}) %collective-permute-start.1) | collective-permute-done | bytes 524320 | tf_op jit(solution)/shard_map/ppermute | solution.py:537
  44.2 0.0 collective-permute-start.6
  44.2 0.0 collective-permute-done.2.refs_7_
  44.2 5.4 %begin.1 = (f32[512,3072]{1,0:T(8,128)}, bf16[1024,512]{1,0:T(8,128)(2,1)}, f32[512,1792]{1,0:T(8,128)S(1)}) custom-call(f32[512,3072]{1,0:T(8,128)S(1)} %get-tuple-element.19.held, bf16[1024,512]{1,0:T(8,128)(2,1)S(1)} %get-tuple-element.21.full, bf16[512,512]{1,0:T(8,128)(2,1)S(1)} %get-tuple-element.22.rest, ...), custom_call_target="tpu_custom_call" | custom-call | flops 10000000000 | bytes 1000000 | tf_op jit(solution)/shard_map/begin/pallas_call | solution.py:475
  49.5 11.5 %collective-permute-done.3.part = bf16[768,512]{1,0:T(8,128)(2,1)S(1)} collective-permute-done((bf16[768,512]{1,0:T(8,128)(2,1)S(1)}, bf16[768,512]{1,0:T(8,128)(2,1)S(1)}, u32[]{:S(2)}, u32[]{:S(2)}) %collective-permute-start.3) | collective-permute-done | bytes 786464 | tf_op jit(solution)/shard_map/ppermute | solution.py:537
  61.0 1.6 %shard_map.50.held = f32[512,3072]{1,0:T(8,128)} custom-call(f32[512,3072]{1,0:T(8,128)} %get-tuple-element.28.held, f32[512,1792]{1,0:T(8,128)S(1)} %get-tuple-element.29.ahead, bf16[768,512]{1,0:T(8,128)(2,1)S(1)} %collective-permute-done.3.part, bf16[512,512]{1,0:T(8,128)(2,1)S(1)} %get-tuple-element.22.rest), custom_call_target="tpu_custom_call", output_to_operand_aliasing={{}: (0, {})} | custom-call | flops 1000000000 | bytes 1000000 | tf_op jit(solution)/shard_map/pallas_call | solution.py:516
  62.6 12.4 %collective-permute-done.4.part = bf16[640,512]{1,0:T(8,128)(2,1)S(1)} collective-permute-done((bf16[640,512]{1,0:T(8,128)(2,1)S(1)}, bf16[640,512]{1,0:T(8,128)(2,1)S(1)}, u32[]{:S(2)}, u32[]{:S(2)}) %collective-permute-start.4) | collective-permute-done | bytes 655392 | tf_op jit(solution)/shard_map/ppermute | solution.py:537
  75.1 1.7 %shard_map.51.held = f32[512,3072]{1,0:T(8,128)} custom-call(f32[512,3072]{1,0:T(8,128)} %shard_map.50.held, f32[512,1792]{1,0:T(8,128)S(1)} %get-tuple-element.29.ahead, bf16[640,512]{1,0:T(8,128)(2,1)S(1)} %collective-permute-done.4.part, bf16[512,512]{1,0:T(8,128)(2,1)S(1)} %get-tuple-element.22.rest), custom_call_target="tpu_custom_call", output_to_operand_aliasing={{}: (0, {})} | custom-call | flops 1000000000 | bytes 1000000 | tf_op jit(solution)/shard_map/pallas_call | solution.py:516
  76.8 3.9 %collective-permute-done.5.part = bf16[256,512]{1,0:T(8,128)(2,1)S(1)} collective-permute-done((bf16[256,512]{1,0:T(8,128)(2,1)S(1)}, bf16[256,512]{1,0:T(8,128)(2,1)S(1)}, u32[]{:S(2)}, u32[]{:S(2)}) %collective-permute-start.5) | collective-permute-done | bytes 262176 | tf_op jit(solution)/shard_map/ppermute | solution.py:537
  80.7 1.1 %shard_map.52.held = f32[512,3072]{1,0:T(8,128)} custom-call(f32[512,3072]{1,0:T(8,128)} %shard_map.51.held, f32[512,1792]{1,0:T(8,128)S(1)} %get-tuple-element.29.ahead, bf16[256,512]{1,0:T(8,128)(2,1)S(1)} %collective-permute-done.5.part, bf16[512,512]{1,0:T(8,128)(2,1)S(1)} %get-tuple-element.22.rest), custom_call_target="tpu_custom_call", output_to_operand_aliasing={{}: (0, {})} | custom-call | flops 1000000000 | bytes 1000000 | tf_op jit(solution)/shard_map/pallas_call | solution.py:516
  81.8 1.2 %collective-permute-done.6.part = bf16[128,512]{1,0:T(8,128)(2,1)S(1)} collective-permute-done((bf16[128,512]{1,0:T(8,128)(2,1)S(1)}, bf16[128,512]{1,0:T(8,128)(2,1)S(1)}, u32[]{:S(2)}, u32[]{:S(2)}) %collective-permute-start.6) | collective-permute-done | bytes 131104 | tf_op jit(solution)/shard_map/ppermute | solution.py:537
  83.0 1.0 %shard_map.53 = f32[512,3072]{1,0:T(8,128)} custom-call(f32[512,3072]{1,0:T(8,128)} %shard_map.52.held, f32[512,1792]{1,0:T(8,128)S(1)} %get-tuple-element.29.ahead, bf16[128,512]{1,0:T(8,128)(2,1)S(1)} %collective-permute-done.6.part, bf16[512,512]{1,0:T(8,128)(2,1)S(1)} %get-tuple-element.22.rest), custom_call_target="tpu_custom_call", output_to_operand_aliasing={{}: (0, {})} | custom-call | flops 1000000000 | bytes 1000000 | tf_op jit(solution)/shard_map/pallas_call | solution.py:516
Async XLA Ops:
  15.0 8.5 %collective-permute-start = (bf16[16,512]{1,0:T(8,128)(2,1)S(1)}, bf16[16,512]{1,0:T(8,128)(2,1)S(1)}, u32[]{:S(2)}, u32[]{:S(2)}) collective-permute-start(bf16[16,512]{1,0:T(8,128)(2,1)S(1)} %get-tuple-element.20.own_piece), channel_id=1, source_target_pairs={{0,64},{1,65},{2,66},{3,67},{4,68},{5,69},{6,70},{7,71},{8,72},{9,... | collective-permute-start | bytes 49160 | tf_op jit(solution)/shard_map/ppermute | solution.py:537
  17.5 26.7 %collective-permute-start.2 = (bf16[768,512]{1,0:T(8,128)(2,1)S(1)}, bf16[768,512]{1,0:T(8,128)(2,1)S(1)}, u32[]{:S(2)}, u32[]{:S(2)}) collective-permute-start(bf16[768,512]{1,0:T(8,128)(2,1)S(1)} %get-tuple-element.18.after.refs_1_), channel_id=1, source_target_pairs={{0,64},{1,65},{2,66},{3,67},{4,68},{5,69},{6,70},{7,71},{8,72},{9,... | collective-permute-start | bytes 2359304 | tf_op jit(solution)/shard_map/ppermute | solution.py:537
  17.6 26.6 %collective-permute-start.1 = (bf16[512,512]{1,0:T(8,128)(2,1)S(1)}, bf16[512,512]{1,0:T(8,128)(2,1)S(1)}, u32[]{:S(2)}, u32[]{:S(2)}) collective-permute-start(bf16[512,512]{1,0:T(8,128)(2,1)S(1)} %get-tuple-element.16.own.refs_0_), channel_id=1, source_target_pairs={{2,66},{4,68},{6,70},{8,72},{10,74},{12,76},{14,78},{16,80},{18,82... | collective-permute-start | bytes 1572872 | tf_op jit(solution)/shard_map/ppermute | solution.py:537
  21.4 39.6 %collective-permute-start.3 = (bf16[768,512]{1,0:T(8,128)(2,1)S(1)}, bf16[768,512]{1,0:T(8,128)(2,1)S(1)}, u32[]{:S(2)}, u32[]{:S(2)}) collective-permute-start(bf16[768,512]{1,0:T(8,128)(2,1)S(1)} %get-tuple-element.23.refs_2_), channel_id=1, source_target_pairs={{0,64},{1,65},{2,66},{3,67},{4,68},{5,69},{6,70},{7,71},{8,72},{9,... | collective-permute-start | bytes 2359304 | tf_op jit(solution)/shard_map/ppermute | solution.py:537
  21.6 53.5 %collective-permute-start.4 = (bf16[640,512]{1,0:T(8,128)(2,1)S(1)}, bf16[640,512]{1,0:T(8,128)(2,1)S(1)}, u32[]{:S(2)}, u32[]{:S(2)}) collective-permute-start(bf16[640,512]{1,0:T(8,128)(2,1)S(1)} %get-tuple-element.24.refs_3_), channel_id=1, source_target_pairs={{0,64},{1,65},{2,66},{3,67},{4,68},{5,69},{6,70},{7,71},{8,72},{9,... | collective-permute-start | bytes 1966088 | tf_op jit(solution)/shard_map/ppermute | solution.py:537
  23.5 57.1 %collective-permute-start.5 = (bf16[256,512]{1,0:T(8,128)(2,1)S(1)}, bf16[256,512]{1,0:T(8,128)(2,1)S(1)}, u32[]{:S(2)}, u32[]{:S(2)}) collective-permute-start(bf16[256,512]{1,0:T(8,128)(2,1)S(1)} %get-tuple-element.25.refs_4_), channel_id=1, source_target_pairs={{0,64},{1,65},{2,66},{3,67},{4,68},{5,69},{6,70},{7,71},{8,72},{9,... | collective-permute-start | bytes 786440 | tf_op jit(solution)/shard_map/ppermute | solution.py:537
  44.2 38.9 %collective-permute-start.6 = (bf16[128,512]{1,0:T(8,128)(2,1)S(1)}, bf16[128,512]{1,0:T(8,128)(2,1)S(1)}, u32[]{:S(2)}, u32[]{:S(2)}) collective-permute-start(bf16[128,512]{1,0:T(8,128)(2,1)S(1)} %get-tuple-element.26.refs_5_), channel_id=1, source_target_pairs={{0,64},{1,65},{2,66},{3,67},{4,68},{5,69},{6,70},{7,71},{8,72},{9,... | collective-permute-start | bytes 393224 | tf_op jit(solution)/shard_map/ppermute | solution.py:537

commit v6 on v5

--- a/solution.py
+++ b/solution.py
@@ -12,8 +12,9 @@
 NT = (((1,), (1,)), ((), ()))
 SIDE = 4
 PIECES = SIDE * SIDE
-PARTS = (512, 768, 768, 640, 256, 128)
-EARLY = 2
+PARTS = (256, 256, 768, 768, 640, 256, 128)
+LEAD = 2
+EARLY = 3
 DMA = pltpu.SemaphoreType.DMA
 HBM = pl.BlockSpec(memory_space=pltpu.HBM)
 VMEM = pl.BlockSpec(memory_space=pltpu.VMEM)
@@ -50,7 +51,8 @@
 
 
 def lead_kernel(panel, *refs):
-    *parts, got, load_sem, send_sem, recv_sem = refs
+    load_sem, send_sem, recv_sem = refs[-3:]
+    parts, got = refs[: -3 - LEAD], refs[-3 - LEAD : -3]
     row, col, core, _, _, _ = place()
     loads = []
     start = 0
@@ -59,47 +61,65 @@
             pltpu.make_async_copy(panel.at[pl.ds(start, part.shape[0])], part, load_sem.at[i])
         )
         start += part.shape[0]
-    for load in loads:
+    copies = [
+        remote(parts[i], got[i], send_sem.at[i], recv_sem.at[i], 1 - row, col)
+        for i in range(LEAD)
+    ]
+    for load in loads[:LEAD]:
         load.start()
 
-    @pl.when(core == 1)
-    def _():
-        copy = remote(parts[0], got, send_sem, recv_sem, 1 - row, col)
+    @pl.when(col > 0)
+    def _():
         greet(1 - row, col)
         pl.semaphore_wait(pltpu.get_barrier_semaphore(), 1)
-        loads[0].wait()
-        copy.start()
-        copy.wait()
-
-    @pl.when(core == 0)
-    def _():
-        loads[0].wait()
-
-    for load in loads[1:]:
+
+    loads[0].wait()
+
+    @pl.when(col > 0)
+    def _():
+        copies[0].start()
+
+    loads[1].wait()
+
+    @pl.when(core == 1)
+    def _():
+        copies[1].start()
+
+    for load in loads[LEAD:]:
+        load.start()
+    for load in loads[LEAD:]:
         load.wait()
 
+    @pl.when(col > 0)
+    def _():
+        copies[0].wait()
+
+    @pl.when(core == 1)
+    def _():
+        copies[1].wait()
+
 
 def lead(panel, lengths):
-    parts = [pltpu.VMEM((length, panel.shape[1]), panel.dtype) for length in lengths]
-    *parts, got = pl.pallas_call(
+    parts = tuple(pltpu.VMEM((length, panel.shape[1]), panel.dtype) for length in lengths)
+    outs = pl.pallas_call(
         lead_kernel,
-        out_shape=(*parts, parts[0]),
+        out_shape=parts + parts[:LEAD],
         in_specs=[HBM],
-        out_specs=(VMEM,) * (len(parts) + 1),
-        scratch_shapes=[DMA((len(lengths),)), DMA, DMA],
+        out_specs=(VMEM,) * (len(parts) + LEAD),
+        scratch_shapes=[DMA((len(lengths),)), DMA((LEAD,)), DMA((LEAD,))],
         compiler_params=pltpu.CompilerParams(
             collective_id=1, has_side_effects=True, vmem_limit_bytes=8 << 20
         ),
         name="lead",
     )(panel)
-    return parts, got
+    return outs[: len(parts)], outs[len(parts) :]
 
 
 def solve(value, before, below, inv, made):
     rest = value[:, : made.shape[1]]
     if below is not None:
         rest = rest - lax.dot_general(
-            before[...], below[...], NT, preferred_element_type=jnp.float32
+            before[...], jnp.concatenate([part[...] for part in below], axis=0), NT, preferred_element_type=jnp.float32
         )
     high = rest.astype(jnp.bfloat16)
     rest = rest - high.astype(jnp.float32)
@@ -124,7 +144,14 @@
 
 
 def solve_kernel(
-    rhs, inverse, own, got, after, held, piece_out,
+    rhs, inverse, *refs,
+):
+    own, got = refs[:LEAD], refs[LEAD : 2 * LEAD]
+    solve_body(rhs, inverse, own, got, *refs[2 * LEAD + 1 :])
+
+
+def solve_body(
+    rhs, inverse, own, got, held, piece_out,
     inv, made, before, land, load_sem, scatter_send, scatter_recv, before_send, before_recv,
 ):
     row, col, core, x_hi, _, _ = place()
@@ -218,7 +245,7 @@
             pltpu.VMEM(rhs.shape, rhs.dtype),
             pltpu.VMEM((length, block), jnp.bfloat16),
         ),
-        in_specs=[HBM] * 2 + [VMEM] * 2 + [ANY],
+        in_specs=[HBM] * 2 + [VMEM] * (2 * LEAD) + [ANY],
         out_specs=(VMEM, VMEM),
         scratch_shapes=[
             pltpu.VMEM((block, block), jnp.bfloat16),
@@ -232,7 +259,7 @@
         ),
         cost_estimate=BUSY,
         name="solve",
-    )(rhs, inverse, own, got, after)
+    )(rhs, inverse, *own, *got, after)
 
 
 def gather_kernel(
@@ -414,8 +441,9 @@
 
 
 def begin_kernel(held, full, rest, *refs, count, early):
-    owns, parts, got = refs[:count], refs[count : count + early], refs[count + early]
-    updated, solved, ahead, work, store_sem = refs[count + early + 1 :]
+    owns, parts = refs[:count], refs[count : count + early]
+    got = refs[count + early : count + early + LEAD]
+    updated, solved, ahead, work, store_sem = refs[count + early + LEAD :]
     row, col = lax.axis_index("row"), lax.axis_index("col")
     block = rest.shape[0]
     ready = work.shape[1]
@@ -429,12 +457,12 @@
             work.at[:, part], updated.at[:, part], store_sem.at[1 + index]
         )
 
-    def step(i, start, mine, theirs):
+    def step(i, start, mine, theirs, led):
         chunk = chunk_of(mine.shape[0])
         here = rows(i, chunk)
         column = pl.ds(pl.multiple_of(start + i * chunk, chunk), chunk)
         own = mine[here, :]
-        if start == 0:
+        if start < block:
             own = jnp.where((col < 2) & (row >= col), jnp.zeros_like(own), own)
         total = lax.dot_general(
             full[rows(row, block), :], own, NT, preferred_element_type=jnp.float32
@@ -445,8 +473,9 @@
             )
             return
         other = theirs[here, :]
-        if start == 0:
-            other = jnp.where(lax.rem(col, 2) == 1, got[here, :], other)
+        if led is not None:
+            other = jnp.where(lax.rem(col, 2) == 1, led[here, :], other)
+        if start < block:
             other = jnp.where((col < 2) & (1 - row >= col), jnp.zeros_like(other), other)
         total += lax.dot_general(rest[...], other, NT, preferred_element_type=jnp.float32)
         work[:, column] = held[:, column] - total
@@ -455,11 +484,14 @@
     stores = []
     for index, mine in enumerate(owns):
         length = mine.shape[0]
-        theirs = parts[index] if index < early else None
+        theirs = parts[index - 1] if 0 < index <= early else None
+        led = got[index] if 0 < index < LEAD else None
+        if index == 0:
+            theirs = got[0]
         pl.loop(0, length // chunk_of(length))(
-            functools.partial(step, start=start, mine=mine, theirs=theirs)
-        )
-        if index < early:
+            functools.partial(step, start=start, mine=mine, theirs=theirs, led=led)
+        )
+        if index <= early:
             stores.append(store(index, start, length))
             stores[-1].start()
         start += length
@@ -471,7 +503,7 @@
 
 def begin(held, full, rest, owns, parts, got):
     half, rows_dev = held.shape
-    ready = sum(part.shape[0] for part in parts)
+    ready = got[0].shape[0] + sum(part.shape[0] for part in parts)
     return pl.pallas_call(
         functools.partial(begin_kernel, count=len(owns), early=len(parts)),
         out_shape=(
@@ -479,34 +511,38 @@
             pltpu.HBM(full.shape, full.dtype),
             pltpu.VMEM((half, rows_dev - ready), jnp.float32),
         ),
-        in_specs=[VMEM] * (4 + len(owns) + len(parts)),
+        in_specs=[VMEM] * (3 + LEAD + len(owns) + len(parts)),
         out_specs=(HBM, HBM, VMEM),
         scratch_shapes=[
             pltpu.VMEM((half, ready), jnp.float32),
-            DMA((1 + len(parts),)),
+            DMA((2 + len(parts),)),
         ],
         compiler_params=pltpu.CompilerParams(vmem_limit_bytes=32 << 20),
         cost_estimate=BUSY,
         name="begin",
-    )(held, full, rest, *owns, *parts, got)
+    )(held, full, rest, *owns, *parts, *got)
 
 
 def finish_kernel(start, offset, held, ahead, part, rest, updated, work, store_sem):
     length = part.shape[0]
     chunk = chunk_of(length)
+    half = work.shape[0] // 2
     stores = []
     for j in range(length // chunk):
         here = pl.ds(j * chunk, chunk)
-        total = lax.dot_general(
-            rest[...], part[here, :], NT, preferred_element_type=jnp.float32
-        )
-        work[:, here] = ahead[:, pl.ds(offset + j * chunk, chunk)] - total
-        stores.append(
-            pltpu.make_async_copy(
-                work.at[:, here], updated.at[:, pl.ds(start + j * chunk, chunk)], store_sem.at[j]
+        there = pl.ds(start + j * chunk, chunk)
+        for h in range(2):
+            tall = pl.ds(h * half, half)
+            total = lax.dot_general(
+                rest[tall, :], part[here, :], NT, preferred_element_type=jnp.float32
             )
-        )
-        stores[-1].start()
+            work[tall, here] = ahead[tall, pl.ds(offset + j * chunk, chunk)] - total
+            stores.append(
+                pltpu.make_async_copy(
+                    work.at[tall, here], updated.at[tall, there], store_sem.at[2 * j + h]
+                )
+            )
+            stores[-1].start()
     for copy in stores:
         copy.wait()
 
@@ -520,7 +556,7 @@
         out_specs=HBM,
         scratch_shapes=[
             pltpu.VMEM((ahead.shape[0], length), jnp.float32),
-            DMA((length // chunk_of(length),)),
+            DMA((2 * length // chunk_of(length),)),
         ],
         input_output_aliases={0: 0},
         compiler_params=pltpu.CompilerParams(vmem_limit_bytes=12 << 20),
@@ -545,11 +581,13 @@
     count = len(PARTS)
     starts = [sum(PARTS[:i]) for i in range(count)]
     sent, got = lead(panel, PARTS)
-    arrived = [swap(sent[i], lambda col: i > 0 or (col % 2 == 0 and col > 0)) for i in range(count)]
-    held, piece = solve_pieces(rhs, inverse, sent[0], got, sent[1])
+    arrived = [got[0]]
+    for i in range(1, count):
+        arrived.append(swap(sent[i], lambda col: i >= LEAD or (col % 2 == 0 and col > 0)))
+    held, piece = solve_pieces(rhs, inverse, sent[:LEAD], got, sent[LEAD])
     taken = swap(piece, lambda col: True)
     full, rest = gather_pieces(piece, taken)
-    updated, solved, ahead = begin(held, full, rest, sent, arrived[:EARLY], got)
+    updated, solved, ahead = begin(held, full, rest, sent, arrived[1:EARLY], got)
     for i in range(EARLY, count):
         updated = finish(updated, ahead, arrived[i], rest, starts[i], starts[i] - starts[EARLY])
     return solved, updated

time: 84.2 us -> 88.7 us (1.053)
  Pallas kernels: 41.8 us -> 47.7 us
  waiting for transfers between devices: 32.9 us -> 31.7 us
    pallas_call x1, Pallas kernels: 1.95 us -> 9.47 us  [lead(): pl.pallas_call(lead_kernel, out_shape=parts + parts[:LEAD], in_specs=[HBM...]
    pallas_call x1, Pallas kernels: 16.6 us -> 15.3 us  [gather_pieces(): pl.pallas_call(gather_kernel, out_shape=(pltpu.VMEM((2 * half, block), jn...]
    ppermute x7, waiting for transfers between devices: 32.9 us -> 31.7 us  [swap(): taken = lax.ppermute(value, ('row', 'col'), pairs)]
  transfers between devices with their start and end apart: 7 -> 7, of which waited for: 5 -> 5; matrix products, arithmetic and copies ran while one was open for 0% -> 0% of each run, Pallas kernels for 31% -> 28%
where the time goes in v6:
time: 88.7 us; the launch traced here: 88.6 us
  Pallas kernels  47.7 us (54%)
  waiting for transfers between devices  31.7 us (36%)
  starting transfers between devices  8.51 us (10%)
    ppermute x7, waiting for transfers between devices, swap(): taken = lax.ppermute(value, ('row', 'col'), pairs)  31.7 us
    pallas_call x1, Pallas kernels, gather_pieces(): pl.pallas_call(gather_kernel, out_shape=(pltpu.VMEM((2 * half, block), jn...  15.3 us
    pallas_call x1, Pallas kernels, solve_pieces(): pl.pallas_call(solve_kernel, out_shape=(pltpu.VMEM(rhs.shape, rhs.dtype),...  12.5 us
    pallas_call x1, Pallas kernels, lead(): pl.pallas_call(lead_kernel, out_shape=parts + parts[:LEAD], in_specs=[HBM...  9.47 us
    ppermute x7, starting transfers between devices, swap(): taken = lax.ppermute(value, ('row', 'col'), pairs)  8.51 us
    pallas_call x4, Pallas kernels, finish(): pl.pallas_call(functools.partial(finish_kernel, start, offset), out_shape...  5.31 us
    pallas_call x1, Pallas kernels, begin(): pl.pallas_call(functools.partial(begin_kernel, count=len(owns), early=len...  5.19 us
  transfers between devices with their start and end apart: 7, of which 5 were waited for; matrix products, arithmetic and copies ran while one was open for 0% of the time, Pallas kernels for 28%

profile of v6, /device:TPU:124, one launch (start us, length us, event | category | flops | bytes accessed | tf_op | source)
XLA Modules:
  0.0 88.6 jit_solution(17353510298847814684)
XLA Ops:
  0.6 9.5 %lead.1 = (bf16[256,512]{1,0:T(8,128)(2,1)S(1)}, bf16[256,512]{1,0:T(8,128)(2,1)S(1)}, bf16[768,512]{1,0:T(8,128)(2,1)S(1)}, bf16[768,512]{1,0:T(8,128)(2,1)S(1)...) custom-call(bf16[3072,512]{1,0:T(8,128)(2,1)} %panel.1), custom_call_target="tpu_custom_call" | custom-call | tf_op jit(solution)/shard_map/lead/pallas_call | solution.py:104
  10.1 12.5 %solve.1 = (f32[512,3072]{1,0:T(8,128)S(1)}, bf16[16,512]{1,0:T(8,128)(2,1)S(1)}) custom-call(f32[512,3072]{1,0:T(8,128)} %rhs.1, bf16[2,512,512]{2,1,0:T(8,128)(2,1)} %inverse.1, bf16[256,512]{1,0:T(8,128)(2,1)S(1)} %get-tuple-element.18.refs_0_, bf16[256,512]{1,0:T(8,128)(2,1)S(1)} %get-tuple-element.19.refs_1_, ...), custom_call_target="tpu_custom_call" | custom-call | flops 10000000000 | bytes 1000000 | tf_op jit(solution)/shard_map/solve/pallas_call | solution.py:242
  22.6 2.4 %collective-permute-start = (bf16[16,512]{1,0:T(8,128)(2,1)S(1)}, bf16[16,512]{1,0:T(8,128)(2,1)S(1)}, u32[]{:S(2)}, u32[]{:S(2)}) collective-permute-start(bf16[16,512]{1,0:T(8,128)(2,1)S(1)} %get-tuple-element.24.own_piece), channel_id=1, source_target_pairs={{0,64},{1,65},{2,66},{3,67},{4,68},{5,69},{6,70},{7,71},{8,72},{9,... | collective-permute-start | bytes 49160 | tf_op jit(solution)/shard_map/ppermute | solution.py:573
  25.0 0.1 collective-permute-start.2
  25.1 3.8 %collective-permute-start.1 = (bf16[256,512]{1,0:T(8,128)(2,1)S(1)}, bf16[256,512]{1,0:T(8,128)(2,1)S(1)}, u32[]{:S(2)}, u32[]{:S(2)}) collective-permute-start(bf16[256,512]{1,0:T(8,128)(2,1)S(1)} %get-tuple-element.19.refs_1_), channel_id=1, source_target_pairs={{2,66},{4,68},{6,70},{8,72},{10,74},{12,76},{14,78},{16,80},{18,82... | collective-permute-start | bytes 786440 | tf_op jit(solution)/shard_map/ppermute | solution.py:573
  28.9 0.2 collective-permute-start.3
  29.1 1.9 %collective-permute-start.4 = (bf16[640,512]{1,0:T(8,128)(2,1)S(1)}, bf16[640,512]{1,0:T(8,128)(2,1)S(1)}, u32[]{:S(2)}, u32[]{:S(2)}) collective-permute-start(bf16[640,512]{1,0:T(8,128)(2,1)S(1)} %get-tuple-element.28.refs_4_), channel_id=1, source_target_pairs={{0,64},{1,65},{2,66},{3,67},{4,68},{5,69},{6,70},{7,71},{8,72},{9,... | collective-permute-start | bytes 1966088 | tf_op jit(solution)/shard_map/ppermute | solution.py:573
  31.0 0.0 collective-permute-done.taken
  31.0 0.1 collective-permute-start.5
  31.1 15.3 %gather.1 = (bf16[1024,512]{1,0:T(8,128)(2,1)S(1)}, bf16[512,512]{1,0:T(8,128)(2,1)S(1)}) custom-call(bf16[16,512]{1,0:T(8,128)(2,1)S(1)} %get-tuple-element.24.own_piece, bf16[16,512]{1,0:T(8,128)(2,1)S(1)} %collective-permute-done.taken), custom_call_target="tpu_custom_call" | custom-call | flops 10000000000 | bytes 1000000 | tf_op jit(solution)/shard_map/gather/pallas_call | solution.py:418
  46.4 3.4 %collective-permute-done.1.refs_7_ = bf16[256,512]{1,0:T(8,128)(2,1)S(1)} collective-permute-done((bf16[256,512]{1,0:T(8,128)(2,1)S(1)}, bf16[256,512]{1,0:T(8,128)(2,1)S(1)}, u32[]{:S(2)}, u32[]{:S(2)}) %collective-permute-start.1) | collective-permute-done | bytes 262176 | tf_op jit(solution)/shard_map/ppermute | solution.py:573
  49.8 0.0 collective-permute-start.6
  49.8 0.0 collective-permute-done.2.refs_8_
  49.8 5.2 %begin.1 = (f32[512,3072]{1,0:T(8,128)}, bf16[1024,512]{1,0:T(8,128)(2,1)}, f32[512,1792]{1,0:T(8,128)S(1)}) custom-call(f32[512,3072]{1,0:T(8,128)S(1)} %get-tuple-element.23.held, bf16[1024,512]{1,0:T(8,128)(2,1)S(1)} %get-tuple-element.25.full, bf16[512,512]{1,0:T(8,128)(2,1)S(1)} %get-tuple-element.26.rest, ...), custom_call_target="tpu_custom_call" | custom-call | flops 10000000000 | bytes 1000000 | tf_op jit(solution)/shard_map/begin/pallas_call | solution.py:507
  55.0 11.7 %collective-permute-done.3.part = bf16[768,512]{1,0:T(8,128)(2,1)S(1)} collective-permute-done((bf16[768,512]{1,0:T(8,128)(2,1)S(1)}, bf16[768,512]{1,0:T(8,128)(2,1)S(1)}, u32[]{:S(2)}, u32[]{:S(2)}) %collective-permute-start.3) | collective-permute-done | bytes 786464 | tf_op jit(solution)/shard_map/ppermute | solution.py:573
  66.6 1.5 %shard_map.50.held = f32[512,3072]{1,0:T(8,128)} custom-call(f32[512,3072]{1,0:T(8,128)} %get-tuple-element.32.held, f32[512,1792]{1,0:T(8,128)S(1)} %get-tuple-element.33.ahead, bf16[768,512]{1,0:T(8,128)(2,1)S(1)} %collective-permute-done.3.part, bf16[512,512]{1,0:T(8,128)(2,1)S(1)} %get-tuple-element.26.rest), custom_call_target="tpu_custom_call", output_to_operand_aliasing={{}: (0, {})} | custom-call | flops 1000000000 | bytes 1000000 | tf_op jit(solution)/shard_map/pallas_call | solution.py:552
  68.1 12.5 %collective-permute-done.4.part = bf16[640,512]{1,0:T(8,128)(2,1)S(1)} collective-permute-done((bf16[640,512]{1,0:T(8,128)(2,1)S(1)}, bf16[640,512]{1,0:T(8,128)(2,1)S(1)}, u32[]{:S(2)}, u32[]{:S(2)}) %collective-permute-start.4) | collective-permute-done | bytes 655392 | tf_op jit(solution)/shard_map/ppermute | solution.py:573
  80.7 1.6 %shard_map.51.held = f32[512,3072]{1,0:T(8,128)} custom-call(f32[512,3072]{1,0:T(8,128)} %shard_map.50.held, f32[512,1792]{1,0:T(8,128)S(1)} %get-tuple-element.33.ahead, bf16[640,512]{1,0:T(8,128)(2,1)S(1)} %collective-permute-done.4.part, bf16[512,512]{1,0:T(8,128)(2,1)S(1)} %get-tuple-element.26.rest), custom_call_target="tpu_custom_call", output_to_operand_aliasing={{}: (0, {})} | custom-call | flops 1000000000 | bytes 1000000 | tf_op jit(solution)/shard_map/pallas_call | solution.py:552
  82.3 3.9 %collective-permute-done.5.part = bf16[256,512]{1,0:T(8,128)(2,1)S(1)} collective-permute-done((bf16[256,512]{1,0:T(8,128)(2,1)S(1)}, bf16[256,512]{1,0:T(8,128)(2,1)S(1)}, u32[]{:S(2)}, u32[]{:S(2)}) %collective-permute-start.5) | collective-permute-done | bytes 262176 | tf_op jit(solution)/shard_map/ppermute | solution.py:573
  86.2 1.1 %shard_map.52.held = f32[512,3072]{1,0:T(8,128)} custom-call(f32[512,3072]{1,0:T(8,128)} %shard_map.51.held, f32[512,1792]{1,0:T(8,128)S(1)} %get-tuple-element.33.ahead, bf16[256,512]{1,0:T(8,128)(2,1)S(1)} %collective-permute-done.5.part, bf16[512,512]{1,0:T(8,128)(2,1)S(1)} %get-tuple-element.26.rest), custom_call_target="tpu_custom_call", output_to_operand_aliasing={{}: (0, {})} | custom-call | flops 1000000000 | bytes 1000000 | tf_op jit(solution)/shard_map/pallas_call | solution.py:552
  87.3 0.3 collective-permute-done.6.part
  87.6 1.0 %shard_map.53 = f32[512,3072]{1,0:T(8,128)} custom-call(f32[512,3072]{1,0:T(8,128)} %shard_map.52.held, f32[512,1792]{1,0:T(8,128)S(1)} %get-tuple-element.33.ahead, bf16[128,512]{1,0:T(8,128)(2,1)S(1)} %collective-permute-done.6.part, bf16[512,512]{1,0:T(8,128)(2,1)S(1)} %get-tuple-element.26.rest), custom_call_target="tpu_custom_call", output_to_operand_aliasing={{}: (0, {})} | custom-call | flops 1000000000 | bytes 1000000 | tf_op jit(solution)/shard_map/pallas_call | solution.py:552
Async XLA Ops:
  22.6 8.4 %collective-permute-start = (bf16[16,512]{1,0:T(8,128)(2,1)S(1)}, bf16[16,512]{1,0:T(8,128)(2,1)S(1)}, u32[]{:S(2)}, u32[]{:S(2)}) collective-permute-start(bf16[16,512]{1,0:T(8,128)(2,1)S(1)} %get-tuple-element.24.own_piece), channel_id=1, source_target_pairs={{0,64},{1,65},{2,66},{3,67},{4,68},{5,69},{6,70},{7,71},{8,72},{9,... | collective-permute-start | bytes 49160 | tf_op jit(solution)/shard_map/ppermute | solution.py:573
  25.0 24.8 %collective-permute-start.2 = (bf16[768,512]{1,0:T(8,128)(2,1)S(1)}, bf16[768,512]{1,0:T(8,128)(2,1)S(1)}, u32[]{:S(2)}, u32[]{:S(2)}) collective-permute-start(bf16[768,512]{1,0:T(8,128)(2,1)S(1)} %get-tuple-element.22.refs_4_.refs_2_), channel_id=1, source_target_pairs={{0,64},{1,65},{2,66},{3,67},{4,68},{5,69},{6,70},{7,71},{8,72},{9,... | collective-permute-start | bytes 2359304 | tf_op jit(solution)/shard_map/ppermute | solution.py:573
  25.1 24.7 %collective-permute-start.1 = (bf16[256,512]{1,0:T(8,128)(2,1)S(1)}, bf16[256,512]{1,0:T(8,128)(2,1)S(1)}, u32[]{:S(2)}, u32[]{:S(2)}) collective-permute-start(bf16[256,512]{1,0:T(8,128)(2,1)S(1)} %get-tuple-element.19.refs_1_), channel_id=1, source_target_pairs={{2,66},{4,68},{6,70},{8,72},{10,74},{12,76},{14,78},{16,80},{18,82... | collective-permute-start | bytes 786440 | tf_op jit(solution)/shard_map/ppermute | solution.py:573
  28.9 37.7 %collective-permute-start.3 = (bf16[768,512]{1,0:T(8,128)(2,1)S(1)}, bf16[768,512]{1,0:T(8,128)(2,1)S(1)}, u32[]{:S(2)}, u32[]{:S(2)}) collective-permute-start(bf16[768,512]{1,0:T(8,128)(2,1)S(1)} %get-tuple-element.27.refs_3_), channel_id=1, source_target_pairs={{0,64},{1,65},{2,66},{3,67},{4,68},{5,69},{6,70},{7,71},{8,72},{9,... | collective-permute-start | bytes 2359304 | tf_op jit(solution)/shard_map/ppermute | solution.py:573
  29.1 51.6 %collective-permute-start.4 = (bf16[640,512]{1,0:T(8,128)(2,1)S(1)}, bf16[640,512]{1,0:T(8,128)(2,1)S(1)}, u32[]{:S(2)}, u32[]{:S(2)}) collective-permute-start(bf16[640,512]{1,0:T(8,128)(2,1)S(1)} %get-tuple-element.28.refs_4_), channel_id=1, source_target_pairs={{0,64},{1,65},{2,66},{3,67},{4,68},{5,69},{6,70},{7,71},{8,72},{9,... | collective-permute-start | bytes 1966088 | tf_op jit(solution)/shard_map/ppermute | solution.py:573
  31.0 55.2 %collective-permute-start.5 = (bf16[256,512]{1,0:T(8,128)(2,1)S(1)}, bf16[256,512]{1,0:T(8,128)(2,1)S(1)}, u32[]{:S(2)}, u32[]{:S(2)}) collective-permute-start(bf16[256,512]{1,0:T(8,128)(2,1)S(1)} %get-tuple-element.29.refs_5_), channel_id=1, source_target_pairs={{0,64},{1,65},{2,66},{3,67},{4,68},{5,69},{6,70},{7,71},{8,72},{9,... | collective-permute-start | bytes 786440 | tf_op jit(solution)/shard_map/ppermute | solution.py:573
  49.8 37.8 %collective-permute-start.6 = (bf16[128,512]{1,0:T(8,128)(2,1)S(1)}, bf16[128,512]{1,0:T(8,128)(2,1)S(1)}, u32[]{:S(2)}, u32[]{:S(2)}) collective-permute-start(bf16[128,512]{1,0:T(8,128)(2,1)S(1)} %get-tuple-element.30.refs_6_), channel_id=1, source_target_pairs={{0,64},{1,65},{2,66},{3,67},{4,68},{5,69},{6,70},{7,71},{8,72},{9,... | collective-permute-start | bytes 393224 | tf_op jit(solution)/shard_map/ppermute | solution.py:573

commit v7 on v5

--- a/solution.py
+++ b/solution.py
@@ -13,6 +13,7 @@
 SIDE = 4
 PIECES = SIDE * SIDE
 PARTS = (512, 768, 768, 640, 256, 128)
+QUICK = 64
 EARLY = 2
 DMA = pltpu.SemaphoreType.DMA
 HBM = pl.BlockSpec(memory_space=pltpu.HBM)
@@ -59,21 +60,39 @@
             pltpu.make_async_copy(panel.at[pl.ds(start, part.shape[0])], part, load_sem.at[i])
         )
         start += part.shape[0]
-    for load in loads:
+    spans = (pl.ds(0, QUICK), pl.ds(QUICK, parts[0].shape[0] - QUICK))
+    lead_loads = [
+        pltpu.make_async_copy(panel.at[span], parts[0].at[span], load_sem.at[len(parts) + i])
+        for i, span in enumerate(spans)
+    ]
+    for load in lead_loads:
         load.start()
 
     @pl.when(core == 1)
     def _():
-        copy = remote(parts[0], got, send_sem, recv_sem, 1 - row, col)
+        copies = [
+            remote(
+                parts[0].at[span], got.at[span], send_sem.at[i], recv_sem.at[i], 1 - row, col
+            )
+            for i, span in enumerate(spans)
+        ]
         greet(1 - row, col)
+        lead_loads[0].wait()
         pl.semaphore_wait(pltpu.get_barrier_semaphore(), 1)
-        loads[0].wait()
-        copy.start()
-        copy.wait()
+        copies[0].start()
+        lead_loads[1].wait()
+        copies[1].start()
+        for load in loads[1:]:
+            load.start()
+        for copy in copies:
+            copy.wait()
 
     @pl.when(core == 0)
     def _():
-        loads[0].wait()
+        for load in loads[1:]:
+            load.start()
+        for load in lead_loads:
+            load.wait()
 
     for load in loads[1:]:
         load.wait()
@@ -86,7 +105,7 @@
         out_shape=(*parts, parts[0]),
         in_specs=[HBM],
         out_specs=(VMEM,) * (len(parts) + 1),
-        scratch_shapes=[DMA((len(lengths),)), DMA, DMA],
+        scratch_shapes=[DMA((len(lengths) + 2,)), DMA((2,)), DMA((2,))],
         compiler_params=pltpu.CompilerParams(
             collective_id=1, has_side_effects=True, vmem_limit_bytes=8 << 20
         ),

time: 84.2 us -> 84.2 us (level)
  no operation moved by 1% of the time
where the time goes in v7:
time: 84.2 us; the launch traced here: 84.1 us
  Pallas kernels  41.8 us (50%)
  waiting for transfers between devices  32.9 us (39%)
  starting transfers between devices  8.61 us (10%)
    ppermute x7, waiting for transfers between devices, swap(): taken = lax.ppermute(value, ('row', 'col'), pairs)  32.9 us
    pallas_call x1, Pallas kernels, gather_pieces(): pl.pallas_call(gather_kernel, out_shape=(pltpu.VMEM((2 * half, block), jn...  16.6 us
    pallas_call x1, Pallas kernels, solve_pieces(): pl.pallas_call(solve_kernel, out_shape=(pltpu.VMEM(rhs.shape, rhs.dtype),...  12.4 us
    ppermute x7, starting transfers between devices, swap(): taken = lax.ppermute(value, ('row', 'col'), pairs)  8.61 us
    pallas_call x4, Pallas kernels, finish(): pl.pallas_call(functools.partial(finish_kernel, start, offset), out_shape...  5.45 us
    pallas_call x1, Pallas kernels, begin(): pl.pallas_call(functools.partial(begin_kernel, count=len(owns), early=len...  5.35 us
    pallas_call x1, Pallas kernels, lead(): pl.pallas_call(lead_kernel, out_shape=(*parts, parts[0]), in_specs=[HBM],...  2.01 us
  transfers between devices with their start and end apart: 7, of which 5 were waited for; matrix products, arithmetic and copies ran while one was open for 0% of the time, Pallas kernels for 31%

profile of v7, /device:TPU:124, one launch (start us, length us, event | category | flops | bytes accessed | tf_op | source)
XLA Modules:
  0.0 84.1 jit_solution(11351203548285242395)
XLA Ops:
  0.6 2.0 %lead.1 = (bf16[512,512]{1,0:T(8,128)(2,1)S(1)}, bf16[768,512]{1,0:T(8,128)(2,1)S(1)}, bf16[768,512]{1,0:T(8,128)(2,1)S(1)}, bf16[640,512]{1,0:T(8,128)(2,1)S(1)...) custom-call(bf16[3072,512]{1,0:T(8,128)(2,1)} %panel.1), custom_call_target="tpu_custom_call" | custom-call | tf_op jit(solution)/shard_map/lead/pallas_call | solution.py:103
  2.6 12.4 %solve.1 = (f32[512,3072]{1,0:T(8,128)S(1)}, bf16[16,512]{1,0:T(8,128)(2,1)S(1)}) custom-call(f32[512,3072]{1,0:T(8,128)} %rhs.1, bf16[2,512,512]{2,1,0:T(8,128)(2,1)} %inverse.1, bf16[512,512]{1,0:T(8,128)(2,1)S(1)} %get-tuple-element.16.own.refs_0_, bf16[512,512]{1,0:T(8,128)(2,1)S(1)} %get-tuple-element.17.got.refs_8_, ...), custom_call_target="tpu_custom_call" | custom-call | flops 10000000000 | bytes 1000000 | tf_op jit(solution)/shard_map/solve/pallas_call | solution.py:234
  15.1 2.5 %collective-permute-start = (bf16[16,512]{1,0:T(8,128)(2,1)S(1)}, bf16[16,512]{1,0:T(8,128)(2,1)S(1)}, u32[]{:S(2)}, u32[]{:S(2)}) collective-permute-start(bf16[16,512]{1,0:T(8,128)(2,1)S(1)} %get-tuple-element.20.own_piece), channel_id=1, source_target_pairs={{0,64},{1,65},{2,66},{3,67},{4,68},{5,69},{6,70},{7,71},{8,72},{9,... | collective-permute-start | bytes 49160 | tf_op jit(solution)/shard_map/ppermute | solution.py:556
  17.6 0.1 collective-permute-start.2
  17.6 3.8 %collective-permute-start.1 = (bf16[512,512]{1,0:T(8,128)(2,1)S(1)}, bf16[512,512]{1,0:T(8,128)(2,1)S(1)}, u32[]{:S(2)}, u32[]{:S(2)}) collective-permute-start(bf16[512,512]{1,0:T(8,128)(2,1)S(1)} %get-tuple-element.16.own.refs_0_), channel_id=1, source_target_pairs={{2,66},{4,68},{6,70},{8,72},{10,74},{12,76},{14,78},{16,80},{18,82... | collective-permute-start | bytes 1572872 | tf_op jit(solution)/shard_map/ppermute | solution.py:556
  21.5 0.2 collective-permute-start.3
  21.7 1.9 %collective-permute-start.4 = (bf16[640,512]{1,0:T(8,128)(2,1)S(1)}, bf16[640,512]{1,0:T(8,128)(2,1)S(1)}, u32[]{:S(2)}, u32[]{:S(2)}) collective-permute-start(bf16[640,512]{1,0:T(8,128)(2,1)S(1)} %get-tuple-element.24.refs_3_), channel_id=1, source_target_pairs={{0,64},{1,65},{2,66},{3,67},{4,68},{5,69},{6,70},{7,71},{8,72},{9,... | collective-permute-start | bytes 1966088 | tf_op jit(solution)/shard_map/ppermute | solution.py:556
  23.6 0.0 collective-permute-done.taken
  23.6 0.1 collective-permute-start.5
  23.7 16.6 %gather.1 = (bf16[1024,512]{1,0:T(8,128)(2,1)S(1)}, bf16[512,512]{1,0:T(8,128)(2,1)S(1)}) custom-call(bf16[16,512]{1,0:T(8,128)(2,1)S(1)} %get-tuple-element.20.own_piece, bf16[16,512]{1,0:T(8,128)(2,1)S(1)} %collective-permute-done.taken), custom_call_target="tpu_custom_call" | custom-call | flops 10000000000 | bytes 1000000 | tf_op jit(solution)/shard_map/gather/pallas_call | solution.py:410
  40.3 4.0 %collective-permute-done.1.refs_6_ = bf16[512,512]{1,0:T(8,128)(2,1)S(1)} collective-permute-done((bf16[512,512]{1,0:T(8,128)(2,1)S(1)}, bf16[512,512]{1,0:T(8,128)(2,1)S(1)}, u32[]{:S(2)}, u32[]{:S(2)}) %collective-permute-start.1) | collective-permute-done | bytes 524320 | tf_op jit(solution)/shard_map/ppermute | solution.py:556
  44.3 0.0 collective-permute-start.6
  44.4 0.0 collective-permute-done.2.refs_7_
  44.4 5.3 %begin.1 = (f32[512,3072]{1,0:T(8,128)}, bf16[1024,512]{1,0:T(8,128)(2,1)}, f32[512,1792]{1,0:T(8,128)S(1)}) custom-call(f32[512,3072]{1,0:T(8,128)S(1)} %get-tuple-element.19.held, bf16[1024,512]{1,0:T(8,128)(2,1)S(1)} %get-tuple-element.21.full, bf16[512,512]{1,0:T(8,128)(2,1)S(1)} %get-tuple-element.22.rest, ...), custom_call_target="tpu_custom_call" | custom-call | flops 10000000000 | bytes 1000000 | tf_op jit(solution)/shard_map/begin/pallas_call | solution.py:494
  49.7 11.5 %collective-permute-done.3.part = bf16[768,512]{1,0:T(8,128)(2,1)S(1)} collective-permute-done((bf16[768,512]{1,0:T(8,128)(2,1)S(1)}, bf16[768,512]{1,0:T(8,128)(2,1)S(1)}, u32[]{:S(2)}, u32[]{:S(2)}) %collective-permute-start.3) | collective-permute-done | bytes 786464 | tf_op jit(solution)/shard_map/ppermute | solution.py:556
  61.2 1.6 %shard_map.50.held = f32[512,3072]{1,0:T(8,128)} custom-call(f32[512,3072]{1,0:T(8,128)} %get-tuple-element.28.held, f32[512,1792]{1,0:T(8,128)S(1)} %get-tuple-element.29.ahead, bf16[768,512]{1,0:T(8,128)(2,1)S(1)} %collective-permute-done.3.part, bf16[512,512]{1,0:T(8,128)(2,1)S(1)} %get-tuple-element.22.rest), custom_call_target="tpu_custom_call", output_to_operand_aliasing={{}: (0, {})} | custom-call | flops 1000000000 | bytes 1000000 | tf_op jit(solution)/shard_map/pallas_call | solution.py:535
  62.8 12.4 %collective-permute-done.4.part = bf16[640,512]{1,0:T(8,128)(2,1)S(1)} collective-permute-done((bf16[640,512]{1,0:T(8,128)(2,1)S(1)}, bf16[640,512]{1,0:T(8,128)(2,1)S(1)}, u32[]{:S(2)}, u32[]{:S(2)}) %collective-permute-start.4) | collective-permute-done | bytes 655392 | tf_op jit(solution)/shard_map/ppermute | solution.py:556
  75.2 1.7 %shard_map.51.held = f32[512,3072]{1,0:T(8,128)} custom-call(f32[512,3072]{1,0:T(8,128)} %shard_map.50.held, f32[512,1792]{1,0:T(8,128)S(1)} %get-tuple-element.29.ahead, bf16[640,512]{1,0:T(8,128)(2,1)S(1)} %collective-permute-done.4.part, bf16[512,512]{1,0:T(8,128)(2,1)S(1)} %get-tuple-element.22.rest), custom_call_target="tpu_custom_call", output_to_operand_aliasing={{}: (0, {})} | custom-call | flops 1000000000 | bytes 1000000 | tf_op jit(solution)/shard_map/pallas_call | solution.py:535
  77.0 3.9 %collective-permute-done.5.part = bf16[256,512]{1,0:T(8,128)(2,1)S(1)} collective-permute-done((bf16[256,512]{1,0:T(8,128)(2,1)S(1)}, bf16[256,512]{1,0:T(8,128)(2,1)S(1)}, u32[]{:S(2)}, u32[]{:S(2)}) %collective-permute-start.5) | collective-permute-done | bytes 262176 | tf_op jit(solution)/shard_map/ppermute | solution.py:556
  80.9 1.1 %shard_map.52.held = f32[512,3072]{1,0:T(8,128)} custom-call(f32[512,3072]{1,0:T(8,128)} %shard_map.51.held, f32[512,1792]{1,0:T(8,128)S(1)} %get-tuple-element.29.ahead, bf16[256,512]{1,0:T(8,128)(2,1)S(1)} %collective-permute-done.5.part, bf16[512,512]{1,0:T(8,128)(2,1)S(1)} %get-tuple-element.22.rest), custom_call_target="tpu_custom_call", output_to_operand_aliasing={{}: (0, {})} | custom-call | flops 1000000000 | bytes 1000000 | tf_op jit(solution)/shard_map/pallas_call | solution.py:535
  82.0 1.1 %collective-permute-done.6.part = bf16[128,512]{1,0:T(8,128)(2,1)S(1)} collective-permute-done((bf16[128,512]{1,0:T(8,128)(2,1)S(1)}, bf16[128,512]{1,0:T(8,128)(2,1)S(1)}, u32[]{:S(2)}, u32[]{:S(2)}) %collective-permute-start.6) | collective-permute-done | bytes 131104 | tf_op jit(solution)/shard_map/ppermute | solution.py:556
  83.1 1.0 %shard_map.53 = f32[512,3072]{1,0:T(8,128)} custom-call(f32[512,3072]{1,0:T(8,128)} %shard_map.52.held, f32[512,1792]{1,0:T(8,128)S(1)} %get-tuple-element.29.ahead, bf16[128,512]{1,0:T(8,128)(2,1)S(1)} %collective-permute-done.6.part, bf16[512,512]{1,0:T(8,128)(2,1)S(1)} %get-tuple-element.22.rest), custom_call_target="tpu_custom_call", output_to_operand_aliasing={{}: (0, {})} | custom-call | flops 1000000000 | bytes 1000000 | tf_op jit(solution)/shard_map/pallas_call | solution.py:535
Async XLA Ops:
  15.1 8.5 %collective-permute-start = (bf16[16,512]{1,0:T(8,128)(2,1)S(1)}, bf16[16,512]{1,0:T(8,128)(2,1)S(1)}, u32[]{:S(2)}, u32[]{:S(2)}) collective-permute-start(bf16[16,512]{1,0:T(8,128)(2,1)S(1)} %get-tuple-element.20.own_piece), channel_id=1, source_target_pairs={{0,64},{1,65},{2,66},{3,67},{4,68},{5,69},{6,70},{7,71},{8,72},{9,... | collective-permute-start | bytes 49160 | tf_op jit(solution)/shard_map/ppermute | solution.py:556
  17.6 26.8 %collective-permute-start.2 = (bf16[768,512]{1,0:T(8,128)(2,1)S(1)}, bf16[768,512]{1,0:T(8,128)(2,1)S(1)}, u32[]{:S(2)}, u32[]{:S(2)}) collective-permute-start(bf16[768,512]{1,0:T(8,128)(2,1)S(1)} %get-tuple-element.18.after.refs_1_), channel_id=1, source_target_pairs={{0,64},{1,65},{2,66},{3,67},{4,68},{5,69},{6,70},{7,71},{8,72},{9,... | collective-permute-start | bytes 2359304 | tf_op jit(solution)/shard_map/ppermute | solution.py:556
  17.6 26.7 %collective-permute-start.1 = (bf16[512,512]{1,0:T(8,128)(2,1)S(1)}, bf16[512,512]{1,0:T(8,128)(2,1)S(1)}, u32[]{:S(2)}, u32[]{:S(2)}) collective-permute-start(bf16[512,512]{1,0:T(8,128)(2,1)S(1)} %get-tuple-element.16.own.refs_0_), channel_id=1, source_target_pairs={{2,66},{4,68},{6,70},{8,72},{10,74},{12,76},{14,78},{16,80},{18,82... | collective-permute-start | bytes 1572872 | tf_op jit(solution)/shard_map/ppermute | solution.py:556
  21.5 39.7 %collective-permute-start.3 = (bf16[768,512]{1,0:T(8,128)(2,1)S(1)}, bf16[768,512]{1,0:T(8,128)(2,1)S(1)}, u32[]{:S(2)}, u32[]{:S(2)}) collective-permute-start(bf16[768,512]{1,0:T(8,128)(2,1)S(1)} %get-tuple-element.23.refs_2_), channel_id=1, source_target_pairs={{0,64},{1,65},{2,66},{3,67},{4,68},{5,69},{6,70},{7,71},{8,72},{9,... | collective-permute-start | bytes 2359304 | tf_op jit(solution)/shard_map/ppermute | solution.py:556
  21.7 53.6 %collective-permute-start.4 = (bf16[640,512]{1,0:T(8,128)(2,1)S(1)}, bf16[640,512]{1,0:T(8,128)(2,1)S(1)}, u32[]{:S(2)}, u32[]{:S(2)}) collective-permute-start(bf16[640,512]{1,0:T(8,128)(2,1)S(1)} %get-tuple-element.24.refs_3_), channel_id=1, source_target_pairs={{0,64},{1,65},{2,66},{3,67},{4,68},{5,69},{6,70},{7,71},{8,72},{9,... | collective-permute-start | bytes 1966088 | tf_op jit(solution)/shard_map/ppermute | solution.py:556
  23.6 57.3 %collective-permute-start.5 = (bf16[256,512]{1,0:T(8,128)(2,1)S(1)}, bf16[256,512]{1,0:T(8,128)(2,1)S(1)}, u32[]{:S(2)}, u32[]{:S(2)}) collective-permute-start(bf16[256,512]{1,0:T(8,128)(2,1)S(1)} %get-tuple-element.25.refs_4_), channel_id=1, source_target_pairs={{0,64},{1,65},{2,66},{3,67},{4,68},{5,69},{6,70},{7,71},{8,72},{9,... | collective-permute-start | bytes 786440 | tf_op jit(solution)/shard_map/ppermute | solution.py:556
  44.3 38.7 %collective-permute-start.6 = (bf16[128,512]{1,0:T(8,128)(2,1)S(1)}, bf16[128,512]{1,0:T(8,128)(2,1)S(1)}, u32[]{:S(2)}, u32[]{:S(2)}) collective-permute-start(bf16[128,512]{1,0:T(8,128)(2,1)S(1)} %get-tuple-element.26.refs_5_), channel_id=1, source_target_pairs={{0,64},{1,65},{2,66},{3,67},{4,68},{5,69},{6,70},{7,71},{8,72},{9,... | collective-permute-start | bytes 393224 | tf_op jit(solution)/shard_map/ppermute | solution.py:556

commit v8 on v5

--- a/solution.py
+++ b/solution.py
@@ -59,23 +59,23 @@
             pltpu.make_async_copy(panel.at[pl.ds(start, part.shape[0])], part, load_sem.at[i])
         )
         start += part.shape[0]
-    for load in loads:
-        load.start()
 
     @pl.when(core == 1)
     def _():
-        copy = remote(parts[0], got, send_sem, recv_sem, 1 - row, col)
+        copy = remote(panel.at[pl.ds(0, got.shape[0])], got, send_sem, recv_sem, 1 - row, col)
         greet(1 - row, col)
         pl.semaphore_wait(pltpu.get_barrier_semaphore(), 1)
-        loads[0].wait()
         copy.start()
+        for load in loads:
+            load.start()
         copy.wait()
 
     @pl.when(core == 0)
     def _():
-        loads[0].wait()
-
-    for load in loads[1:]:
+        for load in loads:
+            load.start()
+
+    for load in loads:
         load.wait()
 
 

time: 84.2 us -> 84.2 us (level)
  no operation moved by 1% of the time
where the time goes in v8:
time: 84.2 us; the launch traced here: 84.1 us
  Pallas kernels  41.9 us (50%)
  waiting for transfers between devices  32.9 us (39%)
  starting transfers between devices  8.61 us (10%)
    ppermute x7, waiting for transfers between devices, swap(): taken = lax.ppermute(value, ('row', 'col'), pairs)  32.9 us
    pallas_call x1, Pallas kernels, gather_pieces(): pl.pallas_call(gather_kernel, out_shape=(pltpu.VMEM((2 * half, block), jn...  16.7 us
    pallas_call x1, Pallas kernels, solve_pieces(): pl.pallas_call(solve_kernel, out_shape=(pltpu.VMEM(rhs.shape, rhs.dtype),...  12.4 us
    ppermute x7, starting transfers between devices, swap(): taken = lax.ppermute(value, ('row', 'col'), pairs)  8.61 us
    pallas_call x4, Pallas kernels, finish(): pl.pallas_call(functools.partial(finish_kernel, start, offset), out_shape...  5.43 us
    pallas_call x1, Pallas kernels, begin(): pl.pallas_call(functools.partial(begin_kernel, count=len(owns), early=len...  5.35 us
    pallas_call x1, Pallas kernels, lead(): pl.pallas_call(lead_kernel, out_shape=(*parts, parts[0]), in_specs=[HBM],...  1.97 us
  transfers between devices with their start and end apart: 7, of which 5 were waited for; matrix products, arithmetic and copies ran while one was open for 0% of the time, Pallas kernels for 31%

profile of v8, /device:TPU:124, one launch (start us, length us, event | category | flops | bytes accessed | tf_op | source)
XLA Modules:
  0.0 84.1 jit_solution(14932591876255794556)
XLA Ops:
  0.6 2.0 %lead.1 = (bf16[512,512]{1,0:T(8,128)(2,1)S(1)}, bf16[768,512]{1,0:T(8,128)(2,1)S(1)}, bf16[768,512]{1,0:T(8,128)(2,1)S(1)}, bf16[640,512]{1,0:T(8,128)(2,1)S(1)...) custom-call(bf16[3072,512]{1,0:T(8,128)(2,1)} %panel.1), custom_call_target="tpu_custom_call" | custom-call | tf_op jit(solution)/shard_map/lead/pallas_call | solution.py:84
  2.6 12.4 %solve.1 = (f32[512,3072]{1,0:T(8,128)S(1)}, bf16[16,512]{1,0:T(8,128)(2,1)S(1)}) custom-call(f32[512,3072]{1,0:T(8,128)} %rhs.1, bf16[2,512,512]{2,1,0:T(8,128)(2,1)} %inverse.1, bf16[512,512]{1,0:T(8,128)(2,1)S(1)} %get-tuple-element.16.own.refs_0_, bf16[512,512]{1,0:T(8,128)(2,1)S(1)} %get-tuple-element.17.got.refs_8_, ...), custom_call_target="tpu_custom_call" | custom-call | flops 10000000000 | bytes 1000000 | tf_op jit(solution)/shard_map/solve/pallas_call | solution.py:215
  15.0 2.5 %collective-permute-start = (bf16[16,512]{1,0:T(8,128)(2,1)S(1)}, bf16[16,512]{1,0:T(8,128)(2,1)S(1)}, u32[]{:S(2)}, u32[]{:S(2)}) collective-permute-start(bf16[16,512]{1,0:T(8,128)(2,1)S(1)} %get-tuple-element.20.own_piece), channel_id=1, source_target_pairs={{0,64},{1,65},{2,66},{3,67},{4,68},{5,69},{6,70},{7,71},{8,72},{9,... | collective-permute-start | bytes 49160 | tf_op jit(solution)/shard_map/ppermute | solution.py:537
  17.5 0.1 collective-permute-start.2
  17.6 3.8 %collective-permute-start.1 = (bf16[512,512]{1,0:T(8,128)(2,1)S(1)}, bf16[512,512]{1,0:T(8,128)(2,1)S(1)}, u32[]{:S(2)}, u32[]{:S(2)}) collective-permute-start(bf16[512,512]{1,0:T(8,128)(2,1)S(1)} %get-tuple-element.16.own.refs_0_), channel_id=1, source_target_pairs={{2,66},{4,68},{6,70},{8,72},{10,74},{12,76},{14,78},{16,80},{18,82... | collective-permute-start | bytes 1572872 | tf_op jit(solution)/shard_map/ppermute | solution.py:537
  21.4 0.2 collective-permute-start.3
  21.6 1.9 %collective-permute-start.4 = (bf16[640,512]{1,0:T(8,128)(2,1)S(1)}, bf16[640,512]{1,0:T(8,128)(2,1)S(1)}, u32[]{:S(2)}, u32[]{:S(2)}) collective-permute-start(bf16[640,512]{1,0:T(8,128)(2,1)S(1)} %get-tuple-element.24.refs_3_), channel_id=1, source_target_pairs={{0,64},{1,65},{2,66},{3,67},{4,68},{5,69},{6,70},{7,71},{8,72},{9,... | collective-permute-start | bytes 1966088 | tf_op jit(solution)/shard_map/ppermute | solution.py:537
  23.6 0.0 collective-permute-done.taken
  23.6 0.1 collective-permute-start.5
  23.6 16.7 %gather.1 = (bf16[1024,512]{1,0:T(8,128)(2,1)S(1)}, bf16[512,512]{1,0:T(8,128)(2,1)S(1)}) custom-call(bf16[16,512]{1,0:T(8,128)(2,1)S(1)} %get-tuple-element.20.own_piece, bf16[16,512]{1,0:T(8,128)(2,1)S(1)} %collective-permute-done.taken), custom_call_target="tpu_custom_call" | custom-call | flops 10000000000 | bytes 1000000 | tf_op jit(solution)/shard_map/gather/pallas_call | solution.py:391
  40.4 3.7 %collective-permute-done.1.refs_6_ = bf16[512,512]{1,0:T(8,128)(2,1)S(1)} collective-permute-done((bf16[512,512]{1,0:T(8,128)(2,1)S(1)}, bf16[512,512]{1,0:T(8,128)(2,1)S(1)}, u32[]{:S(2)}, u32[]{:S(2)}) %collective-permute-start.1) | collective-permute-done | bytes 524320 | tf_op jit(solution)/shard_map/ppermute | solution.py:537
  44.1 0.0 collective-permute-start.6
  44.1 0.0 collective-permute-done.2.refs_7_
  44.1 5.3 %begin.1 = (f32[512,3072]{1,0:T(8,128)}, bf16[1024,512]{1,0:T(8,128)(2,1)}, f32[512,1792]{1,0:T(8,128)S(1)}) custom-call(f32[512,3072]{1,0:T(8,128)S(1)} %get-tuple-element.19.held, bf16[1024,512]{1,0:T(8,128)(2,1)S(1)} %get-tuple-element.21.full, bf16[512,512]{1,0:T(8,128)(2,1)S(1)} %get-tuple-element.22.rest, ...), custom_call_target="tpu_custom_call" | custom-call | flops 10000000000 | bytes 1000000 | tf_op jit(solution)/shard_map/begin/pallas_call | solution.py:475
  49.5 11.5 %collective-permute-done.3.part = bf16[768,512]{1,0:T(8,128)(2,1)S(1)} collective-permute-done((bf16[768,512]{1,0:T(8,128)(2,1)S(1)}, bf16[768,512]{1,0:T(8,128)(2,1)S(1)}, u32[]{:S(2)}, u32[]{:S(2)}) %collective-permute-start.3) | collective-permute-done | bytes 786464 | tf_op jit(solution)/shard_map/ppermute | solution.py:537
  61.0 1.6 %shard_map.50.held = f32[512,3072]{1,0:T(8,128)} custom-call(f32[512,3072]{1,0:T(8,128)} %get-tuple-element.28.held, f32[512,1792]{1,0:T(8,128)S(1)} %get-tuple-element.29.ahead, bf16[768,512]{1,0:T(8,128)(2,1)S(1)} %collective-permute-done.3.part, bf16[512,512]{1,0:T(8,128)(2,1)S(1)} %get-tuple-element.22.rest), custom_call_target="tpu_custom_call", output_to_operand_aliasing={{}: (0, {})} | custom-call | flops 1000000000 | bytes 1000000 | tf_op jit(solution)/shard_map/pallas_call | solution.py:516
  62.6 12.4 %collective-permute-done.4.part = bf16[640,512]{1,0:T(8,128)(2,1)S(1)} collective-permute-done((bf16[640,512]{1,0:T(8,128)(2,1)S(1)}, bf16[640,512]{1,0:T(8,128)(2,1)S(1)}, u32[]{:S(2)}, u32[]{:S(2)}) %collective-permute-start.4) | collective-permute-done | bytes 655392 | tf_op jit(solution)/shard_map/ppermute | solution.py:537
  75.0 1.7 %shard_map.51.held = f32[512,3072]{1,0:T(8,128)} custom-call(f32[512,3072]{1,0:T(8,128)} %shard_map.50.held, f32[512,1792]{1,0:T(8,128)S(1)} %get-tuple-element.29.ahead, bf16[640,512]{1,0:T(8,128)(2,1)S(1)} %collective-permute-done.4.part, bf16[512,512]{1,0:T(8,128)(2,1)S(1)} %get-tuple-element.22.rest), custom_call_target="tpu_custom_call", output_to_operand_aliasing={{}: (0, {})} | custom-call | flops 1000000000 | bytes 1000000 | tf_op jit(solution)/shard_map/pallas_call | solution.py:516
  76.7 3.9 %collective-permute-done.5.part = bf16[256,512]{1,0:T(8,128)(2,1)S(1)} collective-permute-done((bf16[256,512]{1,0:T(8,128)(2,1)S(1)}, bf16[256,512]{1,0:T(8,128)(2,1)S(1)}, u32[]{:S(2)}, u32[]{:S(2)}) %collective-permute-start.5) | collective-permute-done | bytes 262176 | tf_op jit(solution)/shard_map/ppermute | solution.py:537
  80.6 1.1 %shard_map.52.held = f32[512,3072]{1,0:T(8,128)} custom-call(f32[512,3072]{1,0:T(8,128)} %shard_map.51.held, f32[512,1792]{1,0:T(8,128)S(1)} %get-tuple-element.29.ahead, bf16[256,512]{1,0:T(8,128)(2,1)S(1)} %collective-permute-done.5.part, bf16[512,512]{1,0:T(8,128)(2,1)S(1)} %get-tuple-element.22.rest), custom_call_target="tpu_custom_call", output_to_operand_aliasing={{}: (0, {})} | custom-call | flops 1000000000 | bytes 1000000 | tf_op jit(solution)/shard_map/pallas_call | solution.py:516
  81.7 1.3 %collective-permute-done.6.part = bf16[128,512]{1,0:T(8,128)(2,1)S(1)} collective-permute-done((bf16[128,512]{1,0:T(8,128)(2,1)S(1)}, bf16[128,512]{1,0:T(8,128)(2,1)S(1)}, u32[]{:S(2)}, u32[]{:S(2)}) %collective-permute-start.6) | collective-permute-done | bytes 131104 | tf_op jit(solution)/shard_map/ppermute | solution.py:537
  83.0 1.0 %shard_map.53 = f32[512,3072]{1,0:T(8,128)} custom-call(f32[512,3072]{1,0:T(8,128)} %shard_map.52.held, f32[512,1792]{1,0:T(8,128)S(1)} %get-tuple-element.29.ahead, bf16[128,512]{1,0:T(8,128)(2,1)S(1)} %collective-permute-done.6.part, bf16[512,512]{1,0:T(8,128)(2,1)S(1)} %get-tuple-element.22.rest), custom_call_target="tpu_custom_call", output_to_operand_aliasing={{}: (0, {})} | custom-call | flops 1000000000 | bytes 1000000 | tf_op jit(solution)/shard_map/pallas_call | solution.py:516
Async XLA Ops:
  15.0 8.5 %collective-permute-start = (bf16[16,512]{1,0:T(8,128)(2,1)S(1)}, bf16[16,512]{1,0:T(8,128)(2,1)S(1)}, u32[]{:S(2)}, u32[]{:S(2)}) collective-permute-start(bf16[16,512]{1,0:T(8,128)(2,1)S(1)} %get-tuple-element.20.own_piece), channel_id=1, source_target_pairs={{0,64},{1,65},{2,66},{3,67},{4,68},{5,69},{6,70},{7,71},{8,72},{9,... | collective-permute-start | bytes 49160 | tf_op jit(solution)/shard_map/ppermute | solution.py:537
  17.5 26.6 %collective-permute-start.2 = (bf16[768,512]{1,0:T(8,128)(2,1)S(1)}, bf16[768,512]{1,0:T(8,128)(2,1)S(1)}, u32[]{:S(2)}, u32[]{:S(2)}) collective-permute-start(bf16[768,512]{1,0:T(8,128)(2,1)S(1)} %get-tuple-element.18.after.refs_1_), channel_id=1, source_target_pairs={{0,64},{1,65},{2,66},{3,67},{4,68},{5,69},{6,70},{7,71},{8,72},{9,... | collective-permute-start | bytes 2359304 | tf_op jit(solution)/shard_map/ppermute | solution.py:537
  17.6 26.5 %collective-permute-start.1 = (bf16[512,512]{1,0:T(8,128)(2,1)S(1)}, bf16[512,512]{1,0:T(8,128)(2,1)S(1)}, u32[]{:S(2)}, u32[]{:S(2)}) collective-permute-start(bf16[512,512]{1,0:T(8,128)(2,1)S(1)} %get-tuple-element.16.own.refs_0_), channel_id=1, source_target_pairs={{2,66},{4,68},{6,70},{8,72},{10,74},{12,76},{14,78},{16,80},{18,82... | collective-permute-start | bytes 1572872 | tf_op jit(solution)/shard_map/ppermute | solution.py:537
  21.4 39.5 %collective-permute-start.3 = (bf16[768,512]{1,0:T(8,128)(2,1)S(1)}, bf16[768,512]{1,0:T(8,128)(2,1)S(1)}, u32[]{:S(2)}, u32[]{:S(2)}) collective-permute-start(bf16[768,512]{1,0:T(8,128)(2,1)S(1)} %get-tuple-element.23.refs_2_), channel_id=1, source_target_pairs={{0,64},{1,65},{2,66},{3,67},{4,68},{5,69},{6,70},{7,71},{8,72},{9,... | collective-permute-start | bytes 2359304 | tf_op jit(solution)/shard_map/ppermute | solution.py:537
  21.6 53.4 %collective-permute-start.4 = (bf16[640,512]{1,0:T(8,128)(2,1)S(1)}, bf16[640,512]{1,0:T(8,128)(2,1)S(1)}, u32[]{:S(2)}, u32[]{:S(2)}) collective-permute-start(bf16[640,512]{1,0:T(8,128)(2,1)S(1)} %get-tuple-element.24.refs_3_), channel_id=1, source_target_pairs={{0,64},{1,65},{2,66},{3,67},{4,68},{5,69},{6,70},{7,71},{8,72},{9,... | collective-permute-start | bytes 1966088 | tf_op jit(solution)/shard_map/ppermute | solution.py:537
  23.6 57.1 %collective-permute-start.5 = (bf16[256,512]{1,0:T(8,128)(2,1)S(1)}, bf16[256,512]{1,0:T(8,128)(2,1)S(1)}, u32[]{:S(2)}, u32[]{:S(2)}) collective-permute-start(bf16[256,512]{1,0:T(8,128)(2,1)S(1)} %get-tuple-element.25.refs_4_), channel_id=1, source_target_pairs={{0,64},{1,65},{2,66},{3,67},{4,68},{5,69},{6,70},{7,71},{8,72},{9,... | collective-permute-start | bytes 786440 | tf_op jit(solution)/shard_map/ppermute | solution.py:537
  44.1 39.0 %collective-permute-start.6 = (bf16[128,512]{1,0:T(8,128)(2,1)S(1)}, bf16[128,512]{1,0:T(8,128)(2,1)S(1)}, u32[]{:S(2)}, u32[]{:S(2)}) collective-permute-start(bf16[128,512]{1,0:T(8,128)(2,1)S(1)} %get-tuple-element.26.refs_5_), channel_id=1, source_target_pairs={{0,64},{1,65},{2,66},{3,67},{4,68},{5,69},{6,70},{7,71},{8,72},{9,... | collective-permute-start | bytes 393224 | tf_op jit(solution)/shard_map/ppermute | solution.py:537

commit v9 on v8

--- a/solution.py
+++ b/solution.py
@@ -12,7 +12,7 @@
 NT = (((1,), (1,)), ((), ()))
 SIDE = 4
 PIECES = SIDE * SIDE
-PARTS = (512, 768, 768, 640, 256, 128)
+PARTS = (512, 768, 1024, 512, 128, 128)
 EARLY = 2
 DMA = pltpu.SemaphoreType.DMA
 HBM = pl.BlockSpec(memory_space=pltpu.HBM)
@@ -432,7 +432,7 @@
     def step(i, start, mine, theirs):
         chunk = chunk_of(mine.shape[0])
         here = rows(i, chunk)
-        column = pl.ds(pl.multiple_of(start + i * chunk, chunk), chunk)
+        column = pl.ds(pl.multiple_of(start + i * chunk, 128), chunk)
         own = mine[here, :]
         if start == 0:
             own = jnp.where((col < 2) & (row >= col), jnp.zeros_like(own), own)
@@ -440,7 +440,7 @@
             full[rows(row, block), :], own, NT, preferred_element_type=jnp.float32
         )
         if theirs is None:
-            ahead[:, pl.ds(pl.multiple_of(start + i * chunk - ready, chunk), chunk)] = (
+            ahead[:, pl.ds(pl.multiple_of(start + i * chunk - ready, 128), chunk)] = (
                 held[:, column] - total
             )
             return

time: 84.2 us -> 84.2 us (level)
  no operation moved by 1% of the time
where the time goes in v9:
time: 84.2 us; the launch traced here: 84.1 us
  Pallas kernels  41.2 us (49%)
  waiting for transfers between devices  33.5 us (40%)
  starting transfers between devices  8.61 us (10%)
    ppermute x7, waiting for transfers between devices, swap(): taken = lax.ppermute(value, ('row', 'col'), pairs)  33.5 us
    pallas_call x1, Pallas kernels, gather_pieces(): pl.pallas_call(gather_kernel, out_shape=(pltpu.VMEM((2 * half, block), jn...  16.7 us
    pallas_call x1, Pallas kernels, solve_pieces(): pl.pallas_call(solve_kernel, out_shape=(pltpu.VMEM(rhs.shape, rhs.dtype),...  12.4 us
    ppermute x7, starting transfers between devices, swap(): taken = lax.ppermute(value, ('row', 'col'), pairs)  8.61 us
    pallas_call x4, Pallas kernels, finish(): pl.pallas_call(functools.partial(finish_kernel, start, offset), out_shape...  5.28 us
    pallas_call x1, Pallas kernels, begin(): pl.pallas_call(functools.partial(begin_kernel, count=len(owns), early=len...  4.83 us
    pallas_call x1, Pallas kernels, lead(): pl.pallas_call(lead_kernel, out_shape=(*parts, parts[0]), in_specs=[HBM],...  1.97 us
  transfers between devices with their start and end apart: 7, of which 5 were waited for; matrix products, arithmetic and copies ran while one was open for 0% of the time, Pallas kernels for 31%

profile of v9, /device:TPU:124, one launch (start us, length us, event | category | flops | bytes accessed | tf_op | source)
XLA Modules:
  0.0 84.1 jit_solution(14792450003259839108)
XLA Ops:
  0.6 2.0 %lead.1 = (bf16[512,512]{1,0:T(8,128)(2,1)S(1)}, bf16[768,512]{1,0:T(8,128)(2,1)S(1)}, bf16[1024,512]{1,0:T(8,128)(2,1)S(1)}, bf16[512,512]{1,0:T(8,128)(2,1)S(1...) custom-call(bf16[3072,512]{1,0:T(8,128)(2,1)} %panel.1), custom_call_target="tpu_custom_call" | custom-call | tf_op jit(solution)/shard_map/lead/pallas_call | solution.py:84
  2.6 12.4 %solve.1 = (f32[512,3072]{1,0:T(8,128)S(1)}, bf16[16,512]{1,0:T(8,128)(2,1)S(1)}) custom-call(f32[512,3072]{1,0:T(8,128)} %rhs.1, bf16[2,512,512]{2,1,0:T(8,128)(2,1)} %inverse.1, bf16[512,512]{1,0:T(8,128)(2,1)S(1)} %get-tuple-element.16.own.refs_0_, bf16[512,512]{1,0:T(8,128)(2,1)S(1)} %get-tuple-element.17.got.refs_8_, ...), custom_call_target="tpu_custom_call" | custom-call | flops 10000000000 | bytes 1000000 | tf_op jit(solution)/shard_map/solve/pallas_call | solution.py:215
  15.0 2.5 %collective-permute-start = (bf16[16,512]{1,0:T(8,128)(2,1)S(1)}, bf16[16,512]{1,0:T(8,128)(2,1)S(1)}, u32[]{:S(2)}, u32[]{:S(2)}) collective-permute-start(bf16[16,512]{1,0:T(8,128)(2,1)S(1)} %get-tuple-element.20.own_piece), channel_id=1, source_target_pairs={{0,64},{1,65},{2,66},{3,67},{4,68},{5,69},{6,70},{7,71},{8,72},{9,... | collective-permute-start | bytes 49160 | tf_op jit(solution)/shard_map/ppermute | solution.py:537
  17.5 0.1 collective-permute-start.2
  17.6 3.8 %collective-permute-start.1 = (bf16[512,512]{1,0:T(8,128)(2,1)S(1)}, bf16[512,512]{1,0:T(8,128)(2,1)S(1)}, u32[]{:S(2)}, u32[]{:S(2)}) collective-permute-start(bf16[512,512]{1,0:T(8,128)(2,1)S(1)} %get-tuple-element.16.own.refs_0_), channel_id=1, source_target_pairs={{2,66},{4,68},{6,70},{8,72},{10,74},{12,76},{14,78},{16,80},{18,82... | collective-permute-start | bytes 1572872 | tf_op jit(solution)/shard_map/ppermute | solution.py:537
  21.4 0.2 collective-permute-start.3
  21.6 1.9 %collective-permute-start.4 = (bf16[512,512]{1,0:T(8,128)(2,1)S(1)}, bf16[512,512]{1,0:T(8,128)(2,1)S(1)}, u32[]{:S(2)}, u32[]{:S(2)}) collective-permute-start(bf16[512,512]{1,0:T(8,128)(2,1)S(1)} %get-tuple-element.24.refs_3_), channel_id=1, source_target_pairs={{0,64},{1,65},{2,66},{3,67},{4,68},{5,69},{6,70},{7,71},{8,72},{9,... | collective-permute-start | bytes 1572872 | tf_op jit(solution)/shard_map/ppermute | solution.py:537
  23.6 0.0 collective-permute-done.taken
  23.6 0.1 collective-permute-start.5
  23.6 16.7 %gather.1 = (bf16[1024,512]{1,0:T(8,128)(2,1)S(1)}, bf16[512,512]{1,0:T(8,128)(2,1)S(1)}) custom-call(bf16[16,512]{1,0:T(8,128)(2,1)S(1)} %get-tuple-element.20.own_piece, bf16[16,512]{1,0:T(8,128)(2,1)S(1)} %collective-permute-done.taken), custom_call_target="tpu_custom_call" | custom-call | flops 10000000000 | bytes 1000000 | tf_op jit(solution)/shard_map/gather/pallas_call | solution.py:391
  40.4 3.7 %collective-permute-done.1.refs_6_ = bf16[512,512]{1,0:T(8,128)(2,1)S(1)} collective-permute-done((bf16[512,512]{1,0:T(8,128)(2,1)S(1)}, bf16[512,512]{1,0:T(8,128)(2,1)S(1)}, u32[]{:S(2)}, u32[]{:S(2)}) %collective-permute-start.1) | collective-permute-done | bytes 524320 | tf_op jit(solution)/shard_map/ppermute | solution.py:537
  44.1 0.0 collective-permute-start.6
  44.1 0.0 collective-permute-done.2.refs_7_
  44.1 4.8 %begin.1 = (f32[512,3072]{1,0:T(8,128)}, bf16[1024,512]{1,0:T(8,128)(2,1)}, f32[512,1792]{1,0:T(8,128)S(1)}) custom-call(f32[512,3072]{1,0:T(8,128)S(1)} %get-tuple-element.19.held, bf16[1024,512]{1,0:T(8,128)(2,1)S(1)} %get-tuple-element.21.full, bf16[512,512]{1,0:T(8,128)(2,1)S(1)} %get-tuple-element.22.rest, ...), custom_call_target="tpu_custom_call" | custom-call | flops 10000000000 | bytes 1000000 | tf_op jit(solution)/shard_map/begin/pallas_call | solution.py:475
  48.9 17.6 %collective-permute-done.3.part = bf16[1024,512]{1,0:T(8,128)(2,1)S(1)} collective-permute-done((bf16[1024,512]{1,0:T(8,128)(2,1)S(1)}, bf16[1024,512]{1,0:T(8,128)(2,1)S(1)}, u32[]{:S(2)}, u32[]{:S(2)}) %collective-permute-start.3) | collective-permute-done | bytes 1048608 | tf_op jit(solution)/shard_map/ppermute | solution.py:537
  66.6 1.8 %shard_map.50.held = f32[512,3072]{1,0:T(8,128)} custom-call(f32[512,3072]{1,0:T(8,128)} %get-tuple-element.28.held, f32[512,1792]{1,0:T(8,128)S(1)} %get-tuple-element.29.ahead, bf16[1024,512]{1,0:T(8,128)(2,1)S(1)} %collective-permute-done.3.part, bf16[512,512]{1,0:T(8,128)(2,1)S(1)} %get-tuple-element.22.rest), custom_call_target="tpu_custom_call", output_to_operand_aliasing={{}: (0, {})} | custom-call | flops 1000000000 | bytes 1000000 | tf_op jit(solution)/shard_map/pallas_call | solution.py:516
  68.4 9.4 %collective-permute-done.4.part = bf16[512,512]{1,0:T(8,128)(2,1)S(1)} collective-permute-done((bf16[512,512]{1,0:T(8,128)(2,1)S(1)}, bf16[512,512]{1,0:T(8,128)(2,1)S(1)}, u32[]{:S(2)}, u32[]{:S(2)}) %collective-permute-start.4) | collective-permute-done | bytes 524320 | tf_op jit(solution)/shard_map/ppermute | solution.py:537
  77.8 1.5 %shard_map.51.held = f32[512,3072]{1,0:T(8,128)} custom-call(f32[512,3072]{1,0:T(8,128)} %shard_map.50.held, f32[512,1792]{1,0:T(8,128)S(1)} %get-tuple-element.29.ahead, bf16[512,512]{1,0:T(8,128)(2,1)S(1)} %collective-permute-done.4.part, bf16[512,512]{1,0:T(8,128)(2,1)S(1)} %get-tuple-element.22.rest), custom_call_target="tpu_custom_call", output_to_operand_aliasing={{}: (0, {})} | custom-call | flops 1000000000 | bytes 1000000 | tf_op jit(solution)/shard_map/pallas_call | solution.py:516
  79.3 1.3 %collective-permute-done.5.part = bf16[128,512]{1,0:T(8,128)(2,1)S(1)} collective-permute-done((bf16[128,512]{1,0:T(8,128)(2,1)S(1)}, bf16[128,512]{1,0:T(8,128)(2,1)S(1)}, u32[]{:S(2)}, u32[]{:S(2)}) %collective-permute-start.5) | collective-permute-done | bytes 131104 | tf_op jit(solution)/shard_map/ppermute | solution.py:537
  80.6 1.0 %shard_map.52.held = f32[512,3072]{1,0:T(8,128)} custom-call(f32[512,3072]{1,0:T(8,128)} %shard_map.51.held, f32[512,1792]{1,0:T(8,128)S(1)} %get-tuple-element.29.ahead, bf16[128,512]{1,0:T(8,128)(2,1)S(1)} %collective-permute-done.5.part, bf16[512,512]{1,0:T(8,128)(2,1)S(1)} %get-tuple-element.22.rest), custom_call_target="tpu_custom_call", output_to_operand_aliasing={{}: (0, {})} | custom-call | flops 1000000000 | bytes 1000000 | tf_op jit(solution)/shard_map/pallas_call | solution.py:516
  81.6 1.4 %collective-permute-done.6.part = bf16[128,512]{1,0:T(8,128)(2,1)S(1)} collective-permute-done((bf16[128,512]{1,0:T(8,128)(2,1)S(1)}, bf16[128,512]{1,0:T(8,128)(2,1)S(1)}, u32[]{:S(2)}, u32[]{:S(2)}) %collective-permute-start.6) | collective-permute-done | bytes 131104 | tf_op jit(solution)/shard_map/ppermute | solution.py:537
  83.0 1.0 %shard_map.53 = f32[512,3072]{1,0:T(8,128)} custom-call(f32[512,3072]{1,0:T(8,128)} %shard_map.52.held, f32[512,1792]{1,0:T(8,128)S(1)} %get-tuple-element.29.ahead, bf16[128,512]{1,0:T(8,128)(2,1)S(1)} %collective-permute-done.6.part, bf16[512,512]{1,0:T(8,128)(2,1)S(1)} %get-tuple-element.22.rest), custom_call_target="tpu_custom_call", output_to_operand_aliasing={{}: (0, {})} | custom-call | flops 1000000000 | bytes 1000000 | tf_op jit(solution)/shard_map/pallas_call | solution.py:516
Async XLA Ops:
  15.0 8.5 %collective-permute-start = (bf16[16,512]{1,0:T(8,128)(2,1)S(1)}, bf16[16,512]{1,0:T(8,128)(2,1)S(1)}, u32[]{:S(2)}, u32[]{:S(2)}) collective-permute-start(bf16[16,512]{1,0:T(8,128)(2,1)S(1)} %get-tuple-element.20.own_piece), channel_id=1, source_target_pairs={{0,64},{1,65},{2,66},{3,67},{4,68},{5,69},{6,70},{7,71},{8,72},{9,... | collective-permute-start | bytes 49160 | tf_op jit(solution)/shard_map/ppermute | solution.py:537
  17.5 26.6 %collective-permute-start.2 = (bf16[768,512]{1,0:T(8,128)(2,1)S(1)}, bf16[768,512]{1,0:T(8,128)(2,1)S(1)}, u32[]{:S(2)}, u32[]{:S(2)}) collective-permute-start(bf16[768,512]{1,0:T(8,128)(2,1)S(1)} %get-tuple-element.18.after.refs_1_), channel_id=1, source_target_pairs={{0,64},{1,65},{2,66},{3,67},{4,68},{5,69},{6,70},{7,71},{8,72},{9,... | collective-permute-start | bytes 2359304 | tf_op jit(solution)/shard_map/ppermute | solution.py:537
  17.6 26.5 %collective-permute-start.1 = (bf16[512,512]{1,0:T(8,128)(2,1)S(1)}, bf16[512,512]{1,0:T(8,128)(2,1)S(1)}, u32[]{:S(2)}, u32[]{:S(2)}) collective-permute-start(bf16[512,512]{1,0:T(8,128)(2,1)S(1)} %get-tuple-element.16.own.refs_0_), channel_id=1, source_target_pairs={{2,66},{4,68},{6,70},{8,72},{10,74},{12,76},{14,78},{16,80},{18,82... | collective-permute-start | bytes 1572872 | tf_op jit(solution)/shard_map/ppermute | solution.py:537
  21.4 45.1 %collective-permute-start.3 = (bf16[1024,512]{1,0:T(8,128)(2,1)S(1)}, bf16[1024,512]{1,0:T(8,128)(2,1)S(1)}, u32[]{:S(2)}, u32[]{:S(2)}) collective-permute-start(bf16[1024,512]{1,0:T(8,128)(2,1)S(1)} %get-tuple-element.23.refs_2_), channel_id=1, source_target_pairs={{0,64},{1,65},{2,66},{3,67},{4,68},{5,69},{6,70},{7,71},{8,72},{9,... | collective-permute-start | bytes 3145736 | tf_op jit(solution)/shard_map/ppermute | solution.py:537
  21.6 56.2 %collective-permute-start.4 = (bf16[512,512]{1,0:T(8,128)(2,1)S(1)}, bf16[512,512]{1,0:T(8,128)(2,1)S(1)}, u32[]{:S(2)}, u32[]{:S(2)}) collective-permute-start(bf16[512,512]{1,0:T(8,128)(2,1)S(1)} %get-tuple-element.24.refs_3_), channel_id=1, source_target_pairs={{0,64},{1,65},{2,66},{3,67},{4,68},{5,69},{6,70},{7,71},{8,72},{9,... | collective-permute-start | bytes 1572872 | tf_op jit(solution)/shard_map/ppermute | solution.py:537
  23.6 57.1 %collective-permute-start.5 = (bf16[128,512]{1,0:T(8,128)(2,1)S(1)}, bf16[128,512]{1,0:T(8,128)(2,1)S(1)}, u32[]{:S(2)}, u32[]{:S(2)}) collective-permute-start(bf16[128,512]{1,0:T(8,128)(2,1)S(1)} %get-tuple-element.25.refs_4_), channel_id=1, source_target_pairs={{0,64},{1,65},{2,66},{3,67},{4,68},{5,69},{6,70},{7,71},{8,72},{9,... | collective-permute-start | bytes 393224 | tf_op jit(solution)/shard_map/ppermute | solution.py:537
  44.1 39.0 %collective-permute-start.6 = (bf16[128,512]{1,0:T(8,128)(2,1)S(1)}, bf16[128,512]{1,0:T(8,128)(2,1)S(1)}, u32[]{:S(2)}, u32[]{:S(2)}) collective-permute-start(bf16[128,512]{1,0:T(8,128)(2,1)S(1)} %get-tuple-element.26.refs_5_), channel_id=1, source_target_pairs={{0,64},{1,65},{2,66},{3,67},{4,68},{5,69},{6,70},{7,71},{8,72},{9,... | collective-permute-start | bytes 393224 | tf_op jit(solution)/shard_map/ppermute | solution.py:537
